TPU v7x, 128 devices: a whole 4x4x4 slice. The times are simulated.
128 devices in a mesh: sec: 2 (over z_lo), tile: 64 (over y, z_hi, x, core).
Axes of the slice: x: 4, y: 4, z: 4 (z_hi: 2, z_lo: 2; z = z_hi * 2 + z_lo), core: 2. Of those that a mesh axis runs over, the one named last changes fastest.
Arguments:
- atmosphere: bfloat16 [128, 360, 384], P(('sec', 'tile')), may hold values from -6 to 6
- ocean_state: bfloat16 [512, 1440, 128], P('tile', 'sec'), may hold values from -6 to 6
- land_mask: int32 [512, 1440], P('tile', 'sec'), may hold values 0 or 1
- crossing_bands: int32 [64, 4], P('tile'), may hold values from 0 to 127, as said below
- ocean_regrid: float32 [64, 4, 8, 1], P('tile'), may hold values from 0 to 1, as said below
- atmosphere_regrid: float32 [64, 4, 1, 8], P('tile'), may hold values from 0 to 1, as said below
- surface_read: bfloat16 [128], replicated, may hold values from -0.5 to 0.5
- surface_embed: float32 [384], replicated, may hold values from -4 to 4
- flux_read: bfloat16 [384, 8], replicated, may hold values from -0.3125 to 0.3125
- flux_embed: bfloat16 [8, 128], replicated, may hold values from -2 to 2
- legendre_forward: bfloat16 [128, 128, 128], P(('sec', 'tile')), may hold values from -0.5 to 0.5
- legendre_inverse: bfloat16 [128, 128, 128], P(('sec', 'tile')), may hold values from -0.5 to 0.5
- spectral_mix: bfloat16 [2, 384, 384], replicated, may hold values from -0.3125 to 0.3125
- conv_kernel: bfloat16 [2, 7, 7, 128], replicated, may hold values from -0.875 to 0.875
- norm_gain: float32 [2, 128], replicated, may hold values from 0.1 to 1.9
- expand_weight: bfloat16 [2, 128, 512], replicated, may hold values from -0.5 to 0.5
- project_weight: bfloat16 [2, 512, 128], replicated, may hold values from -0.25 to 0.25
- atmosphere_cotangent: bfloat16 [128, 360, 384], P(('sec', 'tile')), may hold values from -6 to 6
- ocean_cotangent: bfloat16 [512, 1440, 128], P('tile', 'sec'), may hold values from -6 to 6
Outputs:
- atmosphere_next: bfloat16 [128, 360, 384], P(('sec', 'tile'))
- ocean_next: bfloat16 [512, 1440, 128], P('tile', 'sec')
- atmosphere_grad: float32 [128, 360, 384], P(('sec', 'tile'))
- ocean_grad: float32 [512, 1440, 128], P('tile', 'sec')
Inputs may be any that keep to these rules, and one draw needn't show every extreme that they name: `crossing_bands`: row j lists between 1 and 4 consecutive distinct atmosphere bands, then repeats its last band; some row lists 4. Its first band is j * 2 - 1, j * 2 or j * 2 + 1, raised to 0 or lowered as far as needed for the list to end at band 128 - 1 at most. `ocean_regrid`: zero in the repeated slots of crossing_bands; the entries of each ocean row sum to one. `atmosphere_regrid`: zero in the repeated slots of crossing_bands.
All inputs are finite; a program needn't handle non-finite values. No bound on the sum of `land_mask` on one device may be relied on, other than what follows from the above.
Results may differ from a plain program's by a relative error of at most 0.008.
Values may be sent and summed in bfloat16 or wider, within the bound.
A program may use at most 128 MiB of HBM per device.

v0:
```python
import jax
import jax.numpy as jnp
from jax import lax
from jax.sharding import Mesh
from jax.sharding import PartitionSpec as P

SEC_TILE = ("sec", "tile_0", "tile_1", "tile_2", "tile_3")
TILE = ("tile_0", "tile_1", "tile_2", "tile_3")


def in_blocks(x, dim, size):
    lengths = x.shape
    blocks = x.reshape(*lengths[:dim], size, lengths[dim] // size, *lengths[dim + 1 :])
    return jnp.moveaxis(blocks, dim, 0)


def laid_out(blocks, dim):
    lengths = list(blocks.shape[1:])
    lengths[dim] *= blocks.shape[0]
    return jnp.moveaxis(blocks, 0, dim).reshape(lengths)


def turned_blocks(blocks, axes, sequence):
    lengths = [lax.axis_size(a) for a in axes]
    blocks = blocks.reshape(*lengths, *blocks.shape[1:])
    for k in sequence:
        blocks = lax.all_to_all(blocks, axes[k], split_axis=k, concat_axis=k, tiled=True)
    return blocks.reshape(-1, *blocks.shape[len(axes) :])


def two_step_exchange(x, groups, sequence, split_dim, concat_dim):
    size = lax.axis_size(groups[0]) * lax.axis_size(groups[1])
    blocks = in_blocks(x, split_dim, size)
    return laid_out(turned_blocks(blocks, groups, sequence), concat_dim)


def with_halo(x, sides, width, wrap):
    for axis, dim in sides:
        size, length = (lax.axis_size(axis), x.shape[dim])
        up = [(i, (i + 1) % size) for i in range(size if wrap else size - 1)]
        down = [(j, i) for i, j in up]
        last = lax.slice_in_dim(x, length - width, length, axis=dim)
        first = lax.slice_in_dim(x, 0, width, axis=dim)
        before = lax.ppermute(last, axis, up)
        after = lax.ppermute(first, axis, down)
        x = jnp.concatenate([before, x, after], axis=dim)
    return x


def wave_table(lon_count, mode_count):
    longitude = jnp.arange(lon_count, dtype=jnp.int32)
    wavenumber = jnp.arange(mode_count, dtype=jnp.int32)
    phase = (longitude[:, None] * wavenumber[None, :] % lon_count).astype(jnp.float32) * (
        2.0 * jnp.pi / lon_count
    )
    scaled = jnp.stack([jnp.cos(phase), -jnp.sin(phase)], axis=2) * jnp.sqrt(
        jnp.float32(2.0 / lon_count)
    )
    return scaled.reshape(lon_count, 2 * mode_count).astype(jnp.bfloat16)


def depthwise(window, kernel):
    radius = kernel.shape[0] // 2
    height = window.shape[0] - 2 * radius
    extent = window.shape[1] - 2 * radius
    wide = window.astype(jnp.float32)
    weights = kernel.astype(jnp.float32)
    total = jnp.zeros((height, extent, window.shape[2]), jnp.float32)
    for shift_row in range(kernel.shape[0]):
        for shift_col in range(kernel.shape[1]):
            total = (
                total
                + wide[shift_row : shift_row + height, shift_col : shift_col + extent]
                * weights[shift_row, shift_col]
            )
    return total


def cell_forward(hidden, gain, expand, project):
    center = hidden - jnp.mean(hidden, axis=-1, keepdims=True)
    inverse_std = lax.rsqrt(jnp.mean(center * center, axis=-1, keepdims=True) + 1e-06)
    normed = (center * inverse_std * gain).astype(jnp.bfloat16)
    before = jnp.dot(normed, expand, preferred_element_type=jnp.float32)
    active = jax.nn.gelu(before).astype(jnp.bfloat16)
    return jnp.dot(active, project, preferred_element_type=jnp.float32)


def cell_backward(hidden, gain, expand, project, mask_value, cotangent):
    center = hidden - jnp.mean(hidden, axis=-1, keepdims=True)
    inverse_std = lax.rsqrt(jnp.mean(center * center, axis=-1, keepdims=True) + 1e-06)
    unit = center * inverse_std
    normed = (unit * gain).astype(jnp.bfloat16)
    before = jnp.dot(normed, expand, preferred_element_type=jnp.float32)
    masked = (mask_value[:, :, None] * cotangent).astype(jnp.bfloat16)
    active_adjoint = jnp.dot(masked, project.T, preferred_element_type=jnp.float32)
    _, gelu_back = jax.vjp(jax.nn.gelu, before)
    before_adjoint = gelu_back(active_adjoint)[0].astype(jnp.bfloat16)
    normed_adjoint = jnp.dot(before_adjoint, expand.T, preferred_element_type=jnp.float32)
    scaled = normed_adjoint * gain
    result = inverse_std * (
        scaled
        - jnp.mean(scaled, axis=-1, keepdims=True)
        - unit * jnp.mean(scaled * unit, axis=-1, keepdims=True)
    )
    return result.astype(jnp.bfloat16)


def ocean_matrix(bands_row, blocks, lat_count):
    lat_band = blocks.shape[2]
    index = bands_row[:, None] * lat_band + jnp.arange(lat_band, dtype=jnp.int32)[None, :]
    onehot = (index[:, :, None] == jnp.arange(lat_count, dtype=jnp.int32)[None, None, :]).astype(
        jnp.float32
    )
    return jnp.einsum("poi,pia->oa", blocks, onehot, precision=lax.Precision.HIGHEST)


def atmosphere_matrix(bands_row, blocks, lat_count):
    lat_band = blocks.shape[1]
    index = bands_row[:, None] * lat_band + jnp.arange(lat_band, dtype=jnp.int32)[None, :]
    onehot = (index[:, :, None] == jnp.arange(lat_count, dtype=jnp.int32)[None, None, :]).astype(
        jnp.float32
    )
    return jnp.einsum("pio,pia->ao", blocks, onehot, precision=lax.Precision.HIGHEST)


def mix_complex(coefficient, mix_real, mix_imag):
    real_part = coefficient[:, :, 0]
    imag_part = coefficient[:, :, 1]
    out_real = jnp.einsum(
        "lmc,cd->lmd", real_part, mix_real, preferred_element_type=jnp.float32
    ) - jnp.einsum("lmc,cd->lmd", imag_part, mix_imag, preferred_element_type=jnp.float32)
    out_imag = jnp.einsum(
        "lmc,cd->lmd", imag_part, mix_real, preferred_element_type=jnp.float32
    ) + jnp.einsum("lmc,cd->lmd", real_part, mix_imag, preferred_element_type=jnp.float32)
    return jnp.stack([out_real, out_imag], axis=2).astype(jnp.bfloat16)


def spectral_block(spectrum, forward, inverse, mixing):
    lat_count, columns, channels = spectrum.shape
    split = spectrum.reshape(lat_count, columns // 2, 2, channels)
    coefficient = jnp.einsum(
        "mla,amrc->lmrc", forward, split, preferred_element_type=jnp.float32
    ).astype(jnp.bfloat16)
    mixed = mix_complex(coefficient, mixing[0], mixing[1])
    returned = jnp.einsum(
        "mal,lmrc->amrc", inverse, mixed, preferred_element_type=jnp.float32
    ).astype(jnp.bfloat16)
    return returned.reshape(lat_count, columns, channels)


def spectral_adjoint(returned_adjoint, forward, inverse, mixing):
    lat_count, columns, channels = returned_adjoint.shape
    split = returned_adjoint.reshape(lat_count, columns // 2, 2, channels)
    mixed_adjoint = jnp.einsum(
        "mal,amrc->lmrc", inverse, split, preferred_element_type=jnp.float32
    ).astype(jnp.bfloat16)
    real_part = mixed_adjoint[:, :, 0]
    imag_part = mixed_adjoint[:, :, 1]
    back_real = jnp.einsum(
        "lmd,cd->lmc", real_part, mixing[0], preferred_element_type=jnp.float32
    ) + jnp.einsum("lmd,cd->lmc", imag_part, mixing[1], preferred_element_type=jnp.float32)
    back_imag = jnp.einsum(
        "lmd,cd->lmc", imag_part, mixing[0], preferred_element_type=jnp.float32
    ) - jnp.einsum("lmd,cd->lmc", real_part, mixing[1], preferred_element_type=jnp.float32)
    coefficient_adjoint = jnp.stack([back_real, back_imag], axis=2).astype(jnp.bfloat16)
    spectrum_adjoint = jnp.einsum(
        "mla,lmrc->amrc", forward, coefficient_adjoint, preferred_element_type=jnp.float32
    ).astype(jnp.bfloat16)
    return spectrum_adjoint.reshape(lat_count, columns, channels)


def to_modes(values):
    return two_step_exchange(
        values, (("sec", "tile_0", "tile_1", "tile_2"), "tile_3"), (1, 0), 1, 0
    )


def to_bands(values):
    return lax.all_to_all(values, SEC_TILE, split_axis=0, concat_axis=1, tiled=True)


def rims(values, width):
    with_rows = with_halo(values, ((TILE, 0),), width, False)
    return with_halo(with_rows, (("sec", 1),), width, True)


def spread_rows(matrix, values):
    return lax.psum_scatter(
        jnp.dot(matrix, values, precision=lax.Precision.HIGHEST),
        SEC_TILE,
        scatter_dimension=0,
        tiled=True,
    )


def collect_rows(matrix, values, lon_count, fields, offset, half):
    piece = lax.all_gather(values, SEC_TILE, axis=0, tiled=True)
    own = lax.dynamic_slice_in_dim(
        piece.reshape(piece.shape[0], lon_count, fields), offset, half, 1
    )
    return jnp.dot(
        matrix, own.reshape(piece.shape[0], half * fields), precision=lax.Precision.HIGHEST
    )


def place_half(values, lon_count, offset):
    shape = (values.shape[0], lon_count) + values.shape[2:]
    empty = jnp.zeros(shape, jnp.float32)
    starts = (jnp.int32(0), offset) + tuple((jnp.int32(0) for extra in values.shape[2:]))
    return lax.dynamic_update_slice(empty, values, starts)


def per_device(
    atmosphere,
    ocean_state,
    land_mask,
    crossing_bands,
    ocean_regrid,
    atmosphere_regrid,
    surface_read,
    surface_embed,
    flux_read,
    flux_embed,
    legendre_forward,
    legendre_inverse,
    spectral_mix,
    conv_kernel,
    norm_gain,
    expand_weight,
    project_weight,
    atmosphere_cotangent,
    ocean_cotangent,
):
    band_total = lax.axis_size(SEC_TILE)
    lat_rows, lon_count, channels = atmosphere.shape
    lat_count = lat_rows * band_total
    ocean_rows, ocean_lon, ocean_channels = ocean_state.shape
    half = lon_count // lax.axis_size("sec")
    offset = lax.axis_index("sec") * half
    ratio = ocean_lon // half
    flux_count = flux_read.shape[1]
    radius = conv_kernel.shape[1] // 2
    layer_count = conv_kernel.shape[0]
    highest = lax.Precision.HIGHEST
    mask_value = land_mask.astype(jnp.float32)
    to_ocean = ocean_matrix(crossing_bands[0], ocean_regrid[0], lat_count)
    to_atmosphere = atmosphere_matrix(crossing_bands[0], atmosphere_regrid[0], lat_count)
    surface = jnp.dot(ocean_state, surface_read, preferred_element_type=jnp.float32)
    coarse = jnp.mean((mask_value * surface).reshape(ocean_rows, half, ratio), axis=2)
    surface_atmosphere = spread_rows(to_atmosphere, place_half(coarse, lon_count, offset))
    flux = jnp.einsum("agc,cf->agf", atmosphere, flux_read, preferred_element_type=jnp.float32)
    flux_ocean = collect_rows(
        to_ocean,
        flux.reshape(lat_rows, lon_count * flux_count),
        lon_count,
        flux_count,
        offset,
        half,
    )
    mixed_input = (
        atmosphere.astype(jnp.float32)
        + surface_atmosphere[:, :, None] * surface_embed[None, None, :]
    ).astype(jnp.bfloat16)
    table = wave_table(lon_count, legendre_forward.shape[0] * band_total)
    spectrum = jnp.einsum(
        "gk,agc->akc", table, mixed_input, preferred_element_type=jnp.float32
    ).astype(jnp.bfloat16)
    returned = to_bands(
        spectral_block(to_modes(spectrum), legendre_forward, legendre_inverse, spectral_mix)
    )
    response = jnp.einsum("gk,akc->agc", table, returned, preferred_element_type=jnp.float32)
    atmosphere_next = (mixed_input.astype(jnp.float32) + jax.nn.gelu(response)).astype(jnp.bfloat16)
    forcing_coarse = jnp.einsum(
        "ogf,fc->ogc",
        flux_ocean.reshape(ocean_rows, half, flux_count),
        flux_embed.astype(jnp.float32),
        precision=highest,
    )
    forcing = jnp.broadcast_to(
        forcing_coarse[:, :, None, :], (ocean_rows, half, ratio, ocean_channels)
    ).reshape(ocean_rows, ocean_lon, ocean_channels)
    state = (ocean_state.astype(jnp.float32) + mask_value[:, :, None] * forcing).astype(
        jnp.bfloat16
    )
    windows = []
    for layer in range(layer_count):
        window = rims(state, radius)
        windows.append(window)
        update = cell_forward(
            depthwise(window, conv_kernel[layer]),
            norm_gain[layer],
            expand_weight[layer],
            project_weight[layer],
        )
        state = (state.astype(jnp.float32) + mask_value[:, :, None] * update).astype(jnp.bfloat16)
    cotangent = ocean_cotangent.astype(jnp.float32)
    for layer in range(layer_count - 1, -1, -1):
        hidden = depthwise(windows[layer], conv_kernel[layer])
        hidden_adjoint = cell_backward(
            hidden,
            norm_gain[layer],
            expand_weight[layer],
            project_weight[layer],
            mask_value,
            cotangent,
        )
        cotangent = cotangent + depthwise(
            rims(hidden_adjoint, radius), conv_kernel[layer, ::-1, ::-1]
        )
    forcing_adjoint = (
        (mask_value[:, :, None] * cotangent)
        .reshape(ocean_rows, half, ratio, ocean_channels)
        .sum(axis=2)
    )
    flux_ocean_adjoint = jnp.einsum(
        "ogc,fc->ogf", forcing_adjoint, flux_embed.astype(jnp.float32), precision=highest
    )
    full_adjoint = place_half(flux_ocean_adjoint, lon_count, offset)
    flux_adjoint = spread_rows(to_ocean.T, full_adjoint.reshape(ocean_rows, lon_count * flux_count))
    flux_adjoint = flux_adjoint.reshape(lat_rows, lon_count, flux_count)
    from_flux = jnp.einsum(
        "agf,cf->agc", flux_adjoint, flux_read.astype(jnp.float32), precision=highest
    )
    atmosphere_adjoint = atmosphere_cotangent.astype(jnp.float32)
    _, gelu_back = jax.vjp(jax.nn.gelu, response)
    response_adjoint = gelu_back(atmosphere_adjoint)[0].astype(jnp.bfloat16)
    returned_adjoint = jnp.einsum(
        "gk,agc->akc", table, response_adjoint, preferred_element_type=jnp.float32
    ).astype(jnp.bfloat16)
    spectrum_adjoint = to_bands(
        spectral_adjoint(
            to_modes(returned_adjoint), legendre_forward, legendre_inverse, spectral_mix
        )
    )
    input_adjoint = atmosphere_adjoint + jnp.einsum(
        "gk,akc->agc", table, spectrum_adjoint, preferred_element_type=jnp.float32
    )
    atmosphere_grad = input_adjoint + from_flux
    surface_adjoint = jnp.einsum("agc,c->ag", input_adjoint, surface_embed, precision=highest)
    coarse_adjoint = collect_rows(to_atmosphere.T, surface_adjoint, lon_count, 1, offset, half)
    widened_adjoint = jnp.broadcast_to(
        coarse_adjoint[:, :, None], (ocean_rows, half, ratio)
    ).reshape(ocean_rows, ocean_lon)
    surface_grad = mask_value * widened_adjoint / ratio
    ocean_grad = (
        cotangent + surface_grad[:, :, None] * surface_read.astype(jnp.float32)[None, None, :]
    )
    return (atmosphere_next, state, atmosphere_grad, ocean_grad)


def solution(mesh):
    finer = Mesh(
        mesh.devices.reshape(mesh.shape["sec"], 4, 2, 4, 2),
        ("sec", "tile_0", "tile_1", "tile_2", "tile_3"),
    )
    placed = (
        P(SEC_TILE, None, None),
        P(TILE, "sec", None),
        P(TILE, "sec"),
        P(TILE, None),
        P(TILE, None, None, None),
        P(TILE, None, None, None),
        P(),
        P(),
        P(),
        P(),
        P(SEC_TILE, None, None),
        P(SEC_TILE, None, None),
        P(),
        P(),
        P(),
        P(),
        P(),
        P(SEC_TILE, None, None),
        P(TILE, "sec", None),
    )
    return jax.shard_map(
        per_device,
        mesh=finer,
        in_specs=placed,
        out_specs=(
            P(SEC_TILE, None, None),
            P(TILE, "sec", None),
            P(SEC_TILE, None, None),
            P(TILE, "sec", None),
        ),
        check_vma=False,
    )
```

profile of v0, /device:TPU:1, one launch (start us, length us, event | category | flops | bytes accessed | tf_op | source)
XLA Modules:
  0.0 916.0 jit_solution(4656370942096807728)
XLA Ops:
  20.9 140.1 %all-reduce.8.cloned.1.call-done = f32[128,360]{1,0:T(8,128)} async-done(((f32[128,360]{1,0:T(8,128)}), f32[128,360]{1,0:T(8,128)}) %all-reduce.8.cloned.1.call-update) | async-done | bytes 184336
  162.3 4.5 all_to_all.38
  167.6 6.6 all-to-all-start.1
  174.8 8.5 all-to-all-done.1
  183.5 173.7 %all-gather.4.cloned.1.call-done = f32[128,1,2880]{2,1,0:T(1,128)} async-done(((f32[1,1,2880]{2,1,0:T(1,128)}), f32[128,1,2880]{2,1,0:T(1,128)}) %all-gather.4.cloned.1.call-update) | async-done | bytes 1474576 | tf_op jit(solution)/shard_map/all_gather | solution.py:197
  374.7 4.4 collective-permute-done.1
  381.7 13.4 %all-to-all-start.2 = ((bf16[128,2,384]{2,1,0:T(2,128)(2,1)}), bf16[128,2,384]{2,1,0:T(2,128)(2,1)}, u32[]{:S(2)}, u32[]{:S(2)}) async-start(bf16[128,2,384]{2,1,0:T(2,128)(2,1)} %copy.75), calls=%async_computation.2 | async-start | bytes 393216 | tf_op jit(solution)/shard_map/all_to_all | solution.py:179
  397.1 20.6 %fusion.376 = (f32[8,720]{1,0:T(8,128)S(1)}, f32[8,720,128]{2,1,0:T(8,128)S(1)}) fusion(f32[128]{0:T(128)S(1)} %get-tuple-element.184, f32[14,726,128]{2,1,0:T(8,128)S(1)} %maximum_convert_fusion, f32[128]{0:T(128)S(1)} %get-tuple-element.185, f32[128]{0:T(128)S(1)} %get-tuple-element.186, f32[128]{0:T(128)S(1)} %get-tuple-element.187, ...), kind=kLoop, calls=%fused_computation.842 | loop fusion | flops 72247680 | bytes 147504128 | tf_op jit(solution)/shard_map/reduce_sum | solution.py:80
  422.0 4.9 add_convert_fusion.1
  445.5 12.4 %all-to-all-start.4 = ((bf16[64,2,1,2,384]{4,3,1,2,0:T(2,128)(2,1)}), bf16[64,2,1,2,384]{4,3,1,2,0:T(2,128)(2,1)}, u32[]{:S(2)}, u32[]{:S(2)}) async-start(bf16[64,2,1,2,384]{4,3,1,2,0:T(2,128)(2,1)} %copy.84), calls=%async_computation.4 | async-start | bytes 393216 | tf_op jit(solution)/shard_map/all_to_all | solution.py:27
  472.6 20.5 %fusion.374 = (f32[8,720]{1,0:T(8,128)S(1)}, f32[8,720,128]{2,1,0:T(8,128)S(1)}) fusion(f32[128]{0:T(128)S(1)} %copy-done.101, f32[14,726,128]{2,1,0:T(8,128)S(1)} %maximum_convert_fusion.1, f32[128]{0:T(128)S(1)} %copy-done.102, f32[128]{0:T(128)S(1)} %copy-done.103, f32[128]{0:T(128)S(1)} %copy-done.104, f32[128]{0:T(128)S(1)} %copy-done.105, ...), kind=kLoop, calls=%fused_computation.841 | loop fusion | flops 72247680 | bytes 147504128 | tf_op jit(solution)/shard_map/reduce_sum | solution.py:80
  495.0 5.4 fusion.219
  500.4 15.5 %multiply_reduce_fusion.5 = (f32[8,720]{1,0:T(8,128)S(1)}, f32[8,720]{1,0:T(8,128)S(1)}, f32[8,720,128]{2,1,0:T(8,128)}) fusion(f32[128]{0:T(128)S(1)} %copy-done.44, f32[8,720]{1,0:T(8,128)S(1)} %add_rsqrt_fusion, f32[8,720,128]{2,1,0:T(8,128)} %copy-done.2, f32[8,720]{1,0:T(8,128)S(1)} %broadcast_multiply_fusion.6, ...), kind=kOutput, calls=%fused_computation.438 | convolution fusion | flops 1575555840 | bytes 19551744 | tf_op jit(solution)/shard_map/dot_general | solution.py:98
  515.9 6.9 multiply_convert_fusion.6
  545.1 64.0 %convert_add_fusion = f32[8,720,128]{2,1,0:T(8,128)} fusion(bf16[8,720,128]{2,1,0:T(8,128)(2,1)S(1)} %copy-done.15, f32[14,726,128]{2,1,0:T(8,128)} %maximum_convert_fusion.2, f32[128]{0:T(128)S(1)} %copy-done.54, f32[128]{0:T(128)S(1)} %copy-done.55, f32[128]{0:T(128)S(1)} %copy-done.56, f32[128]{0:T(128)S(1)} %copy-done.57, f32[128]{0:T(128)S(1)} %copy-done.58, ...), kind=kLoop, calls=%fused_computation.26 | loop fusion | flops 72990720 | bytes 148955648 | tf_op jit(solution)/shard_map/add | solution.py:307
  609.2 13.6 %multiply_reduce_fusion.4 = (f32[8,720]{1,0:T(8,128)S(1)}, f32[8,720]{1,0:T(8,128)S(1)}, f32[8,720,128]{2,1,0:T(8,128)}) fusion(f32[128]{0:T(128)S(1)} %copy-done.43, f32[8,720]{1,0:T(8,128)S(1)} %copy-done.24, f32[8,720,128]{2,1,0:T(8,128)S(1)} %get-tuple-element.17, f32[8,720]{1,0:T(8,128)S(1)} %copy-done.17, bf16[2,128,512]{2,1,0:T(8,128)(2,1)S(1)} %copy-done.20, ...), kind=kOutput, calls=%fused_computation.437 | convolution fusion | flops 1574818560 | bytes 21026304 | tf_op jit(solution)/shard_map/dot_general | solution.py:98
  622.7 7.0 multiply_convert_fusion.4
  638.2 13.8 %all-to-all-start.5 = ((bf16[128,2,384]{2,1,0:T(2,128)(2,1)}), bf16[128,2,384]{2,1,0:T(2,128)(2,1)}, u32[]{:S(2)}, u32[]{:S(2)}) async-start(bf16[128,2,384]{2,1,0:T(2,128)(2,1)} %copy.87), calls=%async_computation.5 | async-start | bytes 393216 | tf_op jit(solution)/shard_map/all_to_all | solution.py:179
  653.8 8.3 all-to-all-done.5
  670.4 59.1 %broadcast_multiply_fusion = (f32[8,720,128]{2,1,0:T(8,128)}, f32[8,720,128]{2,1,0:T(8,128)S(1)}) fusion(f32[8,720]{1,0:T(8,128)S(1)} %copy-done.27, f32[8,720,128]{2,1,0:T(8,128)} %convert_add_fusion, f32[128]{0:T(128)S(1)} %copy-done.47, f32[14,726,128]{2,1,0:T(8,128)} %maximum_convert_fusion.3, f32[128]{0:T(128)S(1)} %copy-done.48, ...), kind=kLoop, calls=%fused_computation.447 | loop fusion | flops 72990720 | bytes 153402368 | tf_op jit(solution)/shard_map/mul | solution.py:311
  729.5 4.5 reduce_sum.115
  737.6 5.0 dynamic_update_slice.7
  748.5 8.4 add_convert_fusion
  756.9 140.1 %all-reduce.10.cloned.1.call-done = (f32[128,2880]{1,0:T(8,128)}, f32[128,360]{1,0:T(8,128)}) async-done(((f32[128,2880]{1,0:T(8,128)}, f32[128,360]{1,0:T(8,128)}), (f32[128,2880]{1,0:T(8,128)}, f32[128,360]{1,0:T(8,128)})) %all-reduce.10.cloned.1.call-update) | async-done | bytes 1658896
  (418 shorter events, 138.2 us)
Async XLA Ops:
  7.2 153.8 %all-reduce.8.cloned.1.call-start = ((), (), s32[]{:S(2)}) async-start(), calls=%async_computation.7 | async-start | bytes 393216
  13.4 343.8 %all-gather.4.cloned.1.call-start = ((), (), s32[]{:S(2)}) async-start(), calls=%async_computation.6 | async-start | bytes 1519104 | tf_op jit(solution)/shard_map/all_gather | solution.py:197
  14.5 407.5 %copy-start.25 = (f32[8,720]{1,0:T(8,128)}, f32[8,720]{1,0:T(8,128)S(1)}, u32[]{:S(2)}) copy-start(f32[8,720]{1,0:T(8,128)S(1)} %convert_element_type.219) | copy-start | bytes 69124
  167.6 15.6 %all-to-all-start.1 = ((bf16[64,2,1,2,384]{4,3,1,2,0:T(2,128)(2,1)}), bf16[64,2,1,2,384]{4,3,1,2,0:T(2,128)(2,1)S(1)}, u32[]{:S(2)}, u32[]{:S(2)}) async-start(bf16[64,2,1,2,384]{4,3,1,2,0:T(2,128)(2,1)} %copy.72), calls=%async_computation.1 | async-start | bytes 393216 | tf_op jit(solution)/shard_map/all_to_all | solution.py:27
  364.9 9.8 %collective-permute-start = (bf16[3,720,128]{2,1,0:T(8,128)(2,1)S(1)}, bf16[3,720,128]{2,1,0:T(8,128)(2,1)S(1)}, u32[]{:S(2)}, u32[]{:S(2)}) collective-permute-start(bf16[3,720,128]{2,1,0:T(8,128)(2,1)S(1)} %get-tuple-element.34), channel_id=1, source_target_pairs={{0,1},{1,2},{2,3},{3,4},{4,5},{5,6},{6,7},{7,8},{8,9},{9,10},{10,1... | collective-permute-start | bytes 1658888 | tf_op jit(solution)/shard_map/ppermute | solution.py:44
  368.3 10.8 %collective-permute-start.1 = (bf16[3,720,128]{2,1,0:T(8,128)(2,1)S(1)}, bf16[3,720,128]{2,1,0:T(8,128)(2,1)S(1)}, u32[]{:S(2)}, u32[]{:S(2)}) collective-permute-start(bf16[3,720,128]{2,1,0:T(8,128)(2,1)S(1)} %get-tuple-element.35), channel_id=1, source_target_pairs={{1,0},{2,1},{3,2},{4,3},{5,4},{6,5},{7,6},{8,7},{9,8},{10,9},{11,1... | collective-permute-start | bytes 1658888 | tf_op jit(solution)/shard_map/ppermute | solution.py:45
  379.1 16.0 %collective-permute-start.2 = (bf16[14,3,128]{2,1,0:T(4,128)(2,1)S(1)}, bf16[14,3,128]{2,1,0:T(4,128)(2,1)S(1)}, u32[]{:S(2)}, u32[]{:S(2)}) collective-permute-start(bf16[14,3,128]{2,1,0:T(4,128)(2,1)S(1)} %get-tuple-element.26), channel_id=1, source_target_pairs={{0,64},{64,0},{1,65},{65,1},{2,66},{66,2},{3,67},{67,3},{4,68},{68... | collective-permute-start | bytes 32264 | tf_op jit(solution)/shard_map/ppermute | solution.py:44
  380.4 14.7 %collective-permute-start.3 = (bf16[14,3,128]{2,1,0:T(4,128)(2,1)S(1)}, bf16[14,3,128]{2,1,0:T(4,128)(2,1)S(1)}, u32[]{:S(2)}, u32[]{:S(2)}) collective-permute-start(bf16[14,3,128]{2,1,0:T(4,128)(2,1)S(1)} %get-tuple-element.27), channel_id=1, source_target_pairs={{64,0},{0,64},{65,1},{1,65},{66,2},{2,66},{67,3},{3,67},{68,4},{4,... | collective-permute-start | bytes 32264 | tf_op jit(solution)/shard_map/ppermute | solution.py:45
  381.7 52.2 %all-to-all-start.2 = ((bf16[128,2,384]{2,1,0:T(2,128)(2,1)}), bf16[128,2,384]{2,1,0:T(2,128)(2,1)}, u32[]{:S(2)}, u32[]{:S(2)}) async-start(bf16[128,2,384]{2,1,0:T(2,128)(2,1)} %copy.75), calls=%async_computation.2 | async-start | bytes 393216 | tf_op jit(solution)/shard_map/all_to_all | solution.py:179
  428.4 31.6 %collective-permute-start.4 = (bf16[3,720,128]{2,1,0:T(8,128)(2,1)}, bf16[3,720,128]{2,1,0:T(8,128)(2,1)S(1)}, u32[]{:S(2)}, u32[]{:S(2)}) collective-permute-start(bf16[3,720,128]{2,1,0:T(8,128)(2,1)} %get-tuple-element.32), channel_id=1, source_target_pairs={{0,1},{1,2},{2,3},{3,4},{4,5},{5,6},{6,7},{7,8},{8,9},{9,10},{10,1... | collective-permute-start | bytes 1658888 | tf_op jit(solution)/shard_map/ppermute | solution.py:44
  432.0 28.0 %collective-permute-start.5 = (bf16[3,720,128]{2,1,0:T(8,128)(2,1)}, bf16[3,720,128]{2,1,0:T(8,128)(2,1)}, u32[]{:S(2)}, u32[]{:S(2)}) collective-permute-start(bf16[3,720,128]{2,1,0:T(8,128)(2,1)} %get-tuple-element.33), channel_id=1, source_target_pairs={{1,0},{2,1},{3,2},{4,3},{5,4},{6,5},{7,6},{8,7},{9,8},{10,9},{11,1... | collective-permute-start | bytes 1658888 | tf_op jit(solution)/shard_map/ppermute | solution.py:45
  445.5 21.3 %all-to-all-start.4 = ((bf16[64,2,1,2,384]{4,3,1,2,0:T(2,128)(2,1)}), bf16[64,2,1,2,384]{4,3,1,2,0:T(2,128)(2,1)}, u32[]{:S(2)}, u32[]{:S(2)}) async-start(bf16[64,2,1,2,384]{4,3,1,2,0:T(2,128)(2,1)} %copy.84), calls=%async_computation.4 | async-start | bytes 393216 | tf_op jit(solution)/shard_map/all_to_all | solution.py:27
  461.4 7.7 collective-permute-start.6
  462.4 6.6 collective-permute-start.7
  522.9 10.3 %collective-permute-start.8 = (bf16[3,720,128]{2,1,0:T(8,128)(2,1)S(1)}, bf16[3,720,128]{2,1,0:T(8,128)(2,1)S(1)}, u32[]{:S(2)}, u32[]{:S(2)}) collective-permute-start(bf16[3,720,128]{2,1,0:T(8,128)(2,1)S(1)} %get-tuple-element.30), channel_id=1, source_target_pairs={{0,1},{1,2},{2,3},{3,4},{4,5},{5,6},{6,7},{7,8},{8,9},{9,10},{10,1... | collective-permute-start | bytes 1658888 | tf_op jit(solution)/shard_map/ppermute | solution.py:44
  526.8 10.8 %collective-permute-start.9 = (bf16[3,720,128]{2,1,0:T(8,128)(2,1)S(1)}, bf16[3,720,128]{2,1,0:T(8,128)(2,1)S(1)}, u32[]{:S(2)}, u32[]{:S(2)}) collective-permute-start(bf16[3,720,128]{2,1,0:T(8,128)(2,1)S(1)} %get-tuple-element.31), channel_id=1, source_target_pairs={{1,0},{2,1},{3,2},{4,3},{5,4},{6,5},{7,6},{8,7},{9,8},{10,9},{11,1... | collective-permute-start | bytes 1658888 | tf_op jit(solution)/shard_map/ppermute | solution.py:45
  537.6 2.8 collective-permute-start.10
  538.7 2.6 collective-permute-start.11
  632.0 31.4 %collective-permute-start.12 = (bf16[3,720,128]{2,1,0:T(8,128)(2,1)}, bf16[3,720,128]{2,1,0:T(8,128)(2,1)S(1)}, u32[]{:S(2)}, u32[]{:S(2)}) collective-permute-start(bf16[3,720,128]{2,1,0:T(8,128)(2,1)} %get-tuple-element.28), channel_id=1, source_target_pairs={{0,1},{1,2},{2,3},{3,4},{4,5},{5,6},{6,7},{7,8},{8,9},{9,10},{10,1... | collective-permute-start | bytes 1658888 | tf_op jit(solution)/shard_map/ppermute | solution.py:44
  635.0 28.4 %collective-permute-start.13 = (bf16[3,720,128]{2,1,0:T(8,128)(2,1)}, bf16[3,720,128]{2,1,0:T(8,128)(2,1)S(1)}, u32[]{:S(2)}, u32[]{:S(2)}) collective-permute-start(bf16[3,720,128]{2,1,0:T(8,128)(2,1)} %get-tuple-element.29), channel_id=1, source_target_pairs={{1,0},{2,1},{3,2},{4,3},{5,4},{6,5},{7,6},{8,7},{9,8},{10,9},{11,1... | collective-permute-start | bytes 1658888 | tf_op jit(solution)/shard_map/ppermute | solution.py:45
  638.2 23.8 %all-to-all-start.5 = ((bf16[128,2,384]{2,1,0:T(2,128)(2,1)}), bf16[128,2,384]{2,1,0:T(2,128)(2,1)}, u32[]{:S(2)}, u32[]{:S(2)}) async-start(bf16[128,2,384]{2,1,0:T(2,128)(2,1)} %copy.87), calls=%async_computation.5 | async-start | bytes 393216 | tf_op jit(solution)/shard_map/all_to_all | solution.py:179
  652.1 244.9 %all-reduce.10.cloned.1.call-start = ((), (), s32[]{:S(2)}) async-start(), calls=%async_computation.8 | async-start | bytes 3407872
  663.5 3.4 collective-permute-start.14
  664.1 2.8 collective-permute-start.15
  (134 other events, 3735.4 us)
Sparse Core Ops, SparseCore 0:
  13.5 147.4 all-reduce.7
  163.3 193.8 all-gather.3
  748.6 148.3 all-reduce.9
where the time goes:
time: 925 us; the launch traced here: 916 us
  waiting for transfers between devices  492 us (53%)
  other arithmetic  207 us (22%)
  matrix products  76.9 us (8%)
  starting transfers between devices  74.6 us (8%)
  local copies, waits for them, and re-layouts  41 us (4%)
  between operations  16.7 us (2%)
    unnamed x5, waiting for transfers between devices  280 us
    all_gather x1, waiting for transfers between devices, collect_rows(): piece = lax.all_gather(values, SEC_TILE, axis=0, tiled=True)  174 us
    add x1, other arithmetic, per_device(): cotangent + depthwise(rims(hidden_adjoint, radius), conv_kernel[layer, ::...  64 us
    mul x1, other arithmetic, per_device(): mask_value[:, :, None] * cotangent  59.1 us
    reduce_sum x2, other arithmetic, cell_forward(): center = hidden - jnp.mean(hidden, axis=-1, keepdims=True)  41.2 us
    dot_general x2, matrix products, cell_backward(): jnp.dot(before_adjoint, expand.T, preferred_element_type=jnp.float32)  29 us
    all_to_all x2, starting transfers between devices, to_bands(): lax.all_to_all(values, SEC_TILE, split_axis=0, concat_axis=1, tiled=True)  27.2 us
    all_to_all x2, starting transfers between devices, turned_blocks(): lax.all_to_all(blocks, axes[k], split_axis=k, concat_axis=k, tiled=True)  19 us
  transfers between devices with their start and end apart: 23, of which 12 were waited for; matrix products, arithmetic and copies ran while one was open for 8% of the time, Pallas kernels for 0%

commit v1 on v0

--- a/solution.py
+++ b/solution.py
@@ -1,37 +1,174 @@
 import jax
 import jax.numpy as jnp
 from jax import lax
-from jax.sharding import Mesh
+from jax.experimental import pallas as pl
+from jax.experimental.pallas import tpu as pltpu
 from jax.sharding import PartitionSpec as P
 
-SEC_TILE = ("sec", "tile_0", "tile_1", "tile_2", "tile_3")
-TILE = ("tile_0", "tile_1", "tile_2", "tile_3")
-
-
-def in_blocks(x, dim, size):
-    lengths = x.shape
-    blocks = x.reshape(*lengths[:dim], size, lengths[dim] // size, *lengths[dim + 1 :])
-    return jnp.moveaxis(blocks, dim, 0)
-
-
-def laid_out(blocks, dim):
-    lengths = list(blocks.shape[1:])
-    lengths[dim] *= blocks.shape[0]
-    return jnp.moveaxis(blocks, 0, dim).reshape(lengths)
-
-
-def turned_blocks(blocks, axes, sequence):
-    lengths = [lax.axis_size(a) for a in axes]
-    blocks = blocks.reshape(*lengths, *blocks.shape[1:])
-    for k in sequence:
-        blocks = lax.all_to_all(blocks, axes[k], split_axis=k, concat_axis=k, tiled=True)
-    return blocks.reshape(-1, *blocks.shape[len(axes) :])
-
-
-def two_step_exchange(x, groups, sequence, split_dim, concat_dim):
-    size = lax.axis_size(groups[0]) * lax.axis_size(groups[1])
-    blocks = in_blocks(x, split_dim, size)
-    return laid_out(turned_blocks(blocks, groups, sequence), concat_dim)
+SEC_TILE = ("sec", "tile")
+TILE = "tile"
+LOGICAL = pl.DeviceIdType.LOGICAL
+DEVICES = 128
+GROUPS = 64
+SLOTS = 8
+LANES = 256
+
+
+def remote(src, dst, send_sem, recv_sem, device):
+    return pltpu.make_async_remote_copy(
+        src_ref=src,
+        dst_ref=dst,
+        send_sem=send_sem,
+        recv_sem=recv_sem,
+        device_id=device,
+        device_id_type=LOGICAL,
+    )
+
+
+def all_to_all_kernel(x_ref, o_ref, landed, send_sem, recv_sem):
+    me = lax.axis_index("sec") * GROUPS + lax.axis_index("tile")
+    barrier = pltpu.get_barrier_semaphore()
+
+    def greet(i, carry):
+        pl.semaphore_signal(
+            barrier, inc=1, device_id=(me + i) % DEVICES, device_id_type=LOGICAL
+        )
+        return carry
+
+    lax.fori_loop(1, DEVICES, greet, 0)
+    pl.semaphore_wait(barrier, DEVICES - 1)
+
+    def send(i, carry):
+        peer = (me + i) % DEVICES
+        remote(x_ref.at[peer], landed.at[me], send_sem, recv_sem, peer).start()
+        return carry
+
+    lax.fori_loop(1, DEVICES, send, 0)
+    landed[me] = x_ref[me]
+    every = landed.at[pl.ds(0, DEVICES - 1)]
+    pltpu.make_async_copy(every, every, recv_sem).wait()
+    pltpu.make_async_copy(every, every, send_sem).wait()
+    o_ref[...] = landed[...]
+
+
+def all_to_all(blocks, number):
+    return pl.pallas_call(
+        all_to_all_kernel,
+        out_shape=jax.ShapeDtypeStruct(blocks.shape, blocks.dtype),
+        in_specs=[pl.BlockSpec(memory_space=pltpu.VMEM)],
+        out_specs=pl.BlockSpec(memory_space=pltpu.VMEM),
+        scratch_shapes=[
+            pltpu.VMEM(blocks.shape, blocks.dtype),
+            pltpu.SemaphoreType.DMA,
+            pltpu.SemaphoreType.DMA,
+        ],
+        compiler_params=pltpu.CompilerParams(collective_id=number, has_side_effects=True),
+        name=f"exchange_{number}",
+    )(blocks)
+
+
+def regrid_kernel(
+    rows_ref, parts_ref, gathered_ref, summed_ref, rows_in, parts_in, sems
+):
+    sec = lax.axis_index("sec")
+    group = lax.axis_index("tile")
+    me = sec * GROUPS + group
+    barrier = pltpu.get_barrier_semaphore()
+
+    def group_device(k):
+        return (k % 2) * GROUPS + (me // 2 + 1 - k // 2 + GROUPS) % GROUPS
+
+    def band_device(slot):
+        return (2 * group - 2 + slot + DEVICES) % DEVICES
+
+    mine = me * 0
+    for k in range(SLOTS):
+        for peer in (group_device(k), band_device(k)):
+            mine = mine + jnp.where(peer == me, 1, 0)
+
+            @pl.when(peer != me)
+            def _():
+                pl.semaphore_signal(barrier, inc=1, device_id=peer, device_id_type=LOGICAL)
+
+    pl.semaphore_wait(barrier, 2 * SLOTS - mine)
+
+    for k in range(SLOTS):
+        target = group_device(k)
+        slot = me % 2 + 2 * (k // 2)
+
+        @pl.when(target != me)
+        def _():
+            remote(
+                rows_ref.at[k % 2], rows_in.at[slot], sems.at[0, k], sems.at[1, slot], target
+            ).start()
+
+        @pl.when(target == me)
+        def _():
+            rows_in[slot] = rows_ref[k % 2]
+
+        band = band_device(k)
+        place = (k // 2) * 2 + sec
+
+        @pl.when(band != me)
+        def _():
+            remote(
+                parts_ref.at[k], parts_in.at[place], sems.at[2, k], sems.at[3, place], band
+            ).start()
+
+        @pl.when(band == me)
+        def _():
+            parts_in[place] = parts_ref[k]
+
+    for k in range(SLOTS):
+
+        @pl.when(band_device(k) != me)
+        def _():
+            remote(rows_ref.at[0], rows_in.at[k], sems.at[0, k], sems.at[1, k], me).wait_recv()
+            remote(parts_ref.at[k], parts_in.at[k], sems.at[2, k], sems.at[3, k], me).wait_send()
+
+        @pl.when(group_device(k) != me)
+        def _():
+            remote(rows_ref.at[0], rows_in.at[k], sems.at[0, k], sems.at[1, k], me).wait_send()
+            remote(parts_ref.at[k], parts_in.at[k], sems.at[2, k], sems.at[3, k], me).wait_recv()
+
+    gathered_ref[...] = rows_in[...]
+    for half in range(2):
+        total = parts_in[half]
+        for k in range(1, 4):
+            total = total + parts_in[2 * k + half]
+        summed_ref[half] = total
+
+
+def regrid(rows, parts, number):
+    _, r, lanes = rows.shape
+    _, q, _ = parts.shape
+    vmem = pl.BlockSpec(memory_space=pltpu.VMEM)
+    return pl.pallas_call(
+        regrid_kernel,
+        out_shape=(
+            jax.ShapeDtypeStruct((SLOTS, r, lanes), jnp.float32),
+            jax.ShapeDtypeStruct((2, q, lanes), jnp.float32),
+        ),
+        in_specs=[vmem, vmem],
+        out_specs=(vmem, vmem),
+        scratch_shapes=[
+            pltpu.VMEM((SLOTS, r, lanes), jnp.float32),
+            pltpu.VMEM((SLOTS, q, lanes), jnp.float32),
+            pltpu.SemaphoreType.DMA((4, SLOTS)),
+        ],
+        compiler_params=pltpu.CompilerParams(collective_id=number, has_side_effects=True),
+        name=f"regrid_{number}",
+    )(rows, parts)
+
+
+def slot_weights(bands_row, blocks, group):
+    slot = bands_row[:, None] - (2 * group - 2)
+    onehot = (slot == jnp.arange(SLOTS, dtype=jnp.int32)[None, :]).astype(jnp.float32)
+    return jnp.sum(onehot[:, :, None] * blocks[:, None, :], axis=0)
+
+
+def padded_lanes(values):
+    return jnp.pad(values, [(0, 0)] * (values.ndim - 1) + [(0, LANES - values.shape[-1])])
 
 
 def with_halo(x, sides, width, wrap):
@@ -105,24 +242,6 @@
     return result.astype(jnp.bfloat16)
 
 
-def ocean_matrix(bands_row, blocks, lat_count):
-    lat_band = blocks.shape[2]
-    index = bands_row[:, None] * lat_band + jnp.arange(lat_band, dtype=jnp.int32)[None, :]
-    onehot = (index[:, :, None] == jnp.arange(lat_count, dtype=jnp.int32)[None, None, :]).astype(
-        jnp.float32
-    )
-    return jnp.einsum("poi,pia->oa", blocks, onehot, precision=lax.Precision.HIGHEST)
-
-
-def atmosphere_matrix(bands_row, blocks, lat_count):
-    lat_band = blocks.shape[1]
-    index = bands_row[:, None] * lat_band + jnp.arange(lat_band, dtype=jnp.int32)[None, :]
-    onehot = (index[:, :, None] == jnp.arange(lat_count, dtype=jnp.int32)[None, None, :]).astype(
-        jnp.float32
-    )
-    return jnp.einsum("pio,pia->ao", blocks, onehot, precision=lax.Precision.HIGHEST)
-
-
 def mix_complex(coefficient, mix_real, mix_imag):
     real_part = coefficient[:, :, 0]
     imag_part = coefficient[:, :, 1]
@@ -169,45 +288,9 @@
     return spectrum_adjoint.reshape(lat_count, columns, channels)
 
 
-def to_modes(values):
-    return two_step_exchange(
-        values, (("sec", "tile_0", "tile_1", "tile_2"), "tile_3"), (1, 0), 1, 0
-    )
-
-
-def to_bands(values):
-    return lax.all_to_all(values, SEC_TILE, split_axis=0, concat_axis=1, tiled=True)
-
-
 def rims(values, width):
     with_rows = with_halo(values, ((TILE, 0),), width, False)
     return with_halo(with_rows, (("sec", 1),), width, True)
-
-
-def spread_rows(matrix, values):
-    return lax.psum_scatter(
-        jnp.dot(matrix, values, precision=lax.Precision.HIGHEST),
-        SEC_TILE,
-        scatter_dimension=0,
-        tiled=True,
-    )
-
-
-def collect_rows(matrix, values, lon_count, fields, offset, half):
-    piece = lax.all_gather(values, SEC_TILE, axis=0, tiled=True)
-    own = lax.dynamic_slice_in_dim(
-        piece.reshape(piece.shape[0], lon_count, fields), offset, half, 1
-    )
-    return jnp.dot(
-        matrix, own.reshape(piece.shape[0], half * fields), precision=lax.Precision.HIGHEST
-    )
-
-
-def place_half(values, lon_count, offset):
-    shape = (values.shape[0], lon_count) + values.shape[2:]
-    empty = jnp.zeros(shape, jnp.float32)
-    starts = (jnp.int32(0), offset) + tuple((jnp.int32(0) for extra in values.shape[2:]))
-    return lax.dynamic_update_slice(empty, values, starts)
 
 
 def per_device(
@@ -233,7 +316,6 @@
 ):
     band_total = lax.axis_size(SEC_TILE)
     lat_rows, lon_count, channels = atmosphere.shape
-    lat_count = lat_rows * band_total
     ocean_rows, ocean_lon, ocean_channels = ocean_state.shape
     half = lon_count // lax.axis_size("sec")
     offset = lax.axis_index("sec") * half
@@ -243,20 +325,24 @@
     layer_count = conv_kernel.shape[0]
     highest = lax.Precision.HIGHEST
     mask_value = land_mask.astype(jnp.float32)
-    to_ocean = ocean_matrix(crossing_bands[0], ocean_regrid[0], lat_count)
-    to_atmosphere = atmosphere_matrix(crossing_bands[0], atmosphere_regrid[0], lat_count)
+    group = lax.axis_index("tile")
+    to_ocean = slot_weights(crossing_bands[0], ocean_regrid[0, :, :, 0], group)
+    to_atmosphere = slot_weights(crossing_bands[0], atmosphere_regrid[0, :, 0, :], group)
     surface = jnp.dot(ocean_state, surface_read, preferred_element_type=jnp.float32)
     coarse = jnp.mean((mask_value * surface).reshape(ocean_rows, half, ratio), axis=2)
-    surface_atmosphere = spread_rows(to_atmosphere, place_half(coarse, lon_count, offset))
-    flux = jnp.einsum("agc,cf->agf", atmosphere, flux_read, preferred_element_type=jnp.float32)
-    flux_ocean = collect_rows(
-        to_ocean,
-        flux.reshape(lat_rows, lon_count * flux_count),
-        lon_count,
-        flux_count,
-        offset,
-        half,
-    )
+    flux = jnp.einsum(
+        "hgc,cf->hfg",
+        atmosphere.reshape(2, half, channels),
+        flux_read,
+        preferred_element_type=jnp.float32,
+    )
+    flux_rows, surface_rows = regrid(
+        padded_lanes(flux),
+        padded_lanes(jnp.dot(to_atmosphere, coarse, precision=highest))[:, None, :],
+        0,
+    )
+    surface_atmosphere = surface_rows[:, 0, :half].reshape(1, lon_count)
+    flux_ocean = jnp.einsum("so,sfg->ogf", to_ocean, flux_rows[:, :, :half], precision=highest)
     mixed_input = (
         atmosphere.astype(jnp.float32)
         + surface_atmosphere[:, :, None] * surface_embed[None, None, :]
@@ -265,14 +351,15 @@
     spectrum = jnp.einsum(
         "gk,agc->akc", table, mixed_input, preferred_element_type=jnp.float32
     ).astype(jnp.bfloat16)
-    returned = to_bands(
-        spectral_block(to_modes(spectrum), legendre_forward, legendre_inverse, spectral_mix)
-    )
+    modes = legendre_forward.shape[0] * band_total
+    at_modes = all_to_all(spectrum.reshape(modes, 2, channels), 1)
+    returned = spectral_block(at_modes, legendre_forward, legendre_inverse, spectral_mix)
+    returned = all_to_all(returned, 2).reshape(1, 2 * modes, channels)
     response = jnp.einsum("gk,akc->agc", table, returned, preferred_element_type=jnp.float32)
     atmosphere_next = (mixed_input.astype(jnp.float32) + jax.nn.gelu(response)).astype(jnp.bfloat16)
     forcing_coarse = jnp.einsum(
         "ogf,fc->ogc",
-        flux_ocean.reshape(ocean_rows, half, flux_count),
+        flux_ocean,
         flux_embed.astype(jnp.float32),
         precision=highest,
     )
@@ -313,13 +400,7 @@
         .sum(axis=2)
     )
     flux_ocean_adjoint = jnp.einsum(
-        "ogc,fc->ogf", forcing_adjoint, flux_embed.astype(jnp.float32), precision=highest
-    )
-    full_adjoint = place_half(flux_ocean_adjoint, lon_count, offset)
-    flux_adjoint = spread_rows(to_ocean.T, full_adjoint.reshape(ocean_rows, lon_count * flux_count))
-    flux_adjoint = flux_adjoint.reshape(lat_rows, lon_count, flux_count)
-    from_flux = jnp.einsum(
-        "agf,cf->agc", flux_adjoint, flux_read.astype(jnp.float32), precision=highest
+        "ogc,fc->ofg", forcing_adjoint, flux_embed.astype(jnp.float32), precision=highest
     )
     atmosphere_adjoint = atmosphere_cotangent.astype(jnp.float32)
     _, gelu_back = jax.vjp(jax.nn.gelu, response)
@@ -327,17 +408,29 @@
     returned_adjoint = jnp.einsum(
         "gk,agc->akc", table, response_adjoint, preferred_element_type=jnp.float32
     ).astype(jnp.bfloat16)
-    spectrum_adjoint = to_bands(
-        spectral_adjoint(
-            to_modes(returned_adjoint), legendre_forward, legendre_inverse, spectral_mix
-        )
-    )
+    at_modes_adjoint = all_to_all(returned_adjoint.reshape(modes, 2, channels), 3)
+    spectrum_adjoint = spectral_adjoint(
+        at_modes_adjoint, legendre_forward, legendre_inverse, spectral_mix
+    )
+    spectrum_adjoint = all_to_all(spectrum_adjoint, 4).reshape(1, 2 * modes, channels)
     input_adjoint = atmosphere_adjoint + jnp.einsum(
         "gk,akc->agc", table, spectrum_adjoint, preferred_element_type=jnp.float32
     )
+    surface_adjoint = jnp.einsum("agc,c->ag", input_adjoint, surface_embed, precision=highest)
+    parts = jnp.einsum("so,ofg->sfg", to_ocean, flux_ocean_adjoint, precision=highest)
+    surface_rows_adjoint, flux_adjoint = regrid(
+        padded_lanes(surface_adjoint.reshape(2, 1, half)), padded_lanes(parts), 5
+    )
+    from_flux = jnp.einsum(
+        "hfg,cf->hgc",
+        flux_adjoint[:, :, :half],
+        flux_read.astype(jnp.float32),
+        precision=highest,
+    ).reshape(1, lon_count, channels)
     atmosphere_grad = input_adjoint + from_flux
-    surface_adjoint = jnp.einsum("agc,c->ag", input_adjoint, surface_embed, precision=highest)
-    coarse_adjoint = collect_rows(to_atmosphere.T, surface_adjoint, lon_count, 1, offset, half)
+    coarse_adjoint = jnp.einsum(
+        "so,sg->og", to_atmosphere, surface_rows_adjoint[:, 0, :half], precision=highest
+    )
     widened_adjoint = jnp.broadcast_to(
         coarse_adjoint[:, :, None], (ocean_rows, half, ratio)
     ).reshape(ocean_rows, ocean_lon)
@@ -349,10 +442,6 @@
 
 
 def solution(mesh):
-    finer = Mesh(
-        mesh.devices.reshape(mesh.shape["sec"], 4, 2, 4, 2),
-        ("sec", "tile_0", "tile_1", "tile_2", "tile_3"),
-    )
     placed = (
         P(SEC_TILE, None, None),
         P(TILE, "sec", None),
@@ -376,7 +465,7 @@
     )
     return jax.shard_map(
         per_device,
-        mesh=finer,
+        mesh=mesh,
         in_specs=placed,
         out_specs=(
             P(SEC_TILE, None, None),

time: 925 us -> 478 us (0.52)
  waiting for transfers between devices: 492 us -> 7.83 us
  Pallas kernels: 0 us -> 103 us
  starting transfers between devices: 74.6 us -> 30.1 us
  between operations: 16.7 us -> 3.38 us
    unnamed x5 -> x0, waiting for transfers between devices: 280 us -> none
    all_gather x1 -> x0, waiting for transfers between devices: 174 us -> none  [collect_rows(): piece = lax.all_gather(values, SEC_TILE, axis=0, tiled=True)]
    pallas_call x0 -> x6, Pallas kernels: none -> 103 us  [the longest x4 63.5 us: all_to_all(): pl.pallas_call(all_to_all_kernel, out_shape=jax.ShapeDtypeStruct(blocks.s...]
    all_to_all x4 -> x0, starting transfers between devices: 46.2 us -> none  [the longest x2 27.2 us: to_bands(): lax.all_to_all(values, SEC_TILE, split_axis=0, concat_axis=1, tiled=True)]
    all_to_all x4 -> x0, waiting for transfers between devices: 20.4 us -> none  [the longest x2 12.1 us: turned_blocks(): lax.all_to_all(blocks, axes[k], split_axis=k, concat_axis=k, tiled=True)]
  transfers between devices with their start and end apart: 23 -> 16, of which waited for: 12 -> 7; matrix products, arithmetic and copies ran while one was open for 8% -> 11% of each run, Pallas kernels for 0% -> 14%
where the time goes in v1:
time: 478 us; the launch traced here: 469 us
  other arithmetic  216 us (45%)
  Pallas kernels  103 us (22%)
  matrix products  74.1 us (16%)
  local copies, waits for them, and re-layouts  34.8 us (7%)
  starting transfers between devices  30.1 us (6%)
  waiting for transfers between devices  7.83 us (2%)
    pallas_call x4, Pallas kernels, all_to_all(): pl.pallas_call(all_to_all_kernel, out_shape=jax.ShapeDtypeStruct(blocks.s...  63.5 us
    add x1, other arithmetic, per_device(): cotangent + depthwise(rims(hidden_adjoint, radius), conv_kernel[layer, ::...  60.9 us
    mul x1, other arithmetic, per_device(): mask_value[:, :, None] * cotangent  60.7 us
    reduce_sum x2, other arithmetic, cell_forward(): center = hidden - jnp.mean(hidden, axis=-1, keepdims=True)  41.5 us
    pallas_call x2, Pallas kernels, regrid(): pl.pallas_call(regrid_kernel, out_shape=(jax.ShapeDtypeStruct((SLOTS, r,...  39.6 us
    dot_general x2, matrix products, cell_backward(): jnp.dot(before_adjoint, expand.T, preferred_element_type=jnp.float32)  28.6 us
    ppermute x8, starting transfers between devices, with_halo(): after = lax.ppermute(first, axis, down)  15.6 us
    ppermute x8, starting transfers between devices, with_halo(): before = lax.ppermute(last, axis, up)  14.6 us
  transfers between devices with their start and end apart: 16, of which 7 were waited for; matrix products, arithmetic and copies ran while one was open for 11% of the time, Pallas kernels for 14%

profile of v1, /device:TPU:1, one launch (start us, length us, event | category | flops | bytes accessed | tf_op | source)
XLA Modules:
  0.0 469.3 jit_solution(6516605464875508809)
XLA Ops:
  8.9 15.5 %regrid_0.1 = (f32[8,8,256]{2,1,0:T(8,128)}, f32[2,1,256]{2,1,0:T(1,128)}) custom-call(f32[2,8,256]{2,1,0:T(8,128)} %pad.16.rows_ref, f32[8,1,256]{2,1,0:T(1,128)} %broadcast_in_dim.6.parts_ref), custom_call_target="tpu_custom_call" | custom-call | tf_op jit(solution)/shard_map/regrid_0/pallas_call | solution.py:146
  31.4 3.3 collective-permute-start
  43.7 18.5 %exchange_1.1 = bf16[128,2,384]{2,1,0:T(2,128)(2,1)} custom-call(bf16[128,2,384]{2,1,0:T(2,128)(2,1)} %reshape.381.x_ref), custom_call_target="tpu_custom_call" | custom-call | tf_op jit(solution)/shard_map/exchange_1/pallas_call | solution.py:55
  69.7 13.5 %exchange_2.1 = bf16[128,2,384]{2,1,0:T(2,128)(2,1)} custom-call(bf16[128,2,384]{2,1,0:T(2,128)(2,1)} %bitcast.600), custom_call_target="tpu_custom_call" | custom-call | tf_op jit(solution)/shard_map/exchange_2/pallas_call | solution.py:55
  87.7 14.2 %exchange_3.1 = bf16[128,2,384]{2,1,0:T(2,128)(2,1)} custom-call(bf16[128,2,384]{2,1,0:T(2,128)(2,1)} %reshape.389.x_ref), custom_call_target="tpu_custom_call" | custom-call | tf_op jit(solution)/shard_map/exchange_3/pallas_call | solution.py:55
  114.3 20.9 %fusion.373 = (f32[8,720]{1,0:T(8,128)S(1)}, f32[8,720,128]{2,1,0:T(8,128)S(1)}) fusion(f32[128]{0:T(128)S(1)} %copy-done.80, f32[14,726,128]{2,1,0:T(8,128)S(1)} %maximum_convert_fusion, f32[128]{0:T(128)S(1)} %copy-done.81, f32[128]{0:T(128)S(1)} %copy-done.82, f32[128]{0:T(128)S(1)} %copy-done.83, f32[128]{0:T(128)S(1)} %copy-done.84, ...), kind=kLoop, calls=%fused_computation.843 | loop fusion | flops 72247680 | bytes 147504128 | tf_op jit(solution)/shard_map/reduce_sum | solution.py:217
  138.9 4.9 %add_convert_fusion.1 = bf16[8,720,128]{2,1,0:T(8,128)(2,1)S(1)} fusion(bf16[8,720,128]{2,1,0:T(8,128)(2,1)S(1)} %copy-done.4, f32[8,720,512]{2,1,0:T(8,128)S(1)} %fusion.218, f32[8,720]{1,0:T(8,128)S(1)} %convert_element_type.234, bf16[2,512,128]{2,1,0:T(8,128)(2,1)S(1)} %copy-done.147), kind=kOutput, calls=%fused_computation.427 | convolution fusion | flops 784465920 | bytes 14901248 | tf_op jit(solution)/shard_map/dot_general | solution.py:222
  145.3 3.7 collective-permute-start.5
  153.6 17.3 %exchange_4.1 = bf16[128,2,384]{2,1,0:T(2,128)(2,1)} custom-call(bf16[128,2,384]{2,1,0:T(2,128)(2,1)} %bitcast.601), custom_call_target="tpu_custom_call" | custom-call | tf_op jit(solution)/shard_map/exchange_4/pallas_call | solution.py:55
  181.9 20.6 %fusion.371 = (f32[8,720]{1,0:T(8,128)S(1)}, f32[8,720,128]{2,1,0:T(8,128)S(1)}) fusion(f32[128]{0:T(128)S(1)} %copy-done.42, f32[14,726,128]{2,1,0:T(8,128)S(1)} %maximum_convert_fusion.1, f32[128]{0:T(128)S(1)} %copy-done.43, f32[128]{0:T(128)S(1)} %copy-done.44, f32[128]{0:T(128)S(1)} %copy-done.45, f32[128]{0:T(128)S(1)} %copy-done.46, ...), kind=kLoop, calls=%fused_computation.842 | loop fusion | flops 72247680 | bytes 147504128 | tf_op jit(solution)/shard_map/reduce_sum | solution.py:217
  205.0 5.4 %fusion.219 = f32[8,720,512]{2,1,0:T(8,128)} fusion(f32[8,720,128]{2,1,0:T(8,128)S(1)} %get-tuple-element.21, f32[128]{0:T(128)S(1)} %get-tuple-element.242, f32[8,720]{1,0:T(8,128)S(1)} %add_rsqrt_fusion, f32[8,720]{1,0:T(8,128)S(1)} %broadcast_multiply_fusion.5, bf16[2,128,512]{2,1,0:T(8,128)(2,1)S(1)} %copy-done.17), kind=kOutput, calls=%fused_computation.440 | convolution fusion | flops 757923840 | bytes 14926336 | tf_op jit(solution)/shard_map/dot_general | solution.py:220
  210.4 14.5 %multiply_reduce_fusion.5 = (f32[8,720]{1,0:T(8,128)}, f32[8,720]{1,0:T(8,128)}, f32[8,720,128]{2,1,0:T(8,128)}) fusion(f32[128]{0:T(128)S(1)} %get-tuple-element.242, f32[8,720]{1,0:T(8,128)} %copy-done.20, f32[8,720,128]{2,1,0:T(8,128)} %copy-done.2, f32[8,720]{1,0:T(8,128)} %copy-done.15, bf16[2,128,512]{2,1,0:T(8,128)(2,1)} %param.34, ...), kind=kOutput, calls=%fused_computation.438 | convolution fusion | flops 1575555840 | bytes 19551744 | tf_op jit(solution)/shard_map/dot_general | solution.py:235
  226.3 6.9 %multiply_convert_fusion.6 = bf16[8,720,128]{2,1,0:T(8,128)(2,1)S(1)} fusion(f32[8,720,128]{2,1,0:T(8,128)} %get-tuple-element.246, f32[8,720,128]{2,1,0:T(8,128)} %copy-done.2, f32[8,720]{1,0:T(8,128)S(1)} %broadcast_multiply_fusion.3, f32[8,720]{1,0:T(8,128)S(1)} %broadcast_multiply_fusion.4, f32[128]{0:T(128)S(1)} %get-tuple-element.242, ...), kind=kLoop, calls=%fused_computation.422 | loop fusion | flops 5898240 | bytes 7465472 | tf_op jit(solution)/shard_map/convert_element_type | solution.py:242
  235.4 3.6 collective-permute-start.9
  254.8 4.4 maximum_convert_fusion.2
  259.4 60.9 %convert_add_fusion = f32[8,720,128]{2,1,0:T(8,128)} fusion(bf16[8,720,128]{2,1,0:T(8,128)(2,1)S(1)} %copy-done.14, f32[14,726,128]{2,1,0:T(8,128)} %maximum_convert_fusion.2, f32[128]{0:T(128)S(1)} %copy-done.61, f32[128]{0:T(128)S(1)} %copy-done.62, f32[128]{0:T(128)S(1)} %copy-done.63, f32[128]{0:T(128)S(1)} %copy-done.64, f32[128]{0:T(128)S(1)} %copy-done.65, ...), kind=kLoop, calls=%fused_computation.26 | loop fusion | flops 72990720 | bytes 148955648 | tf_op jit(solution)/shard_map/add | solution.py:394
  320.3 14.2 %multiply_reduce_fusion.4 = (f32[8,720]{1,0:T(8,128)}, f32[8,720]{1,0:T(8,128)}, f32[8,720,128]{2,1,0:T(8,128)}) fusion(f32[128]{0:T(128)S(1)} %get-tuple-element.243, f32[8,720]{1,0:T(8,128)} %copy-done.19, f32[8,720,128]{2,1,0:T(8,128)S(1)} %get-tuple-element.25, f32[8,720]{1,0:T(8,128)S(1)} %broadcast_multiply_fusion.6, ...), kind=kOutput, calls=%fused_computation.437 | convolution fusion | flops 1574818560 | bytes 21024768 | tf_op jit(solution)/shard_map/dot_general | solution.py:235
  336.0 7.1 %multiply_convert_fusion.4 = bf16[8,720,128]{2,1,0:T(8,128)(2,1)S(1)} fusion(f32[8,720,128]{2,1,0:T(8,128)} %get-tuple-element.247, f32[8,720,128]{2,1,0:T(8,128)S(1)} %get-tuple-element.25, f32[8,720]{1,0:T(8,128)S(1)} %broadcast_multiply_fusion.1, f32[8,720]{1,0:T(8,128)S(1)} %broadcast_multiply_fusion.2, f32[128]{0:T(128)S(1)} %get-tuple-element.243, ...), kind=kLoop, calls=%fused_computation.419 | loop fusion | flops 5898240 | bytes 7465472 | tf_op jit(solution)/shard_map/convert_element_type | solution.py:242
  345.8 3.2 collective-permute-start.12
  357.1 7.9 %add_convert_fusion = bf16[8,720,128]{2,1,0:T(8,128)(2,1)} fusion(bf16[8,720,128]{2,1,0:T(8,128)(2,1)S(1)} %copy-done.10, f32[8,720,512]{2,1,0:T(8,128)} %fusion.219, f32[8,720]{1,0:T(8,128)S(1)} %copy-done.22, bf16[2,512,128]{2,1,0:T(8,128)(2,1)S(1)} %copy-done.148), kind=kOutput, calls=%fused_computation.424 | convolution fusion | flops 784465920 | bytes 14901248 | tf_op jit(solution)/shard_map/dot_general | solution.py:222
  365.0 3.5 maximum_convert_fusion.3
  368.5 60.7 %broadcast_multiply_fusion = (f32[8,720,128]{2,1,0:T(8,128)}, f32[8,720,128]{2,1,0:T(8,128)S(1)}) fusion(f32[8,720]{1,0:T(8,128)S(1)} %copy-done.22, f32[8,720,128]{2,1,0:T(8,128)} %convert_add_fusion, f32[128]{0:T(128)} %get-tuple-element.45, f32[14,726,128]{2,1,0:T(8,128)} %maximum_convert_fusion.3, f32[128]{0:T(128)} %get-tuple-element.46, ...), kind=kLoop, calls=%fused_computation.447 | loop fusion | flops 72990720 | bytes 153402368 | tf_op jit(solution)/shard_map/mul | solution.py:398
  429.2 4.5 reduce_sum.135
  436.4 24.2 %regrid_5.1 = (f32[8,1,256]{2,1,0:T(1,128)}, f32[2,8,256]{2,1,0:T(8,128)}) custom-call(f32[2,1,256]{2,1,0:T(1,128)} %pad.18.rows_ref, f32[8,8,256]{2,1,0:T(8,128)} %pad.19.parts_ref), custom_call_target="tpu_custom_call" | custom-call | tf_op jit(solution)/shard_map/regrid_5/pallas_call | solution.py:146
  (429 shorter events, 112.8 us)
Async XLA Ops:
  0.6 66.4 %copy-start = (bf16[1,128,128]{2,1,0:T(8,128)(2,1)S(1)}, bf16[1,128,128]{2,1,0:T(8,128)(2,1)}, u32[]{:S(2)}) copy-start(bf16[1,128,128]{2,1,0:T(8,128)(2,1)} %param.30) | copy-start | bytes 98308
  3.2 135.6 %copy-start.21 = (f32[8,720]{1,0:T(8,128)}, f32[8,720]{1,0:T(8,128)S(1)}, u32[]{:S(2)}) copy-start(f32[8,720]{1,0:T(8,128)S(1)} %convert_element_type.234) | copy-start | bytes 69124
  27.9 84.1 %copy-start.3 = (bf16[8,720,128]{2,1,0:T(8,128)(2,1)}, bf16[8,720,128]{2,1,0:T(8,128)(2,1)S(1)}, u32[]{:S(2)}) copy-start(bf16[8,720,128]{2,1,0:T(8,128)(2,1)S(1)} %add_convert_fusion.2) | copy-start | bytes 4423684
  27.9 34.3 %copy-start.23 = (bf16[1,128,128]{2,1,0:T(8,128)(2,1)S(1)}, bf16[1,128,128]{2,1,0:T(8,128)(2,1)}, u32[]{:S(2)}) copy-start(bf16[1,128,128]{2,1,0:T(8,128)(2,1)} %param.29) | copy-start | bytes 98308
  27.9 35.5 %copy-start.11 = (bf16[2,384,384]{2,1,0:T(8,128)(2,1)S(1)}, bf16[2,384,384]{2,1,0:T(8,128)(2,1)}, u32[]{:S(2)}) copy-start(bf16[2,384,384]{2,1,0:T(8,128)(2,1)} %param.31) | copy-start | bytes 1769476
  29.0 34.9 %copy-start.26 = (bf16[2,7,7,128]{3,0,2,1:T(2,128)(2,1)S(1)}, bf16[2,7,7,128]{3,0,2,1:T(2,128)(2,1)}, u32[]{:S(2)}) copy-start(bf16[2,7,7,128]{3,0,2,1:T(2,128)(2,1)} %param.32) | copy-start | bytes 75268
  29.0 79.1 %collective-permute-start.1 = (bf16[3,720,128]{2,1,0:T(8,128)(2,1)}, bf16[3,720,128]{2,1,0:T(8,128)(2,1)S(1)}, u32[]{:S(2)}, u32[]{:S(2)}) collective-permute-start(bf16[3,720,128]{2,1,0:T(8,128)(2,1)} %get-tuple-element.43), channel_id=1, source_target_pairs={{1,0},{2,1},{3,2},{4,3},{5,4},{6,5},{7,6},{8,7},{9,8},{10,9},{11,1... | collective-permute-start | bytes 1658888 | tf_op jit(solution)/shard_map/ppermute | solution.py:182
  31.4 76.7 %collective-permute-start = (bf16[3,720,128]{2,1,0:T(8,128)(2,1)}, bf16[3,720,128]{2,1,0:T(8,128)(2,1)S(1)}, u32[]{:S(2)}, u32[]{:S(2)}) collective-permute-start(bf16[3,720,128]{2,1,0:T(8,128)(2,1)} %get-tuple-element.42), channel_id=1, source_target_pairs={{0,1},{1,2},{2,3},{3,4},{4,5},{5,6},{6,7},{7,8},{8,9},{9,10},{10,1... | collective-permute-start | bytes 1658888 | tf_op jit(solution)/shard_map/ppermute | solution.py:181
  37.4 45.8 %copy-start.13 = (bf16[360,128,2]{1,0,2:T(8,128)(2,1)}, bf16[360,128,2]{1,0,2:T(8,128)(2,1)S(1)}, u32[]{:S(2)}) copy-start(bf16[360,128,2]{1,0,2:T(8,128)(2,1)S(1)} %fusion.255) | copy-start | bytes 552964
  64.6 39.8 %copy-start.24 = (f32[7,7,128]{2,1,0:T(8,128)}, f32[7,7,128]{2,1,0:T(8,128)S(1)}, u32[]{:S(2)}) copy-start(f32[7,7,128]{2,1,0:T(8,128)S(1)} %get-tuple-element.22) | copy-start | bytes 75268
  108.1 3.1 collective-permute-start.3
  108.9 3.0 collective-permute-start.2
  145.3 28.7 %collective-permute-start.5 = (bf16[3,720,128]{2,1,0:T(8,128)(2,1)}, bf16[3,720,128]{2,1,0:T(8,128)(2,1)}, u32[]{:S(2)}, u32[]{:S(2)}) collective-permute-start(bf16[3,720,128]{2,1,0:T(8,128)(2,1)} %get-tuple-element.41), channel_id=1, source_target_pairs={{1,0},{2,1},{3,2},{4,3},{5,4},{6,5},{7,6},{8,7},{9,8},{10,9},{11,1... | collective-permute-start | bytes 1658888 | tf_op jit(solution)/shard_map/ppermute | solution.py:182
  149.0 25.0 %collective-permute-start.4 = (bf16[3,720,128]{2,1,0:T(8,128)(2,1)}, bf16[3,720,128]{2,1,0:T(8,128)(2,1)}, u32[]{:S(2)}, u32[]{:S(2)}) collective-permute-start(bf16[3,720,128]{2,1,0:T(8,128)(2,1)} %get-tuple-element.40), channel_id=1, source_target_pairs={{0,1},{1,2},{2,3},{3,4},{4,5},{5,6},{6,7},{7,8},{8,9},{9,10},{10,1... | collective-permute-start | bytes 1658888 | tf_op jit(solution)/shard_map/ppermute | solution.py:181
  174.8 3.0 collective-permute-start.7
  175.7 2.9 collective-permute-start.6
  235.4 12.0 %collective-permute-start.9 = (bf16[3,720,128]{2,1,0:T(8,128)(2,1)}, bf16[3,720,128]{2,1,0:T(8,128)(2,1)}, u32[]{:S(2)}, u32[]{:S(2)}) collective-permute-start(bf16[3,720,128]{2,1,0:T(8,128)(2,1)} %get-tuple-element.39), channel_id=1, source_target_pairs={{1,0},{2,1},{3,2},{4,3},{5,4},{6,5},{7,6},{8,7},{9,8},{10,9},{11,1... | collective-permute-start | bytes 1658888 | tf_op jit(solution)/shard_map/ppermute | solution.py:182
  238.9 8.8 %collective-permute-start.8 = (bf16[3,720,128]{2,1,0:T(8,128)(2,1)}, bf16[3,720,128]{2,1,0:T(8,128)(2,1)}, u32[]{:S(2)}, u32[]{:S(2)}) collective-permute-start(bf16[3,720,128]{2,1,0:T(8,128)(2,1)} %get-tuple-element.38), channel_id=1, source_target_pairs={{0,1},{1,2},{2,3},{3,4},{4,5},{5,6},{6,7},{7,8},{8,9},{9,10},{10,1... | collective-permute-start | bytes 1658888 | tf_op jit(solution)/shard_map/ppermute | solution.py:181
  248.5 5.9 %collective-permute-start.11 = (bf16[14,3,128]{2,1,0:T(4,128)(2,1)S(1)}, bf16[14,3,128]{2,1,0:T(4,128)(2,1)S(1)}, u32[]{:S(2)}, u32[]{:S(2)}) collective-permute-start(bf16[14,3,128]{2,1,0:T(4,128)(2,1)S(1)} %get-tuple-element.31), channel_id=1, source_target_pairs={{64,0},{0,64},{65,1},{1,65},{66,2},{2,66},{67,3},{3,67},{68,4},{4,... | collective-permute-start | bytes 32264 | tf_op jit(solution)/shard_map/ppermute | solution.py:182
  249.4 5.4 %collective-permute-start.10 = (bf16[14,3,128]{2,1,0:T(4,128)(2,1)S(1)}, bf16[14,3,128]{2,1,0:T(4,128)(2,1)S(1)}, u32[]{:S(2)}, u32[]{:S(2)}) collective-permute-start(bf16[14,3,128]{2,1,0:T(4,128)(2,1)S(1)} %get-tuple-element.30), channel_id=1, source_target_pairs={{0,64},{64,0},{1,65},{65,1},{2,66},{66,2},{3,67},{67,3},{4,68},{68... | collective-permute-start | bytes 32264 | tf_op jit(solution)/shard_map/ppermute | solution.py:181
  343.2 10.9 %collective-permute-start.13 = (bf16[3,720,128]{2,1,0:T(8,128)(2,1)S(1)}, bf16[3,720,128]{2,1,0:T(8,128)(2,1)S(1)}, u32[]{:S(2)}, u32[]{:S(2)}) collective-permute-start(bf16[3,720,128]{2,1,0:T(8,128)(2,1)S(1)} %get-tuple-element.37), channel_id=1, source_target_pairs={{1,0},{2,1},{3,2},{4,3},{5,4},{6,5},{7,6},{8,7},{9,8},{10,9},{11,1... | collective-permute-start | bytes 1658888 | tf_op jit(solution)/shard_map/ppermute | solution.py:182
  345.8 9.6 %collective-permute-start.12 = (bf16[3,720,128]{2,1,0:T(8,128)(2,1)S(1)}, bf16[3,720,128]{2,1,0:T(8,128)(2,1)S(1)}, u32[]{:S(2)}, u32[]{:S(2)}) collective-permute-start(bf16[3,720,128]{2,1,0:T(8,128)(2,1)S(1)} %get-tuple-element.36), channel_id=1, source_target_pairs={{0,1},{1,2},{2,3},{3,4},{4,5},{5,6},{6,7},{7,8},{8,9},{9,10},{10,1... | collective-permute-start | bytes 1658888 | tf_op jit(solution)/shard_map/ppermute | solution.py:181
  355.4 9.6 %collective-permute-start.15 = (bf16[14,3,128]{2,1,0:T(4,128)(2,1)S(1)}, bf16[14,3,128]{2,1,0:T(4,128)(2,1)S(1)}, u32[]{:S(2)}, u32[]{:S(2)}) collective-permute-start(bf16[14,3,128]{2,1,0:T(4,128)(2,1)S(1)} %get-tuple-element.29), channel_id=1, source_target_pairs={{64,0},{0,64},{65,1},{1,65},{66,2},{2,66},{67,3},{3,67},{68,4},{4,... | collective-permute-start | bytes 32264 | tf_op jit(solution)/shard_map/ppermute | solution.py:182
  356.1 8.9 %collective-permute-start.14 = (bf16[14,3,128]{2,1,0:T(4,128)(2,1)S(1)}, bf16[14,3,128]{2,1,0:T(4,128)(2,1)S(1)}, u32[]{:S(2)}, u32[]{:S(2)}) collective-permute-start(bf16[14,3,128]{2,1,0:T(4,128)(2,1)S(1)} %get-tuple-element.28), channel_id=1, source_target_pairs={{0,64},{64,0},{1,65},{65,1},{2,66},{66,2},{3,67},{67,3},{4,68},{68... | collective-permute-start | bytes 32264 | tf_op jit(solution)/shard_map/ppermute | solution.py:181
  (141 other events, 849.1 us)

commit v2 on v1

--- a/solution.py
+++ b/solution.py
@@ -1,3 +1,5 @@
+import functools
+
 import jax
 import jax.numpy as jnp
 from jax import lax
@@ -161,6 +163,427 @@
     )(rows, parts)
 
 
+X = 144
+CHUNKS = 5
+ROWS = 8
+WIDE = 736
+EDGE = 8
+CELL = 128
+TAPS = 7
+REACH = 3
+
+
+def spread_taps(bands, taps_ref, layer, flipped):
+    eye = lax.broadcasted_iota(jnp.int32, (CELL, CELL), 0) == lax.broadcasted_iota(
+        jnp.int32, (CELL, CELL), 1
+    )
+
+    def one(v, carry):
+        for u in range(TAPS):
+            if flipped:
+                row = taps_ref[layer, pl.ds((TAPS - 1 - u) * TAPS + (TAPS - 1) - v, 1), :]
+            else:
+                row = taps_ref[layer, pl.ds(u * TAPS + v, 1), :]
+            block = jnp.where(eye, row, 0.0).astype(jnp.bfloat16)
+            for q in range(2):
+                bands[v, pl.ds((u + q) * CELL, CELL), pl.ds(q * CELL, CELL)] = block
+        return carry
+
+    lax.fori_loop(0, TAPS, one, 0)
+
+
+def convolve(window, bands, hidden, x0):
+    total = None
+    for v in range(TAPS):
+        rows = [
+            window[r, pl.ds(x0 + EDGE - REACH + v, X), :].astype(jnp.bfloat16)
+            for r in range(ROWS + 2 * REACH)
+        ]
+        left = jnp.concatenate(
+            [jnp.concatenate(rows[2 * p : 2 * p + 8], axis=1) for p in range(ROWS // 2)], axis=0
+        )
+        part = jnp.dot(left, bands[v], preferred_element_type=jnp.float32)
+        total = part if total is None else total + part
+    for p in range(ROWS // 2):
+        for q in range(2):
+            hidden[2 * p + q] = total[p * X : (p + 1) * X, q * CELL : (q + 1) * CELL]
+
+
+def normalized(hidden):
+    center = hidden - jnp.mean(hidden, axis=-1, keepdims=True)
+    rstd = lax.rsqrt(jnp.mean(center * center, axis=-1, keepdims=True) + 1e-06)
+    return center * rstd, rstd
+
+
+GELU_A = 0.7978845608028654
+GELU_B = GELU_A * 0.044715
+
+
+def gelu_pair(v):
+    square = v * v
+    t = jnp.tanh(v * (GELU_A + GELU_B * square))
+    half = 0.5 * v
+    value = half + half * t
+    slope = (0.5 + 0.5 * t) + (half * (1.0 - t * t)) * (GELU_A + (3.0 * GELU_B) * square)
+    return value, slope
+
+
+def dot32(a, b):
+    return jnp.dot(a, b, preferred_element_type=jnp.float32)
+
+
+def dot_t(a, b):
+    return lax.dot_general(a, b, (((1,), (1,)), ((), ())), preferred_element_type=jnp.float32)
+
+
+def adjoint_cell(masked, slope, unit, rstd, gain, expand, project):
+    before_adj = (slope * dot_t(masked, project)).astype(jnp.bfloat16)
+    scaled = dot_t(before_adj, expand) * gain
+    inner = jnp.mean(scaled * unit, axis=-1, keepdims=True)
+    return (rstd * (scaled - jnp.mean(scaled, axis=-1, keepdims=True) - unit * inner)).astype(
+        jnp.bfloat16
+    )
+
+
+def ocean_kernel(
+    linked,
+    state_ref,
+    mask_ref,
+    cot_ref,
+    taps_ref,
+    gain_ref,
+    expand_ref,
+    project_ref,
+    next_ref,
+    grad_ref,
+    win_a,
+    win_b,
+    bands,
+    hidden,
+    unit_0,
+    rstd_0,
+    slope_0,
+    out_rows,
+    in_rows,
+    in_cols,
+    row_sems,
+    col_sems,
+):
+    sec = lax.axis_index("sec") if linked else 0
+    tile = lax.axis_index("tile") if linked else 0
+    last_tile = GROUPS - 1 if linked else 0
+    me = sec * GROUPS + tile
+    side = (1 - sec) * GROUPS + tile
+    windows = (win_a, win_b)
+
+    if linked:
+        barrier = pltpu.get_barrier_semaphore()
+        pl.semaphore_signal(barrier, inc=1, device_id=side, device_id_type=LOGICAL)
+
+        @pl.when(tile > 0)
+        def _():
+            for peer in (me - 1, side - 1):
+                pl.semaphore_signal(barrier, inc=1, device_id=peer, device_id_type=LOGICAL)
+
+        @pl.when(tile < last_tile)
+        def _():
+            for peer in (me + 1, side + 1):
+                pl.semaphore_signal(barrier, inc=1, device_id=peer, device_id_type=LOGICAL)
+
+    zero_rows = jnp.zeros((REACH, WIDE, CELL), jnp.float32)
+
+    @pl.when(tile == 0)
+    def _():
+        for w in windows:
+            w[0:REACH] = zero_rows
+
+    @pl.when(tile == last_tile)
+    def _():
+        for w in windows:
+            w[REACH + ROWS :] = zero_rows
+
+    if not linked:
+        for w in windows:
+            w[:, 0:EDGE] = jnp.zeros((14, EDGE, CELL), jnp.float32)
+            w[:, WIDE - EDGE :] = jnp.zeros((14, EDGE, CELL), jnp.float32)
+    for v in range(TAPS):
+        bands[v, 0:CELL, CELL:] = jnp.zeros((CELL, CELL), jnp.bfloat16)
+        bands[v, 7 * CELL :, :CELL] = jnp.zeros((CELL, CELL), jnp.bfloat16)
+
+    if linked:
+        count = 1 + jnp.where(tile > 0, 2, 0) + jnp.where(tile < last_tile, 2, 0)
+        pl.semaphore_wait(barrier, count)
+
+    def row_copy(e, way, c, peer):
+        x0 = pl.multiple_of(c * X, 16)
+        return remote(
+            out_rows.at[e, pl.ds(0 if way == 0 else ROWS - REACH, REACH), pl.ds(x0, X)],
+            in_rows.at[e, way, :, pl.ds(x0, X)],
+            row_sems.at[0, e, way, c],
+            row_sems.at[1, e, way, c],
+            peer,
+        )
+
+    def col_copy(e, edge, part, peer):
+        source = windows[e % 2]
+        first, size, place = ((0, ROWS, REACH), (0, REACH, REACH + ROWS), (ROWS - REACH, REACH, 0))[
+            part
+        ]
+        return remote(
+            source.at[
+                pl.ds(REACH + first, size), pl.ds(EDGE if edge == 0 else WIDE - 2 * EDGE, EDGE)
+            ],
+            in_cols.at[e, edge, pl.ds(place, size)],
+            col_sems.at[0, e, edge, part],
+            col_sems.at[1, e, edge, part],
+            peer,
+        )
+
+    def send_chunk(e, k, c):
+        if not linked:
+            return
+
+        @pl.when(tile > 0)
+        def _():
+            row_copy(e, 0, c, me - 1).start()
+
+        @pl.when(tile < last_tile)
+        def _():
+            row_copy(e, 1, c, me + 1).start()
+
+        for edge in range(2):
+
+            @pl.when(k == edge)
+            def _():
+                col_copy(e, edge, 0, side).start()
+
+                @pl.when(tile > 0)
+                def _():
+                    col_copy(e, edge, 1, side - 1).start()
+
+                @pl.when(tile < last_tile)
+                def _():
+                    col_copy(e, edge, 2, side + 1).start()
+
+    def take_rows(e, c):
+        x0 = pl.multiple_of(c * X, 16)
+        window = windows[e % 2]
+
+        @pl.when(tile > 0)
+        def _():
+            row_copy(e, 1, c, me - 1).wait_recv()
+            window[0:REACH, pl.ds(EDGE + x0, X), :] = in_rows[e, 1, :, pl.ds(x0, X), :].astype(
+                jnp.float32
+            )
+
+        @pl.when(tile < last_tile)
+        def _():
+            row_copy(e, 0, c, me + 1).wait_recv()
+            window[REACH + ROWS :, pl.ds(EDGE + x0, X), :] = in_rows[
+                e, 0, :, pl.ds(x0, X), :
+            ].astype(jnp.float32)
+
+    def take_cols(e, edge):
+        window = windows[e % 2]
+        at = pl.ds(0 if edge == 1 else WIDE - EDGE, EDGE)
+        col_copy(e, edge, 0, side).wait_recv()
+        window[pl.ds(REACH, ROWS), at, :] = in_cols[e, edge, pl.ds(REACH, ROWS)]
+
+        @pl.when(tile > 0)
+        def _():
+            col_copy(e, edge, 2, side - 1).wait_recv()
+            window[pl.ds(0, REACH), at, :] = in_cols[e, edge, pl.ds(0, REACH)]
+
+        @pl.when(tile < last_tile)
+        def _():
+            col_copy(e, edge, 1, side + 1).wait_recv()
+            window[pl.ds(REACH + ROWS, REACH), at, :] = in_cols[
+                e, edge, pl.ds(REACH + ROWS, REACH)
+            ]
+
+    def take_halo(e, k):
+        if not linked:
+            return
+
+        @pl.when(k == 0)
+        def _():
+            take_rows(e, 0)
+            take_rows(e, 1)
+            take_cols(e, 1)
+
+        @pl.when(k == 1)
+        def _():
+            take_rows(e, CHUNKS - 1)
+            take_rows(e, CHUNKS - 2)
+            take_cols(e, 0)
+
+        @pl.when(k == 2)
+        def _():
+            take_rows(e, CHUNKS // 2)
+
+    def sent(e):
+        if not linked:
+            return
+
+        def one(c, carry):
+            @pl.when(tile > 0)
+            def _():
+                row_copy(e, 0, c, me - 1).wait_send()
+
+            @pl.when(tile < last_tile)
+            def _():
+                row_copy(e, 1, c, me + 1).wait_send()
+
+            return carry
+
+        lax.fori_loop(0, CHUNKS, one, 0)
+        for edge in range(2):
+            col_copy(e, edge, 0, side).wait_send()
+
+            @pl.when(tile > 0)
+            def _():
+                col_copy(e, edge, 1, side - 1).wait_send()
+
+            @pl.when(tile < last_tile)
+            def _():
+                col_copy(e, edge, 2, side + 1).wait_send()
+
+    def chunk_of(k):
+        return jnp.where(k % 2 == 0, k // 2, CHUNKS - 1 - k // 2)
+
+    def keep(e, y, x0, value):
+        windows[e % 2][y + REACH, pl.ds(EDGE + x0, X), :] = value.astype(jnp.float32)
+        if linked:
+            out_rows[e, y, pl.ds(x0, X), :] = value
+
+    def stage(e, body):
+        def chunk(k, carry):
+            c = chunk_of(k)
+            x0 = pl.multiple_of(c * X, 16)
+            take_halo(e, k)
+            convolve(windows[e % 2], bands, hidden, x0)
+
+            def row(y, inner):
+                body(y, x0, hidden[y])
+                return inner
+
+            lax.fori_loop(0, ROWS, row, 0)
+            if e < 3:
+                send_chunk(e + 1, k, c)
+            return carry
+
+        lax.fori_loop(0, CHUNKS, chunk, 0)
+        sent(e)
+
+    def first(k, carry):
+        c = chunk_of(k)
+        x0 = pl.multiple_of(c * X, 16)
+
+        def row(y, inner):
+            keep(0, y, x0, state_ref[y, pl.ds(x0, X), :])
+            return inner
+
+        lax.fori_loop(0, ROWS, row, 0)
+        send_chunk(0, k, c)
+        return carry
+
+    lax.fori_loop(0, CHUNKS, first, 0)
+
+    def mask_of(y, x0):
+        return mask_ref[y, pl.ds(x0, X), :].astype(jnp.float32)
+
+    def own(e, y, x0):
+        return windows[e % 2][y + REACH, pl.ds(EDGE + x0, X), :]
+
+    spread_taps(bands, taps_ref, 0, False)
+
+    def forward_0(y, x0, hid):
+        unit, rstd = normalized(hid)
+        normed = (unit * gain_ref[0:1, :]).astype(jnp.bfloat16)
+        value, slope = gelu_pair(dot32(normed, expand_ref[0]))
+        update = dot32(value.astype(jnp.bfloat16), project_ref[0])
+        unit_0[y, pl.ds(x0, X), :] = unit
+        rstd_0[y, pl.ds(x0, X), :] = jnp.broadcast_to(rstd, (X, CELL))
+        slope_0[y, pl.ds(x0, X), :] = slope
+        keep(1, y, x0, (own(0, y, x0) + mask_of(y, x0) * update).astype(jnp.bfloat16))
+
+    stage(0, forward_0)
+    spread_taps(bands, taps_ref, 1, False)
+
+    def forward_1(y, x0, hid):
+        unit, rstd = normalized(hid)
+        gain = gain_ref[1:2, :]
+        normed = (unit * gain).astype(jnp.bfloat16)
+        value, slope = gelu_pair(dot32(normed, expand_ref[1]))
+        update = dot32(value.astype(jnp.bfloat16), project_ref[1])
+        mask = mask_of(y, x0)
+        next_ref[y, pl.ds(x0, X), :] = (own(1, y, x0) + mask * update).astype(jnp.bfloat16)
+        masked = (mask * cot_ref[y, pl.ds(x0, X), :].astype(jnp.float32)).astype(jnp.bfloat16)
+        keep(
+            2, y, x0, adjoint_cell(masked, slope, unit, rstd, gain, expand_ref[1], project_ref[1])
+        )
+
+    stage(1, forward_1)
+    spread_taps(bands, taps_ref, 1, True)
+
+    def backward_0(y, x0, hid):
+        cot = cot_ref[y, pl.ds(x0, X), :].astype(jnp.float32) + hid
+        grad_ref[y, pl.ds(x0, X), :] = cot
+        masked = (mask_of(y, x0) * cot).astype(jnp.bfloat16)
+        keep(
+            3,
+            y,
+            x0,
+            adjoint_cell(
+                masked,
+                slope_0[y, pl.ds(x0, X), :],
+                unit_0[y, pl.ds(x0, X), :],
+                rstd_0[y, pl.ds(x0, X), :],
+                gain_ref[0:1, :],
+                expand_ref[0],
+                project_ref[0],
+            ),
+        )
+
+    stage(2, backward_0)
+    spread_taps(bands, taps_ref, 0, True)
+
+    def last(y, x0, hid):
+        grad_ref[y, pl.ds(x0, X), :] = grad_ref[y, pl.ds(x0, X), :] + hid
+
+    stage(3, last)
+
+
+def ocean(state, mask, cotangent, taps, gain, expand, project, linked=True):
+    vmem = pl.BlockSpec(memory_space=pltpu.VMEM)
+    whole = (ROWS, CHUNKS * X, CELL)
+    f32, bf16 = (jnp.float32, jnp.bfloat16)
+    return pl.pallas_call(
+        functools.partial(ocean_kernel, linked),
+        out_shape=(jax.ShapeDtypeStruct(whole, bf16), jax.ShapeDtypeStruct(whole, f32)),
+        in_specs=[vmem] * 7,
+        out_specs=(vmem, vmem),
+        scratch_shapes=[
+            pltpu.VMEM((ROWS + 2 * REACH, WIDE, CELL), f32),
+            pltpu.VMEM((ROWS + 2 * REACH, WIDE, CELL), f32),
+            pltpu.VMEM((TAPS, 8 * CELL, 2 * CELL), bf16),
+            pltpu.VMEM((ROWS, X, CELL), f32),
+            pltpu.VMEM(whole, f32),
+            pltpu.VMEM(whole, f32),
+            pltpu.VMEM((ROWS, CHUNKS * X, 4 * CELL), f32),
+            pltpu.VMEM((4, ROWS, CHUNKS * X, CELL), bf16),
+            pltpu.VMEM((4, 2, REACH, CHUNKS * X, CELL), bf16),
+            pltpu.VMEM((4, 2, ROWS + 2 * REACH, EDGE, CELL), f32),
+            pltpu.SemaphoreType.DMA((2, 4, 2, CHUNKS)),
+            pltpu.SemaphoreType.DMA((2, 4, 2, 3)),
+        ],
+        compiler_params=pltpu.CompilerParams(
+            collective_id=6 if linked else None, has_side_effects=linked, vmem_limit_bytes=67000000
+        ),
+        name="ocean",
+    )(state, mask, cotangent, taps, gain, expand, project)
+
+
 def slot_weights(bands_row, blocks, group):
     slot = bands_row[:, None] - (2 * group - 2)
     onehot = (slot == jnp.arange(SLOTS, dtype=jnp.int32)[None, :]).astype(jnp.float32)
@@ -169,19 +592,6 @@
 
 def padded_lanes(values):
     return jnp.pad(values, [(0, 0)] * (values.ndim - 1) + [(0, LANES - values.shape[-1])])
-
-
-def with_halo(x, sides, width, wrap):
-    for axis, dim in sides:
-        size, length = (lax.axis_size(axis), x.shape[dim])
-        up = [(i, (i + 1) % size) for i in range(size if wrap else size - 1)]
-        down = [(j, i) for i, j in up]
-        last = lax.slice_in_dim(x, length - width, length, axis=dim)
-        first = lax.slice_in_dim(x, 0, width, axis=dim)
-        before = lax.ppermute(last, axis, up)
-        after = lax.ppermute(first, axis, down)
-        x = jnp.concatenate([before, x, after], axis=dim)
-    return x
 
 
 def wave_table(lon_count, mode_count):
@@ -194,52 +604,6 @@
         jnp.float32(2.0 / lon_count)
     )
     return scaled.reshape(lon_count, 2 * mode_count).astype(jnp.bfloat16)
-
-
-def depthwise(window, kernel):
-    radius = kernel.shape[0] // 2
-    height = window.shape[0] - 2 * radius
-    extent = window.shape[1] - 2 * radius
-    wide = window.astype(jnp.float32)
-    weights = kernel.astype(jnp.float32)
-    total = jnp.zeros((height, extent, window.shape[2]), jnp.float32)
-    for shift_row in range(kernel.shape[0]):
-        for shift_col in range(kernel.shape[1]):
-            total = (
-                total
-                + wide[shift_row : shift_row + height, shift_col : shift_col + extent]
-                * weights[shift_row, shift_col]
-            )
-    return total
-
-
-def cell_forward(hidden, gain, expand, project):
-    center = hidden - jnp.mean(hidden, axis=-1, keepdims=True)
-    inverse_std = lax.rsqrt(jnp.mean(center * center, axis=-1, keepdims=True) + 1e-06)
-    normed = (center * inverse_std * gain).astype(jnp.bfloat16)
-    before = jnp.dot(normed, expand, preferred_element_type=jnp.float32)
-    active = jax.nn.gelu(before).astype(jnp.bfloat16)
-    return jnp.dot(active, project, preferred_element_type=jnp.float32)
-
-
-def cell_backward(hidden, gain, expand, project, mask_value, cotangent):
-    center = hidden - jnp.mean(hidden, axis=-1, keepdims=True)
-    inverse_std = lax.rsqrt(jnp.mean(center * center, axis=-1, keepdims=True) + 1e-06)
-    unit = center * inverse_std
-    normed = (unit * gain).astype(jnp.bfloat16)
-    before = jnp.dot(normed, expand, preferred_element_type=jnp.float32)
-    masked = (mask_value[:, :, None] * cotangent).astype(jnp.bfloat16)
-    active_adjoint = jnp.dot(masked, project.T, preferred_element_type=jnp.float32)
-    _, gelu_back = jax.vjp(jax.nn.gelu, before)
-    before_adjoint = gelu_back(active_adjoint)[0].astype(jnp.bfloat16)
-    normed_adjoint = jnp.dot(before_adjoint, expand.T, preferred_element_type=jnp.float32)
-    scaled = normed_adjoint * gain
-    result = inverse_std * (
-        scaled
-        - jnp.mean(scaled, axis=-1, keepdims=True)
-        - unit * jnp.mean(scaled * unit, axis=-1, keepdims=True)
-    )
-    return result.astype(jnp.bfloat16)
 
 
 def mix_complex(coefficient, mix_real, mix_imag):
@@ -286,11 +650,6 @@
         "mla,lmrc->amrc", forward, coefficient_adjoint, preferred_element_type=jnp.float32
     ).astype(jnp.bfloat16)
     return spectrum_adjoint.reshape(lat_count, columns, channels)
-
-
-def rims(values, width):
-    with_rows = with_halo(values, ((TILE, 0),), width, False)
-    return with_halo(with_rows, (("sec", 1),), width, True)
 
 
 def per_device(
@@ -321,8 +680,6 @@
     offset = lax.axis_index("sec") * half
     ratio = ocean_lon // half
     flux_count = flux_read.shape[1]
-    radius = conv_kernel.shape[1] // 2
-    layer_count = conv_kernel.shape[0]
     highest = lax.Precision.HIGHEST
     mask_value = land_mask.astype(jnp.float32)
     group = lax.axis_index("tile")
@@ -369,31 +726,16 @@
     state = (ocean_state.astype(jnp.float32) + mask_value[:, :, None] * forcing).astype(
         jnp.bfloat16
     )
-    windows = []
-    for layer in range(layer_count):
-        window = rims(state, radius)
-        windows.append(window)
-        update = cell_forward(
-            depthwise(window, conv_kernel[layer]),
-            norm_gain[layer],
-            expand_weight[layer],
-            project_weight[layer],
-        )
-        state = (state.astype(jnp.float32) + mask_value[:, :, None] * update).astype(jnp.bfloat16)
-    cotangent = ocean_cotangent.astype(jnp.float32)
-    for layer in range(layer_count - 1, -1, -1):
-        hidden = depthwise(windows[layer], conv_kernel[layer])
-        hidden_adjoint = cell_backward(
-            hidden,
-            norm_gain[layer],
-            expand_weight[layer],
-            project_weight[layer],
-            mask_value,
-            cotangent,
-        )
-        cotangent = cotangent + depthwise(
-            rims(hidden_adjoint, radius), conv_kernel[layer, ::-1, ::-1]
-        )
+    layer_count = conv_kernel.shape[0]
+    state, cotangent = ocean(
+        state,
+        jnp.broadcast_to(mask_value[:, :, None], state.shape).astype(jnp.bfloat16),
+        ocean_cotangent,
+        conv_kernel.reshape(layer_count, TAPS * TAPS, CELL).astype(jnp.float32),
+        norm_gain,
+        expand_weight,
+        project_weight,
+    )
     forcing_adjoint = (
         (mask_value[:, :, None] * cotangent)
         .reshape(ocean_rows, half, ratio, ocean_channels)

time: 478 us -> 284 us (0.59); the launches traced: 469 us -> 283 us
  other arithmetic: 216 us -> 17.8 us
  Pallas kernels: 103 us -> 225 us
  matrix products: 74.1 us -> 24 us
  starting transfers between devices: 30.1 us -> 0 us
  local copies, waits for them, and re-layouts: 34.8 us -> 15.2 us
  waiting for transfers between devices: 7.83 us -> 0 us
    pallas_call x0 -> x1, Pallas kernels: none -> 139 us  [ocean(): pl.pallas_call(functools.partial(ocean_kernel, linked), out_shape=(jax.Sh...]
    add x1 -> x0, other arithmetic: 60.9 us -> none  [per_device(): cotangent + depthwise(rims(hidden_adjoint, radius), conv_kernel[layer, ::...]
    mul x1, other arithmetic: 60.7 us -> 2.76 us  [per_device(): mask_value[:, :, None] * cotangent]
    dot_general x6 -> x0, matrix products: 48.5 us -> none  [the longest x2 28.6 us: cell_backward(): jnp.dot(before_adjoint, expand.T, preferred_element_type=jnp.float32)]
    reduce_sum x4 -> x0, other arithmetic: 45.1 us -> none  [the longest x2 41.5 us: cell_forward(): center = hidden - jnp.mean(hidden, axis=-1, keepdims=True)]
    ppermute x16 -> x0, starting transfers between devices: 30.1 us -> none  [the longest x8 15.6 us: with_halo(): after = lax.ppermute(first, axis, down)]
    convert_element_type x10 -> x2, other arithmetic: 30.2 us -> 0.03 us  [the longest x1 0.02 us: per_device(): conv_kernel.reshape(layer_count, TAPS * TAPS, CELL).astype(jnp.float32)]
    pallas_call x2, Pallas kernels: 39.6 us -> 26.6 us  [regrid(): pl.pallas_call(regrid_kernel, out_shape=(jax.ShapeDtypeStruct((SLOTS, r,...]
  transfers between devices with their start and end apart: 16 -> 0, of which waited for: 7 -> 0; matrix products, arithmetic and copies ran while one was open for 11% -> 0% of each run, Pallas kernels for 14% -> 0%
where the time goes in v2:
time: 284 us; the launch traced here: 283 us
  Pallas kernels  225 us (79%)
  matrix products  24 us (8%)
  other arithmetic  17.8 us (6%)
  local copies, waits for them, and re-layouts  15.2 us (5%)
    pallas_call x1, Pallas kernels, ocean(): pl.pallas_call(functools.partial(ocean_kernel, linked), out_shape=(jax.Sh...  139 us
    pallas_call x4, Pallas kernels, all_to_all(): pl.pallas_call(all_to_all_kernel, out_shape=jax.ShapeDtypeStruct(blocks.s...  59.7 us
    pallas_call x2, Pallas kernels, regrid(): pl.pallas_call(regrid_kernel, out_shape=(jax.ShapeDtypeStruct((SLOTS, r,...  26.6 us

profile of v2, /device:TPU:1, one launch (start us, length us, event | category | flops | bytes accessed | tf_op | source)
XLA Modules:
  0.0 283.2 jit_solution(13333782091660245506)
XLA Ops:
  4.8 2.0 fusion.87
  8.9 15.4 %regrid_0.1 = (f32[8,8,256]{2,1,0:T(8,128)}, f32[2,1,256]{2,1,0:T(1,128)}) custom-call(f32[2,8,256]{2,1,0:T(8,128)} %pad.16.rows_ref, f32[8,1,256]{2,1,0:T(1,128)} %broadcast_in_dim.6.parts_ref), custom_call_target="tpu_custom_call" | custom-call | tf_op jit(solution)/shard_map/regrid_0/pallas_call | solution.py:148
  27.5 15.2 %exchange_1.1 = bf16[128,2,384]{2,1,0:T(2,128)(2,1)} custom-call(bf16[128,2,384]{2,1,0:T(2,128)(2,1)} %reshape.334.x_ref), custom_call_target="tpu_custom_call" | custom-call | tf_op jit(solution)/shard_map/exchange_1/pallas_call | solution.py:57
  46.1 14.7 %exchange_2.1 = bf16[128,2,384]{2,1,0:T(2,128)(2,1)} custom-call(bf16[128,2,384]{2,1,0:T(2,128)(2,1)} %bitcast.161), custom_call_target="tpu_custom_call" | custom-call | tf_op jit(solution)/shard_map/exchange_2/pallas_call | solution.py:57
  60.8 2.2 add_convert_fusion.1
  64.7 1.9 add_convert_fusion.state_ref
  66.6 1.8 mul.232.mask_ref
  69.0 138.8 %ocean.1 = (bf16[8,720,128]{2,1,0:T(8,128)(2,1)}, f32[8,720,128]{2,1,0:T(8,128)}) custom-call(bf16[8,720,128]{2,1,0:T(8,128)(2,1)} %add_convert_fusion.state_ref, bf16[8,720,128]{2,1,0:T(8,128)(2,1)} %mul.232.mask_ref, bf16[8,720,128]{2,1,0:T(8,128)(2,1)} %cot_ref.1, f32[2,49,128]{2,1,0:T(8,128)} %copy.98.taps_ref, f32[2,128]{1,0:T(2,128)} %gain_ref.1, ...), custom_call_target="tpu_custom_call" | custom-call | tf_op jit(solution)/shard_map/ocean/pallas_call | solution.py:561
  207.8 1.8 fusion.4
  210.4 14.9 %exchange_3.1 = bf16[128,2,384]{2,1,0:T(2,128)(2,1)} custom-call(bf16[128,2,384]{2,1,0:T(2,128)(2,1)} %reshape.342.x_ref), custom_call_target="tpu_custom_call" | custom-call | tf_op jit(solution)/shard_map/exchange_3/pallas_call | solution.py:57
  226.8 1.4 fusion.9
  228.1 1.2 fusion.30
  229.4 1.2 fusion.10
  231.7 14.8 %exchange_4.1 = bf16[128,2,384]{2,1,0:T(2,128)(2,1)} custom-call(bf16[128,2,384]{2,1,0:T(2,128)(2,1)} %bitcast.162), custom_call_target="tpu_custom_call" | custom-call | tf_op jit(solution)/shard_map/exchange_4/pallas_call | solution.py:57
  246.5 1.4 fusion
  248.8 1.8 fusion.98
  251.2 2.8 broadcast_multiply_fusion
  254.0 4.5 %reduce_sum.39 = f32[8,180,128]{2,1,0:T(8,128)} reduce(f32[8,180,4,128]{3,2,1,0:T(4,128)} %bitcast.158, f32[]{:T(128)} %constant.15.clone.1), dimensions={2}, to_apply=%region_3.4 | reduce | flops 552960 | bytes 3686404 | tf_op jit(solution)/shard_map/reduce_sum | solution.py:742
  258.4 1.8 convolution_bitcast_fusion.2
  261.1 11.2 %regrid_5.1 = (f32[8,1,256]{2,1,0:T(1,128)}, f32[2,8,256]{2,1,0:T(8,128)}) custom-call(f32[2,1,256]{2,1,0:T(1,128)} %pad.18.rows_ref, f32[8,8,256]{2,1,0:T(8,128)} %pad.19.parts_ref), custom_call_target="tpu_custom_call" | custom-call | tf_op jit(solution)/shard_map/regrid_5/pallas_call | solution.py:148
  272.3 2.0 fusion.75
  274.2 1.9 reshape.348
  276.2 1.9 add.72
  280.1 2.1 multiply_add_fusion
  (94 shorter events, 23.5 us)
Async XLA Ops:
  0.6 44.3 %copy-start = (bf16[1,128,128]{2,1,0:T(8,128)(2,1)S(1)}, bf16[1,128,128]{2,1,0:T(8,128)(2,1)}, u32[]{:S(2)}) copy-start(bf16[1,128,128]{2,1,0:T(8,128)(2,1)} %param.30) | copy-start | bytes 98308
  0.6 25.7 %copy-start.19 = (f32[384]{0:T(512)S(1)}, f32[384]{0:T(512)}, u32[]{:S(2)}) copy-start(f32[384]{0:T(512)} %param.26) | copy-start | bytes 4612
  0.7 25.7 %copy-start.7 = (bf16[1,360,384]{2,1,0:T(8,128)(2,1)S(1)}, bf16[1,360,384]{2,1,0:T(8,128)(2,1)}, u32[]{:S(2)}) copy-start(bf16[1,360,384]{2,1,0:T(8,128)(2,1)} %param.19) | copy-start | bytes 829444
  2.6 40.1 %copy-start.11 = (bf16[1,128,128]{2,1,0:T(8,128)(2,1)S(1)}, bf16[1,128,128]{2,1,0:T(8,128)(2,1)}, u32[]{:S(2)}) copy-start(bf16[1,128,128]{2,1,0:T(8,128)(2,1)} %param.29) | copy-start | bytes 98308
  4.8 39.1 %copy-start.2 = (bf16[2,384,384]{2,1,0:T(8,128)(2,1)S(1)}, bf16[2,384,384]{2,1,0:T(8,128)(2,1)}, u32[]{:S(2)}) copy-start(bf16[2,384,384]{2,1,0:T(8,128)(2,1)} %param.31) | copy-start | bytes 1769476
  25.9 34.9 %copy-start.5 = (bf16[360,128,2]{1,0,2:T(8,128)(2,1)}, bf16[360,128,2]{1,0,2:T(8,128)(2,1)S(1)}, u32[]{:S(2)}) copy-start(bf16[360,128,2]{1,0,2:T(8,128)(2,1)S(1)} %fusion.23) | copy-start | bytes 552964
  26.3 36.8 %copy-start.10 = (bf16[360,256]{0,1:T(8,128)(2,1)}, bf16[360,256]{0,1:T(8,128)(2,1)S(1)}, u32[]{:S(2)}) copy-start(bf16[360,256]{0,1:T(8,128)(2,1)S(1)} %convert_element_type.160) | copy-start | bytes 552964
  43.9 19.2 %copy-start.13 = (f32[8,8,256]{2,1,0:T(8,128)S(1)}, f32[8,8,256]{2,1,0:T(8,128)}, u32[]{:S(2)}) copy-start(f32[8,8,256]{2,1,0:T(8,128)} %get-tuple-element.11) | copy-start | bytes 196612
  43.9 19.4 %copy-start.16 = (bf16[8,128]{1,0:T(8,128)(2,1)S(1)}, bf16[8,128]{1,0:T(8,128)(2,1)}, u32[]{:S(2)}) copy-start(bf16[8,128]{1,0:T(8,128)(2,1)} %param.28) | copy-start | bytes 6148
  60.8 3.9 %copy-start.9 = (s32[8,720]{1,0:T(8,128)S(1)}, s32[8,720]{1,0:T(8,128)}, u32[]{:S(2)}) copy-start(s32[8,720]{1,0:T(8,128)} %param.21) | copy-start | bytes 69124
  60.8 3.9 %copy-start.4 = (bf16[8,720,128]{2,1,0:T(8,128)(2,1)S(1)}, bf16[8,720,128]{2,1,0:T(8,128)(2,1)}, u32[]{:S(2)}) copy-start(bf16[8,720,128]{2,1,0:T(8,128)(2,1)} %param.20) | copy-start | bytes 4423684
  64.7 1.9 copy-start.8
  64.7 3.6 %copy-start.14 = (bf16[2,7,7,128]{3,0,2,1:T(2,128)(2,1)S(1)}, bf16[2,7,7,128]{3,0,2,1:T(2,128)(2,1)}, u32[]{:S(2)}) copy-start(bf16[2,7,7,128]{3,0,2,1:T(2,128)(2,1)} %param.32) | copy-start | bytes 75268
  207.8 18.7 %copy-start.3 = (bf16[2,384,384]{2,1,0:T(8,128)(2,1)S(1)}, bf16[2,384,384]{2,1,0:T(8,128)(2,1)}, u32[]{:S(2)}) copy-start(bf16[2,384,384]{2,1,0:T(8,128)(2,1)} %param.31) | copy-start | bytes 1769476
  207.8 22.8 %copy-start.12 = (bf16[1,128,128]{2,1,0:T(8,128)(2,1)S(1)}, bf16[1,128,128]{2,1,0:T(8,128)(2,1)}, u32[]{:S(2)}) copy-start(bf16[1,128,128]{2,1,0:T(8,128)(2,1)} %param.29) | copy-start | bytes 98308
  226.5 22.3 %copy-start.20 = (f32[384]{0:T(512)S(1)}, f32[384]{0:T(512)}, u32[]{:S(2)}) copy-start(f32[384]{0:T(512)} %param.26) | copy-start | bytes 4612
  226.8 24.4 %copy-start.1 = (f32[8,720,128]{2,1,0:T(8,128)S(1)}, f32[8,720,128]{2,1,0:T(8,128)}, u32[]{:S(2)}) copy-start(f32[8,720,128]{2,1,0:T(8,128)} %get-tuple-element.13) | copy-start | bytes 8847364
  253.9 4.5 %copy-start.17 = (bf16[8,128]{1,0:T(8,128)(2,1)S(1)}, bf16[8,128]{1,0:T(8,128)(2,1)}, u32[]{:S(2)}) copy-start(bf16[8,128]{1,0:T(8,128)(2,1)} %param.28) | copy-start | bytes 6148
  254.0 18.3 %copy-start.15 = (bf16[384,8]{0,1:T(8,128)(2,1)S(1)}, bf16[384,8]{0,1:T(8,128)(2,1)}, u32[]{:S(2)}) copy-start(bf16[384,8]{0,1:T(8,128)(2,1)} %param.27) | copy-start | bytes 18436
  272.3 6.5 %copy-start.18 = (f32[8,1,256]{2,1,0:T(1,128)S(1)}, f32[8,1,256]{2,1,0:T(1,128)}, u32[]{:S(2)}) copy-start(f32[8,1,256]{2,1,0:T(1,128)} %get-tuple-element.15) | copy-start | bytes 24580
  280.1 2.1 copy-start.6

commit v3 on v2

--- a/solution.py
+++ b/solution.py
@@ -2,6 +2,7 @@
 
 import jax
 import jax.numpy as jnp
+import numpy as np
 from jax import lax
 from jax.experimental import pallas as pl
 from jax.experimental.pallas import tpu as pltpu
@@ -25,48 +26,6 @@
         device_id=device,
         device_id_type=LOGICAL,
     )
-
-
-def all_to_all_kernel(x_ref, o_ref, landed, send_sem, recv_sem):
-    me = lax.axis_index("sec") * GROUPS + lax.axis_index("tile")
-    barrier = pltpu.get_barrier_semaphore()
-
-    def greet(i, carry):
-        pl.semaphore_signal(
-            barrier, inc=1, device_id=(me + i) % DEVICES, device_id_type=LOGICAL
-        )
-        return carry
-
-    lax.fori_loop(1, DEVICES, greet, 0)
-    pl.semaphore_wait(barrier, DEVICES - 1)
-
-    def send(i, carry):
-        peer = (me + i) % DEVICES
-        remote(x_ref.at[peer], landed.at[me], send_sem, recv_sem, peer).start()
-        return carry
-
-    lax.fori_loop(1, DEVICES, send, 0)
-    landed[me] = x_ref[me]
-    every = landed.at[pl.ds(0, DEVICES - 1)]
-    pltpu.make_async_copy(every, every, recv_sem).wait()
-    pltpu.make_async_copy(every, every, send_sem).wait()
-    o_ref[...] = landed[...]
-
-
-def all_to_all(blocks, number):
-    return pl.pallas_call(
-        all_to_all_kernel,
-        out_shape=jax.ShapeDtypeStruct(blocks.shape, blocks.dtype),
-        in_specs=[pl.BlockSpec(memory_space=pltpu.VMEM)],
-        out_specs=pl.BlockSpec(memory_space=pltpu.VMEM),
-        scratch_shapes=[
-            pltpu.VMEM(blocks.shape, blocks.dtype),
-            pltpu.SemaphoreType.DMA,
-            pltpu.SemaphoreType.DMA,
-        ],
-        compiler_params=pltpu.CompilerParams(collective_id=number, has_side_effects=True),
-        name=f"exchange_{number}",
-    )(blocks)
 
 
 def regrid_kernel(
@@ -171,6 +130,7 @@
 CELL = 128
 TAPS = 7
 REACH = 3
+ALON = 360
 
 
 def spread_taps(bands, taps_ref, layer, flipped):
@@ -254,8 +214,18 @@
     gain_ref,
     expand_ref,
     project_ref,
+    atmosphere_ref,
+    atmosphere_cot_ref,
+    spectrum_ref,
+    wave_ref,
+    wave_t_ref,
+    forward_ref,
+    inverse_ref,
+    mix_ref,
     next_ref,
     grad_ref,
+    atmosphere_next_ref,
+    input_adj_ref,
     win_a,
     win_b,
     bands,
@@ -268,6 +238,9 @@
     in_cols,
     row_sems,
     col_sems,
+    leaving,
+    landed,
+    swap_sems,
 ):
     sec = lax.axis_index("sec") if linked else 0
     tile = lax.axis_index("tile") if linked else 0
@@ -278,17 +251,14 @@
 
     if linked:
         barrier = pltpu.get_barrier_semaphore()
-        pl.semaphore_signal(barrier, inc=1, device_id=side, device_id_type=LOGICAL)
-
-        @pl.when(tile > 0)
-        def _():
-            for peer in (me - 1, side - 1):
-                pl.semaphore_signal(barrier, inc=1, device_id=peer, device_id_type=LOGICAL)
-
-        @pl.when(tile < last_tile)
-        def _():
-            for peer in (me + 1, side + 1):
-                pl.semaphore_signal(barrier, inc=1, device_id=peer, device_id_type=LOGICAL)
+
+        def greet(i, carry):
+            pl.semaphore_signal(
+                barrier, inc=1, device_id=(me + i) % DEVICES, device_id_type=LOGICAL
+            )
+            return carry
+
+        lax.fori_loop(1, DEVICES, greet, 0)
 
     zero_rows = jnp.zeros((REACH, WIDE, CELL), jnp.float32)
 
@@ -311,8 +281,105 @@
         bands[v, 7 * CELL :, :CELL] = jnp.zeros((CELL, CELL), jnp.bfloat16)
 
     if linked:
-        count = 1 + jnp.where(tile > 0, 2, 0) + jnp.where(tile < last_tile, 2, 0)
-        pl.semaphore_wait(barrier, count)
+        pl.semaphore_wait(barrier, DEVICES - 1)
+
+    def put_blocks(x, values):
+        for j in range(6):
+            leaving[x, pl.ds(j, DEVICES, stride=8), :] = values[:, j * CELL : (j + 1) * CELL]
+        if not linked:
+            return
+
+        def send(i, carry):
+            peer = (me + i) % DEVICES
+            remote(
+                leaving.at[x, pl.ds(pl.multiple_of(peer * 8, 8), 8)],
+                landed.at[x, pl.ds(pl.multiple_of(me * 8, 8), 8)],
+                swap_sems.at[0, x],
+                swap_sems.at[1, x],
+                peer,
+            ).start()
+            return carry
+
+        lax.fori_loop(1, DEVICES, send, 0)
+        mine = pl.ds(pl.multiple_of(me * 8, 8), 8)
+        landed[x, mine, :] = leaving[x, mine, :]
+
+    def take_blocks(x):
+        source = landed
+        if linked:
+            every = landed.at[x, pl.ds(0, (DEVICES - 1) * 8)]
+            pltpu.make_async_copy(every, every, swap_sems.at[1, x]).wait()
+            pltpu.make_async_copy(every, every, swap_sems.at[0, x]).wait()
+        else:
+            source = leaving
+        return jnp.concatenate(
+            [source[x, pl.ds(j, DEVICES, stride=8), :] for j in range(6)], axis=1
+        ).astype(jnp.bfloat16)
+
+    def rounded(values):
+        return values.astype(jnp.bfloat16).astype(jnp.float32)
+
+    half_c = 3 * CELL
+
+    def spectral():
+        coefficient = dot32(forward_ref[...], take_blocks(0)).astype(jnp.bfloat16)
+        real, imag = (coefficient[:, :half_c], coefficient[:, half_c:])
+        mixed = jnp.concatenate(
+            [
+                dot32(real, mix_ref[0]) - dot32(imag, mix_ref[1]),
+                dot32(imag, mix_ref[0]) + dot32(real, mix_ref[1]),
+            ],
+            axis=1,
+        ).astype(jnp.bfloat16)
+        put_blocks(1, rounded(dot32(inverse_ref[...], mixed)))
+
+    def respond():
+        returned = take_blocks(1)
+        returned = jnp.concatenate([returned[:, :half_c], returned[:, half_c:]], axis=0)
+        parts = []
+        for j in range(3):
+            cols = pl.ds(j * CELL, CELL)
+            response = dot32(wave_ref[...], returned[:, j * CELL : (j + 1) * CELL])
+            value, slope = gelu_pair(response)
+            atmosphere_next_ref[:, cols] = (
+                atmosphere_ref[:, cols].astype(jnp.float32) + value
+            ).astype(jnp.bfloat16)
+            response_adj = (slope * atmosphere_cot_ref[:, cols].astype(jnp.float32)).astype(
+                jnp.bfloat16
+            )
+            parts.append(dot32(wave_t_ref[...], response_adj))
+        put_blocks(
+            2,
+            rounded(
+                jnp.concatenate([p[:DEVICES] for p in parts] + [p[DEVICES:] for p in parts], axis=1)
+            ),
+        )
+
+    def dot_first(a, b):
+        return lax.dot_general(
+            a, b, (((0,), (0,)), ((), ())), preferred_element_type=jnp.float32
+        )
+
+    def spectral_back():
+        mixed_adj = dot_first(inverse_ref[...], take_blocks(2)).astype(jnp.bfloat16)
+        real, imag = (mixed_adj[:, :half_c], mixed_adj[:, half_c:])
+        coefficient_adj = jnp.concatenate(
+            [
+                dot_t(real, mix_ref[0]) + dot_t(imag, mix_ref[1]),
+                dot_t(imag, mix_ref[0]) - dot_t(real, mix_ref[1]),
+            ],
+            axis=1,
+        ).astype(jnp.bfloat16)
+        put_blocks(3, rounded(dot_first(forward_ref[...], coefficient_adj)))
+
+    def absorb():
+        spectrum_adj = take_blocks(3)
+        spectrum_adj = jnp.concatenate([spectrum_adj[:, :half_c], spectrum_adj[:, half_c:]], axis=0)
+        for j in range(3):
+            cols = pl.ds(j * CELL, CELL)
+            input_adj_ref[:, cols] = atmosphere_cot_ref[:, cols].astype(jnp.float32) + dot32(
+                wave_ref[...], spectrum_adj[:, j * CELL : (j + 1) * CELL]
+            )
 
     def row_copy(e, way, c, peer):
         x0 = pl.multiple_of(c * X, 16)
@@ -488,6 +555,7 @@
         return carry
 
     lax.fori_loop(0, CHUNKS, first, 0)
+    put_blocks(0, spectrum_ref[...])
 
     def mask_of(y, x0):
         return mask_ref[y, pl.ds(x0, X), :].astype(jnp.float32)
@@ -508,6 +576,7 @@
         keep(1, y, x0, (own(0, y, x0) + mask_of(y, x0) * update).astype(jnp.bfloat16))
 
     stage(0, forward_0)
+    spectral()
     spread_taps(bands, taps_ref, 1, False)
 
     def forward_1(y, x0, hid):
@@ -524,6 +593,7 @@
         )
 
     stage(1, forward_1)
+    respond()
     spread_taps(bands, taps_ref, 1, True)
 
     def backward_0(y, x0, hid):
@@ -546,23 +616,30 @@
         )
 
     stage(2, backward_0)
+    spectral_back()
     spread_taps(bands, taps_ref, 0, True)
 
     def last(y, x0, hid):
         grad_ref[y, pl.ds(x0, X), :] = grad_ref[y, pl.ds(x0, X), :] + hid
 
     stage(3, last)
-
-
-def ocean(state, mask, cotangent, taps, gain, expand, project, linked=True):
+    absorb()
+
+
+def ocean(*operands, linked=True):
     vmem = pl.BlockSpec(memory_space=pltpu.VMEM)
     whole = (ROWS, CHUNKS * X, CELL)
     f32, bf16 = (jnp.float32, jnp.bfloat16)
     return pl.pallas_call(
         functools.partial(ocean_kernel, linked),
-        out_shape=(jax.ShapeDtypeStruct(whole, bf16), jax.ShapeDtypeStruct(whole, f32)),
-        in_specs=[vmem] * 7,
-        out_specs=(vmem, vmem),
+        out_shape=(
+            jax.ShapeDtypeStruct(whole, bf16),
+            jax.ShapeDtypeStruct(whole, f32),
+            jax.ShapeDtypeStruct((ALON, 3 * CELL), bf16),
+            jax.ShapeDtypeStruct((ALON, 3 * CELL), f32),
+        ),
+        in_specs=[vmem] * 15,
+        out_specs=(vmem,) * 4,
         scratch_shapes=[
             pltpu.VMEM((ROWS + 2 * REACH, WIDE, CELL), f32),
             pltpu.VMEM((ROWS + 2 * REACH, WIDE, CELL), f32),
@@ -576,12 +653,22 @@
             pltpu.VMEM((4, 2, ROWS + 2 * REACH, EDGE, CELL), f32),
             pltpu.SemaphoreType.DMA((2, 4, 2, CHUNKS)),
             pltpu.SemaphoreType.DMA((2, 4, 2, 3)),
+            pltpu.VMEM((4, DEVICES * 8, CELL), f32),
+            pltpu.VMEM((4, DEVICES * 8, CELL), f32),
+            pltpu.SemaphoreType.DMA((2, 4)),
         ],
         compiler_params=pltpu.CompilerParams(
             collective_id=6 if linked else None, has_side_effects=linked, vmem_limit_bytes=67000000
         ),
         name="ocean",
-    )(state, mask, cotangent, taps, gain, expand, project)
+    )(*operands)
+
+
+def wave_table():
+    place = np.arange(ALON, dtype=np.int32)[:, None] * np.arange(DEVICES, dtype=np.int32)[None, :]
+    phase = (place % ALON).astype(np.float32) * np.float32(2.0 * np.pi / ALON)
+    both = np.concatenate([np.cos(phase), -np.sin(phase)], axis=1)
+    return (both * np.sqrt(np.float32(2.0 / ALON))).astype(jnp.bfloat16)
 
 
 def slot_weights(bands_row, blocks, group):
@@ -592,64 +679,6 @@
 
 def padded_lanes(values):
     return jnp.pad(values, [(0, 0)] * (values.ndim - 1) + [(0, LANES - values.shape[-1])])
-
-
-def wave_table(lon_count, mode_count):
-    longitude = jnp.arange(lon_count, dtype=jnp.int32)
-    wavenumber = jnp.arange(mode_count, dtype=jnp.int32)
-    phase = (longitude[:, None] * wavenumber[None, :] % lon_count).astype(jnp.float32) * (
-        2.0 * jnp.pi / lon_count
-    )
-    scaled = jnp.stack([jnp.cos(phase), -jnp.sin(phase)], axis=2) * jnp.sqrt(
-        jnp.float32(2.0 / lon_count)
-    )
-    return scaled.reshape(lon_count, 2 * mode_count).astype(jnp.bfloat16)
-
-
-def mix_complex(coefficient, mix_real, mix_imag):
-    real_part = coefficient[:, :, 0]
-    imag_part = coefficient[:, :, 1]
-    out_real = jnp.einsum(
-        "lmc,cd->lmd", real_part, mix_real, preferred_element_type=jnp.float32
-    ) - jnp.einsum("lmc,cd->lmd", imag_part, mix_imag, preferred_element_type=jnp.float32)
-    out_imag = jnp.einsum(
-        "lmc,cd->lmd", imag_part, mix_real, preferred_element_type=jnp.float32
-    ) + jnp.einsum("lmc,cd->lmd", real_part, mix_imag, preferred_element_type=jnp.float32)
-    return jnp.stack([out_real, out_imag], axis=2).astype(jnp.bfloat16)
-
-
-def spectral_block(spectrum, forward, inverse, mixing):
-    lat_count, columns, channels = spectrum.shape
-    split = spectrum.reshape(lat_count, columns // 2, 2, channels)
-    coefficient = jnp.einsum(
-        "mla,amrc->lmrc", forward, split, preferred_element_type=jnp.float32
-    ).astype(jnp.bfloat16)
-    mixed = mix_complex(coefficient, mixing[0], mixing[1])
-    returned = jnp.einsum(
-        "mal,lmrc->amrc", inverse, mixed, preferred_element_type=jnp.float32
-    ).astype(jnp.bfloat16)
-    return returned.reshape(lat_count, columns, channels)
-
-
-def spectral_adjoint(returned_adjoint, forward, inverse, mixing):
-    lat_count, columns, channels = returned_adjoint.shape
-    split = returned_adjoint.reshape(lat_count, columns // 2, 2, channels)
-    mixed_adjoint = jnp.einsum(
-        "mal,amrc->lmrc", inverse, split, preferred_element_type=jnp.float32
-    ).astype(jnp.bfloat16)
-    real_part = mixed_adjoint[:, :, 0]
-    imag_part = mixed_adjoint[:, :, 1]
-    back_real = jnp.einsum(
-        "lmd,cd->lmc", real_part, mixing[0], preferred_element_type=jnp.float32
-    ) + jnp.einsum("lmd,cd->lmc", imag_part, mixing[1], preferred_element_type=jnp.float32)
-    back_imag = jnp.einsum(
-        "lmd,cd->lmc", imag_part, mixing[0], preferred_element_type=jnp.float32
-    ) - jnp.einsum("lmd,cd->lmc", real_part, mixing[1], preferred_element_type=jnp.float32)
-    coefficient_adjoint = jnp.stack([back_real, back_imag], axis=2).astype(jnp.bfloat16)
-    spectrum_adjoint = jnp.einsum(
-        "mla,lmrc->amrc", forward, coefficient_adjoint, preferred_element_type=jnp.float32
-    ).astype(jnp.bfloat16)
-    return spectrum_adjoint.reshape(lat_count, columns, channels)
 
 
 def per_device(
@@ -673,7 +702,6 @@
     atmosphere_cotangent,
     ocean_cotangent,
 ):
-    band_total = lax.axis_size(SEC_TILE)
     lat_rows, lon_count, channels = atmosphere.shape
     ocean_rows, ocean_lon, ocean_channels = ocean_state.shape
     half = lon_count // lax.axis_size("sec")
@@ -704,16 +732,12 @@
         atmosphere.astype(jnp.float32)
         + surface_atmosphere[:, :, None] * surface_embed[None, None, :]
     ).astype(jnp.bfloat16)
-    table = wave_table(lon_count, legendre_forward.shape[0] * band_total)
+    table = wave_table()
     spectrum = jnp.einsum(
-        "gk,agc->akc", table, mixed_input, preferred_element_type=jnp.float32
-    ).astype(jnp.bfloat16)
-    modes = legendre_forward.shape[0] * band_total
-    at_modes = all_to_all(spectrum.reshape(modes, 2, channels), 1)
-    returned = spectral_block(at_modes, legendre_forward, legendre_inverse, spectral_mix)
-    returned = all_to_all(returned, 2).reshape(1, 2 * modes, channels)
-    response = jnp.einsum("gk,akc->agc", table, returned, preferred_element_type=jnp.float32)
-    atmosphere_next = (mixed_input.astype(jnp.float32) + jax.nn.gelu(response)).astype(jnp.bfloat16)
+        "gk,gc->kc", jnp.asarray(table), mixed_input[0], preferred_element_type=jnp.float32
+    )
+    spectrum = spectrum.astype(jnp.bfloat16).astype(jnp.float32)
+    spectrum = jnp.concatenate([spectrum[:DEVICES], spectrum[DEVICES:]], axis=1)
     forcing_coarse = jnp.einsum(
         "ogf,fc->ogc",
         flux_ocean,
@@ -727,7 +751,7 @@
         jnp.bfloat16
     )
     layer_count = conv_kernel.shape[0]
-    state, cotangent = ocean(
+    state, cotangent, atmosphere_next, input_adjoint = ocean(
         state,
         jnp.broadcast_to(mask_value[:, :, None], state.shape).astype(jnp.bfloat16),
         ocean_cotangent,
@@ -735,6 +759,14 @@
         norm_gain,
         expand_weight,
         project_weight,
+        mixed_input[0],
+        atmosphere_cotangent[0],
+        spectrum,
+        jnp.asarray(table),
+        jnp.asarray(np.ascontiguousarray(table.T)),
+        legendre_forward[0],
+        legendre_inverse[0],
+        spectral_mix,
     )
     forcing_adjoint = (
         (mask_value[:, :, None] * cotangent)
@@ -744,21 +776,7 @@
     flux_ocean_adjoint = jnp.einsum(
         "ogc,fc->ofg", forcing_adjoint, flux_embed.astype(jnp.float32), precision=highest
     )
-    atmosphere_adjoint = atmosphere_cotangent.astype(jnp.float32)
-    _, gelu_back = jax.vjp(jax.nn.gelu, response)
-    response_adjoint = gelu_back(atmosphere_adjoint)[0].astype(jnp.bfloat16)
-    returned_adjoint = jnp.einsum(
-        "gk,agc->akc", table, response_adjoint, preferred_element_type=jnp.float32
-    ).astype(jnp.bfloat16)
-    at_modes_adjoint = all_to_all(returned_adjoint.reshape(modes, 2, channels), 3)
-    spectrum_adjoint = spectral_adjoint(
-        at_modes_adjoint, legendre_forward, legendre_inverse, spectral_mix
-    )
-    spectrum_adjoint = all_to_all(spectrum_adjoint, 4).reshape(1, 2 * modes, channels)
-    input_adjoint = atmosphere_adjoint + jnp.einsum(
-        "gk,akc->agc", table, spectrum_adjoint, preferred_element_type=jnp.float32
-    )
-    surface_adjoint = jnp.einsum("agc,c->ag", input_adjoint, surface_embed, precision=highest)
+    surface_adjoint = jnp.einsum("gc,c->g", input_adjoint, surface_embed, precision=highest)
     parts = jnp.einsum("so,ofg->sfg", to_ocean, flux_ocean_adjoint, precision=highest)
     surface_rows_adjoint, flux_adjoint = regrid(
         padded_lanes(surface_adjoint.reshape(2, 1, half)), padded_lanes(parts), 5
@@ -768,7 +786,7 @@
         flux_adjoint[:, :, :half],
         flux_read.astype(jnp.float32),
         precision=highest,
-    ).reshape(1, lon_count, channels)
+    ).reshape(lon_count, channels)
     atmosphere_grad = input_adjoint + from_flux
     coarse_adjoint = jnp.einsum(
         "so,sg->og", to_atmosphere, surface_rows_adjoint[:, 0, :half], precision=highest
@@ -780,7 +798,7 @@
     ocean_grad = (
         cotangent + surface_grad[:, :, None] * surface_read.astype(jnp.float32)[None, None, :]
     )
-    return (atmosphere_next, state, atmosphere_grad, ocean_grad)
+    return (atmosphere_next[None], state, atmosphere_grad[None], ocean_grad)
 
 
 def solution(mesh):

time: 284 us -> 225 us (0.79)
  Pallas kernels: 225 us -> 186 us
  matrix products: 24 us -> 7.91 us
  local copies, waits for them, and re-layouts: 15.2 us -> 12 us
    pallas_call x4 -> x0, Pallas kernels: 59.7 us -> none  [all_to_all(): pl.pallas_call(all_to_all_kernel, out_shape=jax.ShapeDtypeStruct(blocks.s...]
    pallas_call x1, Pallas kernels: 139 us -> 159 us  [ocean(): pl.pallas_call(functools.partial(ocean_kernel, linked), out_shape=(jax.Sh...]
    dot_general x17 -> x2, matrix products: 15.5 us -> 0.97 us  [the longest x1 0.64 us: per_device(): jnp.einsum('gc,c->g', input_adjoint, surface_embed, precision=highest)]
where the time goes in v3:
time: 225 us
  Pallas kernels  186 us (83%)
  other arithmetic  17.7 us (8%)
  local copies, waits for them, and re-layouts  12 us (5%)
  matrix products  7.91 us (4%)
    pallas_call x1, Pallas kernels, ocean(): pl.pallas_call(functools.partial(ocean_kernel, linked), out_shape=(jax.Sh...  159 us
    pallas_call x2, Pallas kernels, regrid(): pl.pallas_call(regrid_kernel, out_shape=(jax.ShapeDtypeStruct((SLOTS, r,...  27.1 us
    reduce_sum x1, other arithmetic, per_device(): forcing_adjoint = (mask_value[:, :, None] * cotangent).reshape(ocean_rows...  4.61 us

profile of v3, /device:TPU:1, one launch (start us, length us, event | category | flops | bytes accessed | tf_op | source)
XLA Modules:
  0.0 224.7 jit_solution(15378373594763582061)
XLA Ops:
  0.7 0.7 subtract_bitcast_fusion
  1.5 0.8 multiply_reduce_fusion
  2.3 2.0 fusion.23
  4.2 0.8 bitcast_multiply_fusion
  6.3 1.0 reshape.128
  8.1 15.5 %regrid_0.1 = (f32[8,8,256]{2,1,0:T(8,128)}, f32[2,1,256]{2,1,0:T(1,128)}) custom-call(f32[2,8,256]{2,1,0:T(8,128)} %pad.16.rows_ref, f32[8,1,256]{2,1,0:T(1,128)} %broadcast_in_dim.10.parts_ref), custom_call_target="tpu_custom_call" | custom-call | tf_op jit(solution)/shard_map/regrid_0/pallas_call | solution.py:107
  23.6 0.7 slice_reduce_fusion
  25.0 0.8 pad_maximum_fusion.spectrum_ref
  26.0 0.8 fusion.7
  27.4 1.9 add_convert_fusion.state_ref
  29.3 1.8 mul.101.mask_ref
  31.7 159.0 %ocean.1 = (bf16[8,720,128]{2,1,0:T(8,128)(2,1)}, f32[8,720,128]{2,1,0:T(8,128)}, bf16[360,384]{1,0:T(8,128)(2,1)}, f32[360,384]{1,0:T(8,128)}) custom-call(bf16[8,720,128]{2,1,0:T(8,128)(2,1)} %add_convert_fusion.state_ref, bf16[8,720,128]{2,1,0:T(8,128)(2,1)} %mul.101.mask_ref, bf16[8,720,128]{2,1,0:T(8,128)(2,1)} %cot_ref.1, ...), custom_call_target="tpu_custom_call" | custom-call | tf_op jit(solution)/shard_map/ocean/pallas_call | solution.py:633
  190.7 3.4 %broadcast_multiply_fusion = f32[8,720,128]{2,1,0:T(8,128)} fusion(f32[8,720,128]{2,1,0:T(8,128)} %get-tuple-element.17, f32[8,720]{1,0:T(8,128)S(1)} %get-tuple-element.25), kind=kLoop, calls=%fused_computation.2 | loop fusion | flops 737280 | bytes 5921280 | tf_op jit(solution)/shard_map/mul | solution.py:772
  194.2 4.6 %reduce_sum.39 = f32[8,180,128]{2,1,0:T(8,128)} reduce(f32[8,180,4,128]{3,2,1,0:T(4,128)} %bitcast.63, f32[]{:T(128)} %constant.7.clone.1), dimensions={2}, to_apply=%region_3.4 | reduce | flops 552960 | bytes 3686404 | tf_op jit(solution)/shard_map/reduce_sum | solution.py:774
  198.8 1.8 convolution_bitcast_fusion
  202.8 11.7 %regrid_5.1 = (f32[8,1,256]{2,1,0:T(1,128)}, f32[2,8,256]{2,1,0:T(8,128)}) custom-call(f32[2,1,256]{2,1,0:T(1,128)} %pad.18.rows_ref, f32[8,8,256]{2,1,0:T(8,128)} %pad.19.parts_ref), custom_call_target="tpu_custom_call" | custom-call | tf_op jit(solution)/shard_map/regrid_5/pallas_call | solution.py:107
  214.5 1.1 fusion.13
  215.6 0.8 broadcast_in_dim.14
  216.4 1.7 copy.69
  218.1 0.7 multiply_multiply_fusion
  219.5 2.0 multiply_add_fusion
  222.1 0.9 add_bitcast_fusion
  222.9 0.7 copy.89
  223.6 1.1 copy.90
  (63 shorter events, 7.6 us)
Async XLA Ops:
  0.6 6.7 %copy-start = (bf16[384,8]{0,1:T(8,128)(2,1)S(1)}, bf16[384,8]{0,1:T(8,128)(2,1)}, u32[]{:S(2)}) copy-start(bf16[384,8]{0,1:T(8,128)(2,1)} %param.29) | copy-start | bytes 18436
  0.6 23.9 %copy-start.7 = (bf16[360,256]{1,0:T(8,128)(2,1)S(1)}, bf16[360,256]{1,0:T(8,128)(2,1)}, u32[]{:S(2)}) copy-start(bf16[360,256]{1,0:T(8,128)(2,1)} %constant.21.clone.wave_ref) | copy-start | bytes 552964
  0.7 23.8 %copy-start.6 = (bf16[1,360,384]{2,1,0:T(8,128)(2,1)S(1)}, bf16[1,360,384]{2,1,0:T(8,128)(2,1)}, u32[]{:S(2)}) copy-start(bf16[1,360,384]{2,1,0:T(8,128)(2,1)} %param.21) | copy-start | bytes 829444
  0.7 23.8 %copy-start.16 = (f32[384]{0:T(512)S(1)}, f32[384]{0:T(512)}, u32[]{:S(2)}) copy-start(f32[384]{0:T(512)} %param.28) | copy-start | bytes 4612
  2.2 23.8 %copy-start.14 = (bf16[8,128]{1,0:T(8,128)(2,1)S(1)}, bf16[8,128]{1,0:T(8,128)(2,1)}, u32[]{:S(2)}) copy-start(bf16[8,128]{1,0:T(8,128)(2,1)} %param.30) | copy-start | bytes 6148
  23.6 2.2 copy-start.11
  24.6 1.4 copy-start.3
  24.9 2.4 %copy-start.9 = (s32[8,720]{1,0:T(8,128)S(1)}, s32[8,720]{1,0:T(8,128)}, u32[]{:S(2)}) copy-start(s32[8,720]{1,0:T(8,128)} %param.23) | copy-start | bytes 69124
  25.0 2.4 %copy-start.2 = (bf16[8,720,128]{2,1,0:T(8,128)(2,1)S(1)}, bf16[8,720,128]{2,1,0:T(8,128)(2,1)}, u32[]{:S(2)}) copy-start(bf16[8,720,128]{2,1,0:T(8,128)(2,1)} %param.22) | copy-start | bytes 4423684
  27.4 3.6 %copy-start.12 = (bf16[2,7,7,128]{3,0,2,1:T(2,128)(2,1)S(1)}, bf16[2,7,7,128]{3,0,2,1:T(2,128)(2,1)}, u32[]{:S(2)}) copy-start(bf16[2,7,7,128]{3,0,2,1:T(2,128)(2,1)} %param.34) | copy-start | bytes 75268
  194.2 4.6 %copy-start.15 = (bf16[8,128]{1,0:T(8,128)(2,1)S(1)}, bf16[8,128]{1,0:T(8,128)(2,1)}, u32[]{:S(2)}) copy-start(bf16[8,128]{1,0:T(8,128)(2,1)} %param.30) | copy-start | bytes 6148
  194.2 7.3 %copy-start.17 = (f32[384]{0:T(512)S(1)}, f32[384]{0:T(512)}, u32[]{:S(2)}) copy-start(f32[384]{0:T(512)} %param.28) | copy-start | bytes 4612
  194.2 7.3 %copy-start.4 = (f32[360,384]{1,0:T(8,128)S(1)}, f32[360,384]{1,0:T(8,128)}, u32[]{:S(2)}) copy-start(f32[360,384]{1,0:T(8,128)} %get-tuple-element.16) | copy-start | bytes 1658884
  194.2 23.9 %copy-start.10 = (s32[8,720]{1,0:T(8,128)S(1)}, s32[8,720]{1,0:T(8,128)}, u32[]{:S(2)}) copy-start(s32[8,720]{1,0:T(8,128)} %param.23) | copy-start | bytes 69124
  194.2 25.3 %copy-start.1 = (f32[8,720,128]{2,1,0:T(8,128)S(1)}, f32[8,720,128]{2,1,0:T(8,128)}, u32[]{:S(2)}) copy-start(f32[8,720,128]{2,1,0:T(8,128)} %get-tuple-element.17) | copy-start | bytes 8847364
  219.5 2.1 copy-start.13
  221.5 1.4 copy-start.8
  221.5 2.1 copy-start.5

commit v4 on v3

--- a/solution.py
+++ b/solution.py
@@ -28,19 +28,68 @@
     )
 
 
+def regrid_peers():
+    sec = lax.axis_index("sec")
+    group = lax.axis_index("tile")
+    me = sec * GROUPS + group
+
+    def group_device(k):
+        return (k % 2) * GROUPS + (me // 2 + 1 - k // 2 + GROUPS) % GROUPS
+
+    def band_device(slot):
+        return (2 * group - 2 + slot + DEVICES) % DEVICES
+
+    return sec, me, group_device, band_device
+
+
+def swap_rows(rows_ref, parts_ref, rows_in, parts_in, sems):
+    sec, me, group_device, band_device = regrid_peers()
+
+    for k in range(SLOTS):
+        target = group_device(k)
+        slot = me % 2 + 2 * (k // 2)
+
+        @pl.when(target != me)
+        def _():
+            remote(
+                rows_ref.at[k % 2], rows_in.at[slot], sems.at[0, k], sems.at[1, slot], target
+            ).start()
+
+        @pl.when(target == me)
+        def _():
+            rows_in[slot] = rows_ref[k % 2]
+
+        band = band_device(k)
+        place = (k // 2) * 2 + sec
+
+        @pl.when(band != me)
+        def _():
+            remote(
+                parts_ref.at[k], parts_in.at[place], sems.at[2, k], sems.at[3, place], band
+            ).start()
+
+        @pl.when(band == me)
+        def _():
+            parts_in[place] = parts_ref[k]
+
+    for k in range(SLOTS):
+
+        @pl.when(band_device(k) != me)
+        def _():
+            remote(rows_ref.at[0], rows_in.at[k], sems.at[0, k], sems.at[1, k], me).wait_recv()
+            remote(parts_ref.at[k], parts_in.at[k], sems.at[2, k], sems.at[3, k], me).wait_send()
+
+        @pl.when(group_device(k) != me)
+        def _():
+            remote(rows_ref.at[0], rows_in.at[k], sems.at[0, k], sems.at[1, k], me).wait_send()
+            remote(parts_ref.at[k], parts_in.at[k], sems.at[2, k], sems.at[3, k], me).wait_recv()
+
+
 def regrid_kernel(
     rows_ref, parts_ref, gathered_ref, summed_ref, rows_in, parts_in, sems
 ):
-    sec = lax.axis_index("sec")
-    group = lax.axis_index("tile")
-    me = sec * GROUPS + group
+    _, me, group_device, band_device = regrid_peers()
     barrier = pltpu.get_barrier_semaphore()
-
-    def group_device(k):
-        return (k % 2) * GROUPS + (me // 2 + 1 - k // 2 + GROUPS) % GROUPS
-
-    def band_device(slot):
-        return (2 * group - 2 + slot + DEVICES) % DEVICES
 
     mine = me * 0
     for k in range(SLOTS):
@@ -53,45 +102,7 @@
 
     pl.semaphore_wait(barrier, 2 * SLOTS - mine)
 
-    for k in range(SLOTS):
-        target = group_device(k)
-        slot = me % 2 + 2 * (k // 2)
-
-        @pl.when(target != me)
-        def _():
-            remote(
-                rows_ref.at[k % 2], rows_in.at[slot], sems.at[0, k], sems.at[1, slot], target
-            ).start()
-
-        @pl.when(target == me)
-        def _():
-            rows_in[slot] = rows_ref[k % 2]
-
-        band = band_device(k)
-        place = (k // 2) * 2 + sec
-
-        @pl.when(band != me)
-        def _():
-            remote(
-                parts_ref.at[k], parts_in.at[place], sems.at[2, k], sems.at[3, place], band
-            ).start()
-
-        @pl.when(band == me)
-        def _():
-            parts_in[place] = parts_ref[k]
-
-    for k in range(SLOTS):
-
-        @pl.when(band_device(k) != me)
-        def _():
-            remote(rows_ref.at[0], rows_in.at[k], sems.at[0, k], sems.at[1, k], me).wait_recv()
-            remote(parts_ref.at[k], parts_in.at[k], sems.at[2, k], sems.at[3, k], me).wait_send()
-
-        @pl.when(group_device(k) != me)
-        def _():
-            remote(rows_ref.at[0], rows_in.at[k], sems.at[0, k], sems.at[1, k], me).wait_send()
-            remote(parts_ref.at[k], parts_in.at[k], sems.at[2, k], sems.at[3, k], me).wait_recv()
-
+    swap_rows(rows_ref, parts_ref, rows_in, parts_in, sems)
     gathered_ref[...] = rows_in[...]
     for half in range(2):
         total = parts_in[half]
@@ -152,7 +163,7 @@
     lax.fori_loop(0, TAPS, one, 0)
 
 
-def convolve(window, bands, hidden, x0):
+def convolve(window, bands, sums, x0):
     total = None
     for v in range(TAPS):
         rows = [
@@ -164,9 +175,7 @@
         )
         part = jnp.dot(left, bands[v], preferred_element_type=jnp.float32)
         total = part if total is None else total + part
-    for p in range(ROWS // 2):
-        for q in range(2):
-            hidden[2 * p + q] = total[p * X : (p + 1) * X, q * CELL : (q + 1) * CELL]
+    sums[...] = total
 
 
 def normalized(hidden):
@@ -181,11 +190,15 @@
 
 def gelu_pair(v):
     square = v * v
-    t = jnp.tanh(v * (GELU_A + GELU_B * square))
-    half = 0.5 * v
-    value = half + half * t
-    slope = (0.5 + 0.5 * t) + (half * (1.0 - t * t)) * (GELU_A + (3.0 * GELU_B) * square)
+    w = 0.5 + 0.5 * jnp.tanh(v * (GELU_A + GELU_B * square))
+    value = v * w
+    slope = w + value * (1.0 - w) * (2.0 * GELU_A + (6.0 * GELU_B) * square)
     return value, slope
+
+
+def split(values):
+    high = values.astype(jnp.bfloat16)
+    return high, (values - high.astype(jnp.float32)).astype(jnp.bfloat16)
 
 
 def dot32(a, b):
@@ -194,15 +207,6 @@
 
 def dot_t(a, b):
     return lax.dot_general(a, b, (((1,), (1,)), ((), ())), preferred_element_type=jnp.float32)
-
-
-def adjoint_cell(masked, slope, unit, rstd, gain, expand, project):
-    before_adj = (slope * dot_t(masked, project)).astype(jnp.bfloat16)
-    scaled = dot_t(before_adj, expand) * gain
-    inner = jnp.mean(scaled * unit, axis=-1, keepdims=True)
-    return (rstd * (scaled - jnp.mean(scaled, axis=-1, keepdims=True) - unit * inner)).astype(
-        jnp.bfloat16
-    )
 
 
 def ocean_kernel(
@@ -222,6 +226,13 @@
     forward_ref,
     inverse_ref,
     mix_ref,
+    embed_rows_ref,
+    group_ref,
+    to_ocean_ref,
+    to_atmosphere_ref,
+    surface_embed_ref,
+    surface_read_ref,
+    flux_read_ref,
     next_ref,
     grad_ref,
     atmosphere_next_ref,
@@ -229,10 +240,14 @@
     win_a,
     win_b,
     bands,
-    hidden,
+    sums,
     unit_0,
     rstd_0,
     slope_0,
+    unit_1,
+    rstd_1,
+    before,
+    active,
     out_rows,
     in_rows,
     in_cols,
@@ -241,6 +256,13 @@
     leaving,
     landed,
     swap_sems,
+    flux_rows,
+    coarse_rows,
+    rows_out,
+    parts_out,
+    rows_in,
+    parts_in,
+    regrid_sems,
 ):
     sec = lax.axis_index("sec") if linked else 0
     tile = lax.axis_index("tile") if linked else 0
@@ -523,20 +545,78 @@
         if linked:
             out_rows[e, y, pl.ds(x0, X), :] = value
 
-    def stage(e, body):
+    half_cells = ROWS // 2 * X
+
+    def origin(k):
+        return pl.multiple_of(chunk_of(k) * X, 16)
+
+    def conv(e, k):
+        convolve(windows[e % 2], bands, sums, origin(k))
+
+    def halves(one):
+        def half(q, inner):
+            one(q, pl.ds(pl.multiple_of(q * half_cells, 16), half_cells))
+            return inner
+
+        lax.fori_loop(0, 2, half, 0)
+
+    def half_of(q):
+        return sums[:, pl.ds(pl.multiple_of(q * CELL, CELL), CELL)]
+
+    def row_part(values, p):
+        return values[p * X : (p + 1) * X]
+
+    def stacked(read):
+        return jnp.concatenate([read(p) for p in range(ROWS // 2)], axis=0)
+
+    def forward_stage(e, layer, keep_norm, keep_slope, finish):
+        def normalize(k):
+            def one(q, at):
+                unit, rstd = normalized(half_of(q))
+                keep_norm(k, at, unit, rstd)
+                dense = (unit * gain_ref[layer : layer + 1, :]).astype(jnp.bfloat16)
+                before[at, :] = dot32(dense, expand_ref[layer])
+
+            halves(one)
+
+        def activate(k, y):
+            at = pl.ds(pl.multiple_of(y * X, 16), X)
+            value, slope = gelu_pair(before[at, :])
+            active[at, :] = value.astype(jnp.bfloat16)
+            keep_slope(k, at, slope)
+
+        def close(k):
+            def one(q, at):
+                finish(k, q, at, dot32(active[at, :], project_ref[layer]))
+
+            halves(one)
+            send_chunk(e + 1, k, chunk_of(k))
+
         def chunk(k, carry):
-            c = chunk_of(k)
-            x0 = pl.multiple_of(c * X, 16)
             take_halo(e, k)
-            convolve(windows[e % 2], bands, hidden, x0)
-
-            def row(y, inner):
-                body(y, x0, hidden[y])
+            conv(e, k)
+            normalize(k)
+
+            def piece(y, inner):
+                activate(k, y)
                 return inner
 
-            lax.fori_loop(0, ROWS, row, 0)
+            lax.fori_loop(0, ROWS, piece, 0)
+            close(k)
+            return carry
+
+        lax.fori_loop(0, CHUNKS, chunk, 0)
+        sent(e)
+
+    def backward_stage(e, one, after=None):
+        def chunk(k, carry):
+            take_halo(e, k)
+            conv(e, k)
+            halves(lambda q, at: one(k, q, at))
+            if after is not None:
+                after(k)
             if e < 3:
-                send_chunk(e + 1, k, c)
+                send_chunk(e + 1, k, chunk_of(k))
             return carry
 
         lax.fori_loop(0, CHUNKS, chunk, 0)
@@ -565,69 +645,147 @@
 
     spread_taps(bands, taps_ref, 0, False)
 
-    def forward_0(y, x0, hid):
-        unit, rstd = normalized(hid)
-        normed = (unit * gain_ref[0:1, :]).astype(jnp.bfloat16)
-        value, slope = gelu_pair(dot32(normed, expand_ref[0]))
-        update = dot32(value.astype(jnp.bfloat16), project_ref[0])
-        unit_0[y, pl.ds(x0, X), :] = unit
-        rstd_0[y, pl.ds(x0, X), :] = jnp.broadcast_to(rstd, (X, CELL))
-        slope_0[y, pl.ds(x0, X), :] = slope
-        keep(1, y, x0, (own(0, y, x0) + mask_of(y, x0) * update).astype(jnp.bfloat16))
-
-    stage(0, forward_0)
+    def keep_norm_0(k, at, unit, rstd):
+        c = chunk_of(k)
+        unit_0[c, at, :] = unit
+        rstd_0[c, at, :] = jnp.broadcast_to(rstd, unit.shape)
+
+    def keep_slope_0(k, at, slope):
+        slope_0[chunk_of(k), at, :] = slope.astype(jnp.bfloat16)
+
+    def finish_0(k, q, at, update):
+        x0 = origin(k)
+        for p in range(ROWS // 2):
+            y = 2 * p + q
+            new = own(0, y, x0) + mask_of(y, x0) * row_part(update, p)
+            keep(1, y, x0, new.astype(jnp.bfloat16))
+
+    forward_stage(0, 0, keep_norm_0, keep_slope_0, finish_0)
     spectral()
     spread_taps(bands, taps_ref, 1, False)
 
-    def forward_1(y, x0, hid):
-        unit, rstd = normalized(hid)
-        gain = gain_ref[1:2, :]
-        normed = (unit * gain).astype(jnp.bfloat16)
-        value, slope = gelu_pair(dot32(normed, expand_ref[1]))
-        update = dot32(value.astype(jnp.bfloat16), project_ref[1])
-        mask = mask_of(y, x0)
-        next_ref[y, pl.ds(x0, X), :] = (own(1, y, x0) + mask * update).astype(jnp.bfloat16)
-        masked = (mask * cot_ref[y, pl.ds(x0, X), :].astype(jnp.float32)).astype(jnp.bfloat16)
-        keep(
-            2, y, x0, adjoint_cell(masked, slope, unit, rstd, gain, expand_ref[1], project_ref[1])
+    def adjoint(e, k, q, at, masked, slope, unit, rstd, layer):
+        x0 = origin(k)
+        active[at, :] = (slope * dot_t(masked, project_ref[layer])).astype(jnp.bfloat16)
+        scaled = dot_t(active[at, :], expand_ref[layer]) * gain_ref[layer : layer + 1, :]
+        inner = jnp.mean(scaled * unit, axis=-1, keepdims=True)
+        result = rstd * (scaled - jnp.mean(scaled, axis=-1, keepdims=True) - unit * inner)
+        for p in range(ROWS // 2):
+            keep(e, 2 * p + q, x0, row_part(result, p).astype(jnp.bfloat16))
+
+    def cot_of(y, x0):
+        return cot_ref[y, pl.ds(x0, X), :].astype(jnp.float32)
+
+    def keep_norm_1(k, at, unit, rstd):
+        unit_1[at, :] = unit
+        rstd_1[at, :] = jnp.broadcast_to(rstd, unit.shape)
+
+    def keep_slope_1(k, at, slope):
+        before[at, :] = slope
+
+    def finish_1(k, q, at, update):
+        x0 = origin(k)
+        for p in range(ROWS // 2):
+            y = 2 * p + q
+            new = own(1, y, x0) + mask_of(y, x0) * row_part(update, p)
+            next_ref[y, pl.ds(x0, X), :] = new.astype(jnp.bfloat16)
+        masked = stacked(lambda p: mask_of(2 * p + q, x0) * cot_of(2 * p + q, x0))
+        adjoint(
+            2, k, q, at, masked.astype(jnp.bfloat16), before[at, :], unit_1[at, :], rstd_1[at, :], 1
         )
 
-    stage(1, forward_1)
+    forward_stage(1, 1, keep_norm_1, keep_slope_1, finish_1)
     respond()
     spread_taps(bands, taps_ref, 1, True)
 
-    def backward_0(y, x0, hid):
-        cot = cot_ref[y, pl.ds(x0, X), :].astype(jnp.float32) + hid
-        grad_ref[y, pl.ds(x0, X), :] = cot
-        masked = (mask_of(y, x0) * cot).astype(jnp.bfloat16)
-        keep(
-            3,
-            y,
-            x0,
-            adjoint_cell(
-                masked,
-                slope_0[y, pl.ds(x0, X), :],
-                unit_0[y, pl.ds(x0, X), :],
-                rstd_0[y, pl.ds(x0, X), :],
-                gain_ref[0:1, :],
-                expand_ref[0],
-                project_ref[0],
-            ),
-        )
-
-    stage(2, backward_0)
+    def backward_0(k, q, at):
+        c, x0 = (chunk_of(k), origin(k))
+        hid = half_of(q)
+        parts = []
+        for p in range(ROWS // 2):
+            y = 2 * p + q
+            cot = cot_of(y, x0) + row_part(hid, p)
+            grad_ref[y, pl.ds(x0, X), :] = cot
+            parts.append(mask_of(y, x0) * cot)
+        masked = jnp.concatenate(parts, axis=0).astype(jnp.bfloat16)
+        slope = slope_0[c, at, :].astype(jnp.float32)
+        adjoint(3, k, q, at, masked, slope, unit_0[c, at, :], rstd_0[c, at, :], 0)
+
+    backward_stage(2, backward_0)
     spectral_back()
     spread_taps(bands, taps_ref, 0, True)
 
-    def last(y, x0, hid):
-        grad_ref[y, pl.ds(x0, X), :] = grad_ref[y, pl.ds(x0, X), :] + hid
-
-    stage(3, last)
+    def last(k, q, at):
+        x0 = origin(k)
+        hid = half_of(q)
+        for p in range(ROWS // 2):
+            y = 2 * p + q
+            grad_ref[y, pl.ds(x0, X), :] = grad_ref[y, pl.ds(x0, X), :] + row_part(hid, p)
+
+    def gather_flux(k):
+        x0 = origin(k)
+        lanes = jnp.concatenate(
+            [mask_of(y, x0) * grad_ref[y, pl.ds(x0, X), :] for y in range(ROWS)], axis=1
+        )
+        high, rest = split(lanes)
+        flux_rows[pl.ds(x0, X), :] = dot32(high, embed_rows_ref[...]) + dot32(
+            rest, embed_rows_ref[...]
+        )
+
+    backward_stage(3, last, gather_flux)
     absorb()
+    half = ALON // 2
+    high, rest = split(flux_rows[...])
+    flux_by_row = dot_first(high, group_ref[...]) + dot_first(rest, group_ref[...])
+    for slot in range(SLOTS):
+        total = to_ocean_ref[slot, 0] * flux_by_row[0:8]
+        for o in range(1, ROWS):
+            total = total + to_ocean_ref[slot, o] * flux_by_row[8 * o : 8 * o + 8]
+        parts_out[slot] = total
+    embed_high, embed_rest = split(jnp.broadcast_to(surface_embed_ref[...], (8, half_c)))
+    rows_out[...] = jnp.zeros((2, 1, LANES), jnp.float32)
+    for h in range(2):
+        high, rest = split(input_adj_ref[pl.ds(h * half, half), :])
+        row = dot_t(embed_high, high) + dot_t(embed_rest, high) + dot_t(embed_high, rest)
+        rows_out[h, :, 0:half] = row[0:1]
+    swap_rows(rows_out, parts_out, rows_in, parts_in, regrid_sems)
+    for o in range(ROWS):
+        total = to_atmosphere_ref[0, o] * rows_in[0]
+        for slot in range(1, SLOTS):
+            total = total + to_atmosphere_ref[slot, o] * rows_in[slot]
+        coarse_rows[o : o + 1, :] = total
+    coarse_high, coarse_rest = split(coarse_rows[...])
+    read = surface_read_ref[...] * 0.25
+    row_number = lax.broadcasted_iota(jnp.int32, (ROWS, CELL), 0)
+
+    def widen(o, carry):
+        pick = jnp.where(row_number == o, 1.0, 0.0).astype(jnp.bfloat16)
+        spread = dot32(group_ref[...], dot_first(coarse_high, pick).astype(jnp.bfloat16)) + dot32(
+            group_ref[...], dot_first(coarse_rest, pick).astype(jnp.bfloat16)
+        )
+        grad_ref[o] = grad_ref[o] + mask_ref[o].astype(jnp.float32) * spread * read
+        return carry
+
+    lax.fori_loop(0, ROWS, widen, 0)
+    flux_read_twice = jnp.concatenate([flux_read_ref[...], flux_read_ref[...]], axis=0)
+    for h in range(2):
+        total = parts_in[h]
+        for k in range(1, 4):
+            total = total + parts_in[2 * k + h]
+        high, rest = split(total)
+        from_flux = dot_first(
+            jnp.concatenate([high.astype(jnp.float32), rest.astype(jnp.float32)], axis=0).astype(
+                jnp.bfloat16
+            ),
+            flux_read_twice,
+        )
+        at = pl.ds(h * half, half)
+        input_adj_ref[at, :] = input_adj_ref[at, :] + from_flux[:half]
 
 
 def ocean(*operands, linked=True):
     vmem = pl.BlockSpec(memory_space=pltpu.VMEM)
+    smem = pl.BlockSpec(memory_space=pltpu.SMEM)
     whole = (ROWS, CHUNKS * X, CELL)
     f32, bf16 = (jnp.float32, jnp.bfloat16)
     return pl.pallas_call(
@@ -638,16 +796,20 @@
             jax.ShapeDtypeStruct((ALON, 3 * CELL), bf16),
             jax.ShapeDtypeStruct((ALON, 3 * CELL), f32),
         ),
-        in_specs=[vmem] * 15,
+        in_specs=[vmem] * 17 + [smem] * 2 + [vmem] * 3,
         out_specs=(vmem,) * 4,
         scratch_shapes=[
             pltpu.VMEM((ROWS + 2 * REACH, WIDE, CELL), f32),
             pltpu.VMEM((ROWS + 2 * REACH, WIDE, CELL), f32),
             pltpu.VMEM((TAPS, 8 * CELL, 2 * CELL), bf16),
-            pltpu.VMEM((ROWS, X, CELL), f32),
-            pltpu.VMEM(whole, f32),
-            pltpu.VMEM(whole, f32),
-            pltpu.VMEM((ROWS, CHUNKS * X, 4 * CELL), f32),
+            pltpu.VMEM((ROWS // 2 * X, 2 * CELL), f32),
+            pltpu.VMEM((CHUNKS, ROWS * X, CELL), f32),
+            pltpu.VMEM((CHUNKS, ROWS * X, CELL), f32),
+            pltpu.VMEM((CHUNKS, ROWS * X, 4 * CELL), bf16),
+            pltpu.VMEM((ROWS * X, CELL), f32),
+            pltpu.VMEM((ROWS * X, CELL), f32),
+            pltpu.VMEM((ROWS * X, 4 * CELL), f32),
+            pltpu.VMEM((ROWS * X, 4 * CELL), bf16),
             pltpu.VMEM((4, ROWS, CHUNKS * X, CELL), bf16),
             pltpu.VMEM((4, 2, REACH, CHUNKS * X, CELL), bf16),
             pltpu.VMEM((4, 2, ROWS + 2 * REACH, EDGE, CELL), f32),
@@ -656,6 +818,13 @@
             pltpu.VMEM((4, DEVICES * 8, CELL), f32),
             pltpu.VMEM((4, DEVICES * 8, CELL), f32),
             pltpu.SemaphoreType.DMA((2, 4)),
+            pltpu.VMEM((CHUNKS * X, ROWS * SLOTS), f32),
+            pltpu.VMEM((ROWS, LANES), f32),
+            pltpu.VMEM((2, 1, LANES), f32),
+            pltpu.VMEM((SLOTS, 8, LANES), f32),
+            pltpu.VMEM((SLOTS, 1, LANES), f32),
+            pltpu.VMEM((SLOTS, 8, LANES), f32),
+            pltpu.SemaphoreType.DMA((4, SLOTS)),
         ],
         compiler_params=pltpu.CompilerParams(
             collective_id=6 if linked else None, has_side_effects=linked, vmem_limit_bytes=67000000
@@ -751,7 +920,13 @@
         jnp.bfloat16
     )
     layer_count = conv_kernel.shape[0]
-    state, cotangent, atmosphere_next, input_adjoint = ocean(
+    embed_rows = (
+        jnp.eye(ocean_rows, dtype=flux_embed.dtype)[:, None, :, None]
+        * flux_embed.T[None, :, None, :]
+    ).reshape(ocean_rows * ocean_channels, ocean_rows * flux_count)
+    grouping = np.arange(ocean_lon)[:, None] // ratio == np.arange(LANES)[None, :]
+    grouping = grouping.astype(jnp.bfloat16)
+    state, ocean_grad, atmosphere_next, atmosphere_grad = ocean(
         state,
         jnp.broadcast_to(mask_value[:, :, None], state.shape).astype(jnp.bfloat16),
         ocean_cotangent,
@@ -767,36 +942,13 @@
         legendre_forward[0],
         legendre_inverse[0],
         spectral_mix,
-    )
-    forcing_adjoint = (
-        (mask_value[:, :, None] * cotangent)
-        .reshape(ocean_rows, half, ratio, ocean_channels)
-        .sum(axis=2)
-    )
-    flux_ocean_adjoint = jnp.einsum(
-        "ogc,fc->ofg", forcing_adjoint, flux_embed.astype(jnp.float32), precision=highest
-    )
-    surface_adjoint = jnp.einsum("gc,c->g", input_adjoint, surface_embed, precision=highest)
-    parts = jnp.einsum("so,ofg->sfg", to_ocean, flux_ocean_adjoint, precision=highest)
-    surface_rows_adjoint, flux_adjoint = regrid(
-        padded_lanes(surface_adjoint.reshape(2, 1, half)), padded_lanes(parts), 5
-    )
-    from_flux = jnp.einsum(
-        "hfg,cf->hgc",
-        flux_adjoint[:, :, :half],
-        flux_read.astype(jnp.float32),
-        precision=highest,
-    ).reshape(lon_count, channels)
-    atmosphere_grad = input_adjoint + from_flux
-    coarse_adjoint = jnp.einsum(
-        "so,sg->og", to_atmosphere, surface_rows_adjoint[:, 0, :half], precision=highest
-    )
-    widened_adjoint = jnp.broadcast_to(
-        coarse_adjoint[:, :, None], (ocean_rows, half, ratio)
-    ).reshape(ocean_rows, ocean_lon)
-    surface_grad = mask_value * widened_adjoint / ratio
-    ocean_grad = (
-        cotangent + surface_grad[:, :, None] * surface_read.astype(jnp.float32)[None, None, :]
+        embed_rows,
+        jnp.asarray(grouping),
+        to_ocean,
+        to_atmosphere,
+        surface_embed[None, :],
+        surface_read.astype(jnp.float32)[None, :],
+        flux_read.T,
     )
     return (atmosphere_next[None], state, atmosphere_grad[None], ocean_grad)
 

time: 225 us -> 184 us (0.82)
  Pallas kernels: 186 us -> 157 us
  other arithmetic: 17.7 us -> 5.85 us
  local copies, waits for them, and re-layouts: 12 us -> 15.5 us
  matrix products: 7.91 us -> 4.59 us
    pallas_call x1, Pallas kernels: 159 us -> 142 us  [ocean(): pl.pallas_call(functools.partial(ocean_kernel, linked), out_shape=(jax.Sh...]
    pallas_call x2 -> x1, Pallas kernels: 27.1 us -> 15.5 us  [regrid(): pl.pallas_call(regrid_kernel, out_shape=(jax.ShapeDtypeStruct((SLOTS, r,...]
    unnamed x39 -> x31, local copies, waits for them, and re-layouts: 1.91 us -> 8.15 us
    reduce_sum x1 -> x0, other arithmetic: 4.61 us -> none  [per_device(): forcing_adjoint = (mask_value[:, :, None] * cotangent).reshape(ocean_rows...]
    dot_general x5 -> x0, matrix products: 4.15 us -> none  [the longest x1 1.81 us: per_device(): jnp.einsum('ogc,fc->ofg', forcing_adjoint, flux_embed.astype(jnp.float32)...]
    mul x1 -> x0, other arithmetic: 3.43 us -> none  [per_device(): mask_value[:, :, None] * cotangent]
where the time goes in v4:
time: 184 us
  Pallas kernels  157 us (85%)
  local copies, waits for them, and re-layouts  15.5 us (8%)
  other arithmetic  5.85 us (3%)
  matrix products  4.59 us (2%)
    pallas_call x1, Pallas kernels, ocean(): pl.pallas_call(functools.partial(ocean_kernel, linked), out_shape=(jax.Sh...  142 us
    pallas_call x1, Pallas kernels, regrid(): pl.pallas_call(regrid_kernel, out_shape=(jax.ShapeDtypeStruct((SLOTS, r,...  15.5 us
    unnamed x31, local copies, waits for them, and re-layouts  8.15 us

profile of v4, /device:TPU:1, one launch (start us, length us, event | category | flops | bytes accessed | tf_op | source)
XLA Modules:
  0.0 183.9 jit_solution(904023895973181684)
XLA Ops:
  0.7 0.7 subtract_bitcast_fusion
  1.4 1.2 bitcast_convert_fusion.1.surface_read_ref
  2.6 1.3 broadcast_in_dim.16.surface_embed_ref
  3.9 0.8 multiply_reduce_fusion
  4.7 2.0 %fusion.14 = f32[1,8,720]{2,0,1:T(1,128)S(1)} fusion(bf16[8,720,128]{2,1,0:T(8,128)(2,1)} %param.23, bf16[128]{0:T(256)(128)(2,1)} %param.28), kind=kOutput, calls=%fused_computation.30 | convolution fusion | flops 1474560 | bytes 1497856 | tf_op jit(solution)/shard_map/dot_general | solution.py:885
  6.8 0.6 copy.43.taps_ref
  7.5 0.8 copy.44.embed_rows_ref
  8.6 0.6 pad.8.rows_ref
  10.0 0.6 broadcast_in_dim.14.parts_ref
  10.6 15.5 %regrid_0.1 = (f32[8,8,256]{2,1,0:T(8,128)}, f32[2,1,256]{2,1,0:T(1,128)}) custom-call(f32[2,8,256]{2,1,0:T(8,128)} %pad.8.rows_ref, f32[8,1,256]{2,1,0:T(1,128)} %broadcast_in_dim.14.parts_ref), custom_call_target="tpu_custom_call" | custom-call | tf_op jit(solution)/shard_map/regrid_0/pallas_call | solution.py:118
  26.0 1.1 convolution_bitcast_fusion
  27.1 0.7 slice_reduce_fusion
  28.5 0.3 copy-done.2
  28.8 0.8 pad_maximum_fusion.spectrum_ref
  29.6 0.8 fusion.5
  30.4 1.8 mul.96.mask_ref
  32.2 0.5 broadcast_in_dim.15
  32.7 0.9 copy-done
  33.5 1.8 add_convert_fusion.state_ref
  35.4 141.6 %ocean.1 = (bf16[8,720,128]{2,1,0:T(8,128)(2,1)}, f32[8,720,128]{2,1,0:T(8,128)}, bf16[360,384]{1,0:T(8,128)(2,1)}, f32[360,384]{1,0:T(8,128)}) custom-call(bf16[8,720,128]{2,1,0:T(8,128)(2,1)} %add_convert_fusion.state_ref, bf16[8,720,128]{2,1,0:T(8,128)(2,1)} %mul.96.mask_ref, bf16[8,720,128]{2,1,0:T(8,128)(2,1)} %cot_ref.1, f32[2,49,128]{2,1,0:T(8,128)} %copy.43.taps_ref, ...), custom_call_target="tpu_custom_call" | custom-call | tf_op jit(solution)/shard_map/ocean/pallas_call | solution.py:791
  177.0 1.7 copy.59
  178.7 2.7 %copy.60 = bf16[8,720,128]{2,1,0:T(8,128)(2,1)} copy(bf16[8,720,128]{2,1,0:T(8,128)(2,1)} %get-tuple-element.27) | data formatting | bytes 2949120
  181.4 0.8 copy.61
  182.3 1.6 copy.62
  (41 shorter events, 1.8 us)
Async XLA Ops:
  0.6 6.8 %copy-start.11 = (bf16[8,128]{1,0:T(8,128)(2,1)S(1)}, bf16[8,128]{1,0:T(8,128)(2,1)}, u32[]{:S(2)}) copy-start(bf16[8,128]{1,0:T(8,128)(2,1)} %param.31) | copy-start | bytes 6148
  0.6 6.0 %copy-start.6 = (s32[8,720]{1,0:T(8,128)S(1)}, s32[8,720]{1,0:T(8,128)}, u32[]{:S(2)}) copy-start(s32[8,720]{1,0:T(8,128)} %param.24) | copy-start | bytes 69124
  0.7 7.7 %copy-start.3 = (bf16[1,360,384]{2,1,0:T(8,128)(2,1)S(1)}, bf16[1,360,384]{2,1,0:T(8,128)(2,1)}, u32[]{:S(2)}) copy-start(bf16[1,360,384]{2,1,0:T(8,128)(2,1)} %param.22) | copy-start | bytes 829444
  0.7 6.1 %copy-start.9 = (bf16[2,7,7,128]{3,0,2,1:T(2,128)(2,1)S(1)}, bf16[2,7,7,128]{3,0,2,1:T(2,128)(2,1)}, u32[]{:S(2)}) copy-start(bf16[2,7,7,128]{3,0,2,1:T(2,128)(2,1)} %param.35) | copy-start | bytes 75268
  4.7 5.0 %copy-start.8 = (f32[8,8]{1,0:T(8,128)}, f32[8,8]{1,0:T(8,128)S(1)}, u32[]{:S(2)}) copy-start(f32[8,8]{1,0:T(8,128)S(1)} %get-tuple-element.17.to_atmosphere_ref) | copy-start | bytes 772
  4.7 21.4 %copy-start.7 = (f32[8,8]{1,0:T(8,128)}, f32[8,8]{1,0:T(8,128)S(1)}, u32[]{:S(2)}) copy-start(f32[8,8]{1,0:T(8,128)S(1)} %get-tuple-element.16.to_ocean_ref) | copy-start | bytes 772
  4.7 3.7 %copy-start.10 = (bf16[384,8]{0,1:T(8,128)(2,1)S(1)}, bf16[384,8]{0,1:T(8,128)(2,1)}, u32[]{:S(2)}) copy-start(bf16[384,8]{0,1:T(8,128)(2,1)} %param.30) | copy-start | bytes 18436
  6.8 21.1 %copy-start.12 = (f32[384]{0:T(512)S(1)}, f32[384]{0:T(512)}, u32[]{:S(2)}) copy-start(f32[384]{0:T(512)} %param.29) | copy-start | bytes 4612
  7.5 20.5 %copy-start.4 = (bf16[360,256]{1,0:T(8,128)(2,1)S(1)}, bf16[360,256]{1,0:T(8,128)(2,1)}, u32[]{:S(2)}) copy-start(bf16[360,256]{1,0:T(8,128)(2,1)} %constant.21.clone.wave_ref) | copy-start | bytes 552964
  28.1 0.7 copy-start.2
  32.2 1.4 copy-start
  177.0 4.5 %copy-start.5 = (f32[360,384]{1,0:T(8,128)S(1)}, f32[360,384]{1,0:T(8,128)}, u32[]{:S(2)}) copy-start(f32[360,384]{1,0:T(8,128)} %get-tuple-element.14) | copy-start | bytes 1658884
  178.7 3.5 %copy-start.1 = (f32[8,720,128]{2,1,0:T(8,128)S(1)}, f32[8,720,128]{2,1,0:T(8,128)}, u32[]{:S(2)}) copy-start(f32[8,720,128]{2,1,0:T(8,128)} %get-tuple-element.29) | copy-start | bytes 8847364

commit v5 on v4

--- a/solution.py
+++ b/solution.py
@@ -15,6 +15,15 @@
 GROUPS = 64
 SLOTS = 8
 LANES = 256
+X = 144
+CHUNKS = 5
+ROWS = 8
+WIDE = 736
+EDGE = 8
+CELL = 128
+TAPS = 7
+REACH = 3
+ALON = 360
 
 
 def remote(src, dst, send_sem, recv_sem, device):
@@ -42,7 +51,7 @@
     return sec, me, group_device, band_device
 
 
-def swap_rows(rows_ref, parts_ref, rows_in, parts_in, sems):
+def send_rows(rows_ref, parts_ref, rows_in, parts_in, sems):
     sec, me, group_device, band_device = regrid_peers()
 
     for k in range(SLOTS):
@@ -72,6 +81,10 @@
         def _():
             parts_in[place] = parts_ref[k]
 
+
+def wait_rows(rows_ref, parts_ref, rows_in, parts_in, sems):
+    _, me, group_device, band_device = regrid_peers()
+
     for k in range(SLOTS):
 
         @pl.when(band_device(k) != me)
@@ -83,65 +96,6 @@
         def _():
             remote(rows_ref.at[0], rows_in.at[k], sems.at[0, k], sems.at[1, k], me).wait_send()
             remote(parts_ref.at[k], parts_in.at[k], sems.at[2, k], sems.at[3, k], me).wait_recv()
-
-
-def regrid_kernel(
-    rows_ref, parts_ref, gathered_ref, summed_ref, rows_in, parts_in, sems
-):
-    _, me, group_device, band_device = regrid_peers()
-    barrier = pltpu.get_barrier_semaphore()
-
-    mine = me * 0
-    for k in range(SLOTS):
-        for peer in (group_device(k), band_device(k)):
-            mine = mine + jnp.where(peer == me, 1, 0)
-
-            @pl.when(peer != me)
-            def _():
-                pl.semaphore_signal(barrier, inc=1, device_id=peer, device_id_type=LOGICAL)
-
-    pl.semaphore_wait(barrier, 2 * SLOTS - mine)
-
-    swap_rows(rows_ref, parts_ref, rows_in, parts_in, sems)
-    gathered_ref[...] = rows_in[...]
-    for half in range(2):
-        total = parts_in[half]
-        for k in range(1, 4):
-            total = total + parts_in[2 * k + half]
-        summed_ref[half] = total
-
-
-def regrid(rows, parts, number):
-    _, r, lanes = rows.shape
-    _, q, _ = parts.shape
-    vmem = pl.BlockSpec(memory_space=pltpu.VMEM)
-    return pl.pallas_call(
-        regrid_kernel,
-        out_shape=(
-            jax.ShapeDtypeStruct((SLOTS, r, lanes), jnp.float32),
-            jax.ShapeDtypeStruct((2, q, lanes), jnp.float32),
-        ),
-        in_specs=[vmem, vmem],
-        out_specs=(vmem, vmem),
-        scratch_shapes=[
-            pltpu.VMEM((SLOTS, r, lanes), jnp.float32),
-            pltpu.VMEM((SLOTS, q, lanes), jnp.float32),
-            pltpu.SemaphoreType.DMA((4, SLOTS)),
-        ],
-        compiler_params=pltpu.CompilerParams(collective_id=number, has_side_effects=True),
-        name=f"regrid_{number}",
-    )(rows, parts)
-
-
-X = 144
-CHUNKS = 5
-ROWS = 8
-WIDE = 736
-EDGE = 8
-CELL = 128
-TAPS = 7
-REACH = 3
-ALON = 360
 
 
 def spread_taps(bands, taps_ref, layer, flipped):
@@ -163,9 +117,21 @@
     lax.fori_loop(0, TAPS, one, 0)
 
 
-def convolve(window, bands, sums, x0):
+VECTOR_TAPS = 2
+STRIP = 16
+
+
+def tap_row(taps_ref, layer, flipped, u, v):
+    at = (TAPS - 1 - u) * TAPS + TAPS - 1 - v if flipped else u * TAPS + v
+    return taps_ref[layer, at : at + 1, :]
+
+
+def convolve(window, bands, sums, x0, taps_ref, layer, flipped):
+    count = TAPS - VECTOR_TAPS
+    strips = X // STRIP
     total = None
-    for v in range(TAPS):
+    done = 0
+    for v in range(count):
         rows = [
             window[r, pl.ds(x0 + EDGE - REACH + v, X), :].astype(jnp.bfloat16)
             for r in range(ROWS + 2 * REACH)
@@ -175,7 +141,21 @@
         )
         part = jnp.dot(left, bands[v], preferred_element_type=jnp.float32)
         total = part if total is None else total + part
-    sums[...] = total
+        upto = strips * (v + 1) // count
+        for strip in range(done, upto):
+            parts = [None] * ROWS
+            for w in range(count, TAPS):
+                for r in range(ROWS + 2 * REACH):
+                    cells = window[r, pl.ds(x0 + EDGE - REACH + w + strip * STRIP, STRIP), :]
+                    for y in range(max(0, r - TAPS + 1), min(ROWS, r + 1)):
+                        term = cells * tap_row(taps_ref, layer, flipped, r - y, w)
+                        parts[y] = term if parts[y] is None else parts[y] + term
+            for y in range(ROWS):
+                sums[
+                    pl.ds(y // 2 * X + strip * STRIP, STRIP), y % 2 * CELL : (y % 2 + 1) * CELL
+                ] = parts[y]
+        done = upto
+    sums[...] = sums[...] + total
 
 
 def normalized(hidden):
@@ -212,21 +192,22 @@
 def ocean_kernel(
     linked,
     state_ref,
-    mask_ref,
+    land_ref,
     cot_ref,
     taps_ref,
     gain_ref,
     expand_ref,
     project_ref,
-    atmosphere_ref,
+    raw_ref,
     atmosphere_cot_ref,
-    spectrum_ref,
     wave_ref,
     wave_t_ref,
     forward_ref,
     inverse_ref,
     mix_ref,
     embed_rows_ref,
+    read_rows_ref,
+    flux_embed_ref,
     group_ref,
     to_ocean_ref,
     to_atmosphere_ref,
@@ -263,6 +244,14 @@
     rows_in,
     parts_in,
     regrid_sems,
+    mask_ref,
+    atmosphere_ref,
+    first_rows_out,
+    first_parts_out,
+    first_rows_in,
+    first_parts_in,
+    first_sems,
+    flux_cells,
 ):
     sec = lax.axis_index("sec") if linked else 0
     tile = lax.axis_index("tile") if linked else 0
@@ -302,8 +291,6 @@
         bands[v, 0:CELL, CELL:] = jnp.zeros((CELL, CELL), jnp.bfloat16)
         bands[v, 7 * CELL :, :CELL] = jnp.zeros((CELL, CELL), jnp.bfloat16)
 
-    if linked:
-        pl.semaphore_wait(barrier, DEVICES - 1)
 
     def put_blocks(x, values):
         for j in range(6):
@@ -551,7 +538,8 @@
         return pl.multiple_of(chunk_of(k) * X, 16)
 
     def conv(e, k):
-        convolve(windows[e % 2], bands, sums, origin(k))
+        layer, flipped = ((0, False), (1, False), (1, True), (0, True))[e]
+        convolve(windows[e % 2], bands, sums, origin(k), taps_ref, layer, flipped)
 
     def halves(one):
         def half(q, inner):
@@ -622,28 +610,100 @@
         lax.fori_loop(0, CHUNKS, chunk, 0)
         sent(e)
 
+    half = ALON // 2
+    row_number = lax.broadcasted_iota(jnp.int32, (ROWS, CELL), 0)
+    land = land_ref[...].astype(jnp.float32).astype(jnp.bfloat16)
+
+    def picked(o):
+        return jnp.where(row_number == o, 1.0, 0.0).astype(jnp.bfloat16)
+
+    def spread_mask(o, carry):
+        mask_ref[o] = dot_first(land, picked(o)).astype(jnp.bfloat16)
+        return carry
+
+    lax.fori_loop(0, ROWS, spread_mask, 0)
+
+    lanes = jnp.concatenate([mask_ref[y] * state_ref[y] for y in range(ROWS)], axis=1)
+    high, rest = split(dot32(lanes, read_rows_ref[...]))
+    coarse = 0.25 * (dot_first(high, group_ref[...]) + dot_first(rest, group_ref[...]))
+    for slot in range(SLOTS):
+        total = to_atmosphere_ref[slot, 0] * coarse[0:1]
+        for o in range(1, ROWS):
+            total = total + to_atmosphere_ref[slot, o] * coarse[o : o + 1]
+        first_parts_out[slot] = total
+    flux = dot_t(flux_read_ref[...], raw_ref[...])
+    first_rows_out[...] = jnp.zeros((2, 8, LANES), jnp.float32)
+    first_rows_out[0, :, 0:half] = flux[:, 0:half]
+    first_rows_out[1, :, 0:half] = flux[:, half:]
+    pl.semaphore_wait(pltpu.get_barrier_semaphore(), DEVICES - 1)
+    send_rows(first_rows_out, first_parts_out, first_rows_in, first_parts_in, first_sems)
+    spread_taps(bands, taps_ref, 0, False)
+    wait_rows(first_rows_out, first_parts_out, first_rows_in, first_parts_in, first_sems)
+
+    for o in range(ROWS):
+        total = to_ocean_ref[0, o] * first_rows_in[0]
+        for slot in range(1, SLOTS):
+            total = total + to_ocean_ref[slot, o] * first_rows_in[slot]
+        parts_out[o] = total
+    high, rest = split(jnp.concatenate([parts_out[o] for o in range(ROWS)], axis=0))
+    flux_cells[0 : ROWS * 8, :] = dot_t(high, group_ref[...])
+    flux_cells[ROWS * 8 :, :] = dot_t(rest, group_ref[...])
+    flux_embed_twice = jnp.concatenate([flux_embed_ref[...]] * 2, axis=0).astype(jnp.bfloat16)
+
+    def force(o, carry):
+        at = pl.multiple_of(o * 8, 8)
+        cells = jnp.concatenate(
+            [flux_cells[pl.ds(at, 8), :], flux_cells[pl.ds(at + ROWS * 8, 8), :]], axis=0
+        ).astype(jnp.bfloat16)
+        forcing = dot_first(cells, flux_embed_twice)
+        start = (
+            state_ref[o].astype(jnp.float32) + mask_ref[o].astype(jnp.float32) * forcing
+        ).astype(jnp.bfloat16)
+        win_a[o + REACH, EDGE : EDGE + CHUNKS * X, :] = start.astype(jnp.float32)
+        out_rows[0, o] = start
+        return carry
+
+    lax.fori_loop(0, ROWS, force, 0)
+
     def first(k, carry):
-        c = chunk_of(k)
-        x0 = pl.multiple_of(c * X, 16)
-
-        def row(y, inner):
-            keep(0, y, x0, state_ref[y, pl.ds(x0, X), :])
-            return inner
-
-        lax.fori_loop(0, ROWS, row, 0)
-        send_chunk(0, k, c)
+        send_chunk(0, k, chunk_of(k))
         return carry
 
     lax.fori_loop(0, CHUNKS, first, 0)
-    put_blocks(0, spectrum_ref[...])
+
+    embed_high, embed_rest = split(surface_embed_ref[...])
+    for h in range(2):
+        total = first_parts_in[h]
+        for k in range(1, 4):
+            total = total + first_parts_in[2 * k + h]
+        high, rest = split(total)
+        blank = jnp.zeros((5, LANES), jnp.float32)
+        left = jnp.concatenate(
+            [high.astype(jnp.float32), high.astype(jnp.float32), rest.astype(jnp.float32), blank],
+            axis=0,
+        ).astype(jnp.bfloat16)
+        blank = jnp.zeros((5, half_c), jnp.float32)
+        right = jnp.concatenate(
+            [
+                embed_high.astype(jnp.float32),
+                embed_rest.astype(jnp.float32),
+                embed_high.astype(jnp.float32),
+                blank,
+            ],
+            axis=0,
+        ).astype(jnp.bfloat16)
+        input_adj_ref[pl.ds(h * half, half), :] = dot_first(left, right)[:half]
+    atmosphere_ref[...] = (raw_ref[...].astype(jnp.float32) + input_adj_ref[...]).astype(
+        jnp.bfloat16
+    )
+    spectrum = dot32(wave_t_ref[...], atmosphere_ref[...])
+    put_blocks(0, rounded(jnp.concatenate([spectrum[:DEVICES], spectrum[DEVICES:]], axis=1)))
 
     def mask_of(y, x0):
         return mask_ref[y, pl.ds(x0, X), :].astype(jnp.float32)
 
     def own(e, y, x0):
         return windows[e % 2][y + REACH, pl.ds(EDGE + x0, X), :]
-
-    spread_taps(bands, taps_ref, 0, False)
 
     def keep_norm_0(k, at, unit, rstd):
         c = chunk_of(k)
@@ -734,7 +794,6 @@
 
     backward_stage(3, last, gather_flux)
     absorb()
-    half = ALON // 2
     high, rest = split(flux_rows[...])
     flux_by_row = dot_first(high, group_ref[...]) + dot_first(rest, group_ref[...])
     for slot in range(SLOTS):
@@ -748,7 +807,8 @@
         high, rest = split(input_adj_ref[pl.ds(h * half, half), :])
         row = dot_t(embed_high, high) + dot_t(embed_rest, high) + dot_t(embed_high, rest)
         rows_out[h, :, 0:half] = row[0:1]
-    swap_rows(rows_out, parts_out, rows_in, parts_in, regrid_sems)
+    send_rows(rows_out, parts_out, rows_in, parts_in, regrid_sems)
+    wait_rows(rows_out, parts_out, rows_in, parts_in, regrid_sems)
     for o in range(ROWS):
         total = to_atmosphere_ref[0, o] * rows_in[0]
         for slot in range(1, SLOTS):
@@ -756,10 +816,8 @@
         coarse_rows[o : o + 1, :] = total
     coarse_high, coarse_rest = split(coarse_rows[...])
     read = surface_read_ref[...] * 0.25
-    row_number = lax.broadcasted_iota(jnp.int32, (ROWS, CELL), 0)
-
     def widen(o, carry):
-        pick = jnp.where(row_number == o, 1.0, 0.0).astype(jnp.bfloat16)
+        pick = picked(o)
         spread = dot32(group_ref[...], dot_first(coarse_high, pick).astype(jnp.bfloat16)) + dot32(
             group_ref[...], dot_first(coarse_rest, pick).astype(jnp.bfloat16)
         )
@@ -796,7 +854,7 @@
             jax.ShapeDtypeStruct((ALON, 3 * CELL), bf16),
             jax.ShapeDtypeStruct((ALON, 3 * CELL), f32),
         ),
-        in_specs=[vmem] * 17 + [smem] * 2 + [vmem] * 3,
+        in_specs=[vmem] * 18 + [smem] * 2 + [vmem] * 3,
         out_specs=(vmem,) * 4,
         scratch_shapes=[
             pltpu.VMEM((ROWS + 2 * REACH, WIDE, CELL), f32),
@@ -825,6 +883,14 @@
             pltpu.VMEM((SLOTS, 1, LANES), f32),
             pltpu.VMEM((SLOTS, 8, LANES), f32),
             pltpu.SemaphoreType.DMA((4, SLOTS)),
+            pltpu.VMEM(whole, bf16),
+            pltpu.VMEM((ALON, 3 * CELL), bf16),
+            pltpu.VMEM((2, 8, LANES), f32),
+            pltpu.VMEM((SLOTS, 1, LANES), f32),
+            pltpu.VMEM((SLOTS, 8, LANES), f32),
+            pltpu.VMEM((SLOTS, 1, LANES), f32),
+            pltpu.SemaphoreType.DMA((4, SLOTS)),
+            pltpu.VMEM((2 * ROWS * 8, CHUNKS * X), f32),
         ],
         compiler_params=pltpu.CompilerParams(
             collective_id=6 if linked else None, has_side_effects=linked, vmem_limit_bytes=67000000
@@ -844,10 +910,6 @@
     slot = bands_row[:, None] - (2 * group - 2)
     onehot = (slot == jnp.arange(SLOTS, dtype=jnp.int32)[None, :]).astype(jnp.float32)
     return jnp.sum(onehot[:, :, None] * blocks[:, None, :], axis=0)
-
-
-def padded_lanes(values):
-    return jnp.pad(values, [(0, 0)] * (values.ndim - 1) + [(0, LANES - values.shape[-1])])
 
 
 def per_device(
@@ -874,75 +936,40 @@
     lat_rows, lon_count, channels = atmosphere.shape
     ocean_rows, ocean_lon, ocean_channels = ocean_state.shape
     half = lon_count // lax.axis_size("sec")
-    offset = lax.axis_index("sec") * half
     ratio = ocean_lon // half
     flux_count = flux_read.shape[1]
-    highest = lax.Precision.HIGHEST
-    mask_value = land_mask.astype(jnp.float32)
     group = lax.axis_index("tile")
     to_ocean = slot_weights(crossing_bands[0], ocean_regrid[0, :, :, 0], group)
     to_atmosphere = slot_weights(crossing_bands[0], atmosphere_regrid[0, :, 0, :], group)
-    surface = jnp.dot(ocean_state, surface_read, preferred_element_type=jnp.float32)
-    coarse = jnp.mean((mask_value * surface).reshape(ocean_rows, half, ratio), axis=2)
-    flux = jnp.einsum(
-        "hgc,cf->hfg",
-        atmosphere.reshape(2, half, channels),
-        flux_read,
-        preferred_element_type=jnp.float32,
-    )
-    flux_rows, surface_rows = regrid(
-        padded_lanes(flux),
-        padded_lanes(jnp.dot(to_atmosphere, coarse, precision=highest))[:, None, :],
-        0,
-    )
-    surface_atmosphere = surface_rows[:, 0, :half].reshape(1, lon_count)
-    flux_ocean = jnp.einsum("so,sfg->ogf", to_ocean, flux_rows[:, :, :half], precision=highest)
-    mixed_input = (
-        atmosphere.astype(jnp.float32)
-        + surface_atmosphere[:, :, None] * surface_embed[None, None, :]
-    ).astype(jnp.bfloat16)
     table = wave_table()
-    spectrum = jnp.einsum(
-        "gk,gc->kc", jnp.asarray(table), mixed_input[0], preferred_element_type=jnp.float32
-    )
-    spectrum = spectrum.astype(jnp.bfloat16).astype(jnp.float32)
-    spectrum = jnp.concatenate([spectrum[:DEVICES], spectrum[DEVICES:]], axis=1)
-    forcing_coarse = jnp.einsum(
-        "ogf,fc->ogc",
-        flux_ocean,
-        flux_embed.astype(jnp.float32),
-        precision=highest,
-    )
-    forcing = jnp.broadcast_to(
-        forcing_coarse[:, :, None, :], (ocean_rows, half, ratio, ocean_channels)
-    ).reshape(ocean_rows, ocean_lon, ocean_channels)
-    state = (ocean_state.astype(jnp.float32) + mask_value[:, :, None] * forcing).astype(
-        jnp.bfloat16
-    )
     layer_count = conv_kernel.shape[0]
     embed_rows = (
         jnp.eye(ocean_rows, dtype=flux_embed.dtype)[:, None, :, None]
         * flux_embed.T[None, :, None, :]
     ).reshape(ocean_rows * ocean_channels, ocean_rows * flux_count)
+    read_rows = (
+        jnp.eye(ocean_rows, dtype=surface_read.dtype)[:, None, :] * surface_read[None, :, None]
+    ).reshape(ocean_rows * ocean_channels, ocean_rows)
     grouping = np.arange(ocean_lon)[:, None] // ratio == np.arange(LANES)[None, :]
     grouping = grouping.astype(jnp.bfloat16)
     state, ocean_grad, atmosphere_next, atmosphere_grad = ocean(
-        state,
-        jnp.broadcast_to(mask_value[:, :, None], state.shape).astype(jnp.bfloat16),
+        ocean_state,
+        land_mask,
         ocean_cotangent,
         conv_kernel.reshape(layer_count, TAPS * TAPS, CELL).astype(jnp.float32),
         norm_gain,
         expand_weight,
         project_weight,
-        mixed_input[0],
+        atmosphere[0],
         atmosphere_cotangent[0],
-        spectrum,
         jnp.asarray(table),
         jnp.asarray(np.ascontiguousarray(table.T)),
         legendre_forward[0],
         legendre_inverse[0],
         spectral_mix,
         embed_rows,
+        read_rows,
+        flux_embed.astype(jnp.float32),
         jnp.asarray(grouping),
         to_ocean,
         to_atmosphere,

time: 184 us -> 170 us (0.924)
  Pallas kernels: 157 us -> 151 us
  local copies, waits for them, and re-layouts: 15.5 us -> 10.4 us
  matrix products: 4.59 us -> 0 us
    pallas_call x1 -> x0, Pallas kernels: 15.5 us -> none  [regrid(): pl.pallas_call(regrid_kernel, out_shape=(jax.ShapeDtypeStruct((SLOTS, r,...]
    pallas_call x1, Pallas kernels: 142 us -> 151 us  [ocean(): pl.pallas_call(functools.partial(ocean_kernel, linked), out_shape=(jax.Sh...]
    dot_general x6 -> x0, matrix products: 4.59 us -> none  [the longest x1 1.98 us: per_device(): jnp.dot(ocean_state, surface_read, preferred_element_type=jnp.float32)]
    unnamed x31 -> x9, local copies, waits for them, and re-layouts: 8.15 us -> 6.91 us
where the time goes in v5:
time: 170 us; the launch traced here: 169 us
  Pallas kernels  151 us (89%)
  local copies, waits for them, and re-layouts  10.4 us (6%)
  other arithmetic  6.99 us (4%)
    pallas_call x1, Pallas kernels, ocean(): pl.pallas_call(functools.partial(ocean_kernel, linked), out_shape=(jax.Sh...  151 us
    unnamed x9, local copies, waits for them, and re-layouts  6.91 us

profile of v5, /device:TPU:1, one launch (start us, length us, event | category | flops | bytes accessed | tf_op | source)
XLA Modules:
  0.0 169.4 jit_solution(15768310103199248265)
XLA Ops:
  0.6 0.7 subtract_bitcast_fusion
  1.3 1.2 bitcast_convert_fusion.1.surface_read_ref
  2.5 0.1 fusion.1
  2.6 1.3 broadcast_in_dim.10.surface_embed_ref
  3.8 0.1 copy.31
  3.9 0.7 broadcast_bitcast_fusion
  4.6 1.3 convert_element_type.34.flux_embed_ref
  5.9 1.4 multiply_reduce_fusion
  7.2 0.8 bitcast_convert_fusion
  8.0 0.6 copy.32.taps_ref
  8.6 0.8 multiply_bitcast_fusion
  9.4 0.8 copy.33.embed_rows_ref
  10.3 0.9 bitcast_multiply_fusion.read_rows_ref
  11.2 151.3 %ocean.1 = (bf16[8,720,128]{2,1,0:T(8,128)(2,1)}, f32[8,720,128]{2,1,0:T(8,128)}, bf16[360,384]{1,0:T(8,128)(2,1)}, f32[360,384]{1,0:T(8,128)}) custom-call(bf16[8,720,128]{2,1,0:T(8,128)(2,1)} %state_ref.1, s32[8,720]{1,0:T(8,128)} %land_ref.1, bf16[8,720,128]{2,1,0:T(8,128)(2,1)} %cot_ref.1, f32[2,49,128]{2,1,0:T(8,128)} %copy.32.taps_ref, ...), custom_call_target="tpu_custom_call" | custom-call | tf_op jit(solution)/shard_map/ocean/pallas_call | solution.py:849
  162.5 0.0 copy-start.1
  162.5 1.7 %copy.41 = bf16[1,360,384]{2,1,0:T(8,128)(2,1)} copy(bf16[1,360,384]{2,1,0:T(8,128)(2,1)} %bitcast.32) | data formatting | bytes 552960
  164.3 0.0 copy-start
  164.3 2.7 %copy.42 = bf16[8,720,128]{2,1,0:T(8,128)(2,1)} copy(bf16[8,720,128]{2,1,0:T(8,128)(2,1)} %get-tuple-element.19) | data formatting | bytes 2949120
  167.0 0.0 copy-done.1
  167.0 0.8 copy.43
  167.8 0.0 copy-done
  167.8 1.6 copy.44
  (2 shorter events, 0.0 us)
Async XLA Ops:
  162.5 4.5 %copy-start.1 = (f32[360,384]{1,0:T(8,128)S(1)}, f32[360,384]{1,0:T(8,128)}, u32[]{:S(2)}) copy-start(f32[360,384]{1,0:T(8,128)} %get-tuple-element.10) | copy-start | bytes 1658884
  164.3 3.5 %copy-start = (f32[8,720,128]{2,1,0:T(8,128)S(1)}, f32[8,720,128]{2,1,0:T(8,128)}, u32[]{:S(2)}) copy-start(f32[8,720,128]{2,1,0:T(8,128)} %get-tuple-element.21) | copy-start | bytes 8847364

commit v6 on v5

--- a/solution.py
+++ b/solution.py
@@ -24,6 +24,7 @@
 TAPS = 7
 REACH = 3
 ALON = 360
+EARLY = 7
 
 
 def remote(src, dst, send_sem, recv_sem, device):
@@ -194,7 +195,7 @@
     state_ref,
     land_ref,
     cot_ref,
-    taps_ref,
+    kernel_ref,
     gain_ref,
     expand_ref,
     project_ref,
@@ -205,8 +206,6 @@
     forward_ref,
     inverse_ref,
     mix_ref,
-    embed_rows_ref,
-    read_rows_ref,
     flux_embed_ref,
     group_ref,
     to_ocean_ref,
@@ -252,6 +251,9 @@
     first_parts_in,
     first_sems,
     flux_cells,
+    taps_ref,
+    embed_rows_ref,
+    read_rows_ref,
 ):
     sec = lax.axis_index("sec") if linked else 0
     tile = lax.axis_index("tile") if linked else 0
@@ -292,24 +294,30 @@
         bands[v, 7 * CELL :, :CELL] = jnp.zeros((CELL, CELL), jnp.bfloat16)
 
 
+    def send_block(x, i):
+        peer = lax.rem(me + i, DEVICES)
+        remote(
+            leaving.at[x, pl.ds(pl.multiple_of(peer * 8, 8), 8)],
+            landed.at[x, pl.ds(pl.multiple_of(me * 8, 8), 8)],
+            swap_sems.at[0, x],
+            swap_sems.at[1, x],
+            peer,
+        ).start()
+
+    def send_share(x, turn, turns):
+        share = (DEVICES - 1 - EARLY) // turns
+        for j in range(share):
+            send_block(x, EARLY + 1 + turn * share + j)
+
     def put_blocks(x, values):
         for j in range(6):
             leaving[x, pl.ds(j, DEVICES, stride=8), :] = values[:, j * CELL : (j + 1) * CELL]
-        if not linked:
-            return
 
         def send(i, carry):
-            peer = (me + i) % DEVICES
-            remote(
-                leaving.at[x, pl.ds(pl.multiple_of(peer * 8, 8), 8)],
-                landed.at[x, pl.ds(pl.multiple_of(me * 8, 8), 8)],
-                swap_sems.at[0, x],
-                swap_sems.at[1, x],
-                peer,
-            ).start()
+            send_block(x, i)
             return carry
 
-        lax.fori_loop(1, DEVICES, send, 0)
+        lax.fori_loop(1, DEVICES if x == 3 else EARLY + 1, send, 0)
         mine = pl.ds(pl.multiple_of(me * 8, 8), 8)
         landed[x, mine, :] = leaving[x, mine, :]
 
@@ -586,6 +594,7 @@
             normalize(k)
 
             def piece(y, inner):
+                send_share(e, k * ROWS + y, CHUNKS * ROWS)
                 activate(k, y)
                 return inner
 
@@ -600,7 +609,13 @@
         def chunk(k, carry):
             take_halo(e, k)
             conv(e, k)
-            halves(lambda q, at: one(k, q, at))
+
+            def part(q, at):
+                if e == 2:
+                    send_share(e, k * 2 + q, CHUNKS * 2)
+                one(k, q, at)
+
+            halves(part)
             if after is not None:
                 after(k)
             if e < 3:
@@ -622,6 +637,23 @@
         return carry
 
     lax.fori_loop(0, ROWS, spread_mask, 0)
+
+    for layer in range(2):
+        for u in range(TAPS):
+            taps_ref[layer, u * TAPS : (u + 1) * TAPS, :] = kernel_ref[layer, u].astype(jnp.float32)
+
+    def numbers(width):
+        return [lax.broadcasted_iota(jnp.int32, (8, width), axis) for axis in range(2)]
+
+    read_row = jnp.where(row_number == 0, surface_read_ref[...], 0.0).astype(jnp.bfloat16)
+    for y in range(ROWS):
+        at = pl.ds(y * CELL, CELL)
+        row, column = numbers(ROWS)
+        pick = jnp.where((row == 0) & (column == y), 1.0, 0.0).astype(jnp.bfloat16)
+        read_rows_ref[at, :] = dot_first(read_row, pick).astype(jnp.bfloat16)
+        row, column = numbers(ROWS * 8)
+        pick = jnp.where(column == row + y * 8, 1.0, 0.0).astype(jnp.bfloat16)
+        embed_rows_ref[at, :] = dot_first(flux_embed_ref[...], pick).astype(jnp.bfloat16)
 
     lanes = jnp.concatenate([mask_ref[y] * state_ref[y] for y in range(ROWS)], axis=1)
     high, rest = split(dot32(lanes, read_rows_ref[...]))
@@ -648,7 +680,8 @@
     high, rest = split(jnp.concatenate([parts_out[o] for o in range(ROWS)], axis=0))
     flux_cells[0 : ROWS * 8, :] = dot_t(high, group_ref[...])
     flux_cells[ROWS * 8 :, :] = dot_t(rest, group_ref[...])
-    flux_embed_twice = jnp.concatenate([flux_embed_ref[...]] * 2, axis=0).astype(jnp.bfloat16)
+    flux_embed_twice = jnp.concatenate([flux_embed_ref[...].astype(jnp.float32)] * 2, axis=0)
+    flux_embed_twice = flux_embed_twice.astype(jnp.bfloat16)
 
     def force(o, carry):
         at = pl.multiple_of(o * 8, 8)
@@ -854,7 +887,7 @@
             jax.ShapeDtypeStruct((ALON, 3 * CELL), bf16),
             jax.ShapeDtypeStruct((ALON, 3 * CELL), f32),
         ),
-        in_specs=[vmem] * 18 + [smem] * 2 + [vmem] * 3,
+        in_specs=[vmem] * 16 + [smem] * 2 + [vmem] * 3,
         out_specs=(vmem,) * 4,
         scratch_shapes=[
             pltpu.VMEM((ROWS + 2 * REACH, WIDE, CELL), f32),
@@ -891,6 +924,9 @@
             pltpu.VMEM((SLOTS, 1, LANES), f32),
             pltpu.SemaphoreType.DMA((4, SLOTS)),
             pltpu.VMEM((2 * ROWS * 8, CHUNKS * X), f32),
+            pltpu.VMEM((2, TAPS * TAPS, CELL), f32),
+            pltpu.VMEM((ROWS * CELL, ROWS * 8), bf16),
+            pltpu.VMEM((ROWS * CELL, ROWS), bf16),
         ],
         compiler_params=pltpu.CompilerParams(
             collective_id=6 if linked else None, has_side_effects=linked, vmem_limit_bytes=67000000
@@ -933,30 +969,21 @@
     atmosphere_cotangent,
     ocean_cotangent,
 ):
-    lat_rows, lon_count, channels = atmosphere.shape
-    ocean_rows, ocean_lon, ocean_channels = ocean_state.shape
+    lon_count = atmosphere.shape[1]
+    ocean_lon = ocean_state.shape[1]
     half = lon_count // lax.axis_size("sec")
     ratio = ocean_lon // half
-    flux_count = flux_read.shape[1]
     group = lax.axis_index("tile")
     to_ocean = slot_weights(crossing_bands[0], ocean_regrid[0, :, :, 0], group)
     to_atmosphere = slot_weights(crossing_bands[0], atmosphere_regrid[0, :, 0, :], group)
     table = wave_table()
-    layer_count = conv_kernel.shape[0]
-    embed_rows = (
-        jnp.eye(ocean_rows, dtype=flux_embed.dtype)[:, None, :, None]
-        * flux_embed.T[None, :, None, :]
-    ).reshape(ocean_rows * ocean_channels, ocean_rows * flux_count)
-    read_rows = (
-        jnp.eye(ocean_rows, dtype=surface_read.dtype)[:, None, :] * surface_read[None, :, None]
-    ).reshape(ocean_rows * ocean_channels, ocean_rows)
     grouping = np.arange(ocean_lon)[:, None] // ratio == np.arange(LANES)[None, :]
     grouping = grouping.astype(jnp.bfloat16)
     state, ocean_grad, atmosphere_next, atmosphere_grad = ocean(
         ocean_state,
         land_mask,
         ocean_cotangent,
-        conv_kernel.reshape(layer_count, TAPS * TAPS, CELL).astype(jnp.float32),
+        conv_kernel,
         norm_gain,
         expand_weight,
         project_weight,
@@ -967,9 +994,7 @@
         legendre_forward[0],
         legendre_inverse[0],
         spectral_mix,
-        embed_rows,
-        read_rows,
-        flux_embed.astype(jnp.float32),
+        flux_embed,
         jnp.asarray(grouping),
         to_ocean,
         to_atmosphere,

time: 170 us -> 173 us (1.018)
  Pallas kernels: 151 us -> 159 us
  other arithmetic: 6.99 us -> 3.33 us
    pallas_call x1, Pallas kernels: 151 us -> 159 us  [ocean(): pl.pallas_call(functools.partial(ocean_kernel, linked), out_shape=(jax.Sh...]
    convert_element_type x3 -> x0, other arithmetic: 2.04 us -> none  [the longest x1 1.27 us: per_device(): flux_embed.astype(jnp.float32)]
where the time goes in v6:
time: 173 us; the launch traced here: 172 us
  Pallas kernels  159 us (92%)
  local copies, waits for them, and re-layouts  9.48 us (5%)
  other arithmetic  3.33 us (2%)
    pallas_call x1, Pallas kernels, ocean(): pl.pallas_call(functools.partial(ocean_kernel, linked), out_shape=(jax.Sh...  159 us
    unnamed x9, local copies, waits for them, and re-layouts  8.24 us

profile of v6, /device:TPU:1, one launch (start us, length us, event | category | flops | bytes accessed | tf_op | source)
XLA Modules:
  0.0 172.4 jit_solution(11472544555164534705)
XLA Ops:
  0.6 0.7 subtract_bitcast_fusion
  1.3 1.2 bitcast_convert_fusion.surface_read_ref
  2.5 0.1 fusion
  2.6 1.2 broadcast_in_dim.18.surface_embed_ref
  3.8 1.4 multiply_reduce_fusion
  5.2 1.4 copy.27.kernel_ref
  6.6 158.9 %ocean.1 = (bf16[8,720,128]{2,1,0:T(8,128)(2,1)}, f32[8,720,128]{2,1,0:T(8,128)}, bf16[360,384]{1,0:T(8,128)(2,1)}, f32[360,384]{1,0:T(8,128)}) custom-call(bf16[8,720,128]{2,1,0:T(8,128)(2,1)} %state_ref.1, s32[8,720]{1,0:T(8,128)} %land_ref.1, bf16[8,720,128]{2,1,0:T(8,128)(2,1)} %cot_ref.1, bf16[2,7,7,128]{3,2,1,0:T(8,128)(2,1)} %copy.27.kernel_ref, ...), custom_call_target="tpu_custom_call" | custom-call | tf_op jit(solution)/shard_map/ocean/pallas_call | solution.py:882
  165.5 0.0 copy-start.1
  165.5 1.7 %copy.32 = bf16[1,360,384]{2,1,0:T(8,128)(2,1)} copy(bf16[1,360,384]{2,1,0:T(8,128)(2,1)} %bitcast.17) | data formatting | bytes 552960
  167.3 0.0 copy-start
  167.3 2.7 %copy.33 = bf16[8,720,128]{2,1,0:T(8,128)(2,1)} copy(bf16[8,720,128]{2,1,0:T(8,128)(2,1)} %get-tuple-element.19) | data formatting | bytes 2949120
  170.0 0.0 copy-done.1
  170.0 0.8 copy.34
  170.8 0.0 copy-done
  170.8 1.6 copy.35
Async XLA Ops:
  165.5 4.5 %copy-start.1 = (f32[360,384]{1,0:T(8,128)S(1)}, f32[360,384]{1,0:T(8,128)}, u32[]{:S(2)}) copy-start(f32[360,384]{1,0:T(8,128)} %get-tuple-element.10) | copy-start | bytes 1658884
  167.3 3.5 %copy-start = (f32[8,720,128]{2,1,0:T(8,128)S(1)}, f32[8,720,128]{2,1,0:T(8,128)}, u32[]{:S(2)}) copy-start(f32[8,720,128]{2,1,0:T(8,128)} %get-tuple-element.21) | copy-start | bytes 8847364

commit v7 on v6

--- a/solution.py
+++ b/solution.py
@@ -24,7 +24,6 @@
 TAPS = 7
 REACH = 3
 ALON = 360
-EARLY = 7
 
 
 def remote(src, dst, send_sem, recv_sem, device):
@@ -304,11 +303,6 @@
             peer,
         ).start()
 
-    def send_share(x, turn, turns):
-        share = (DEVICES - 1 - EARLY) // turns
-        for j in range(share):
-            send_block(x, EARLY + 1 + turn * share + j)
-
     def put_blocks(x, values):
         for j in range(6):
             leaving[x, pl.ds(j, DEVICES, stride=8), :] = values[:, j * CELL : (j + 1) * CELL]
@@ -317,7 +311,7 @@
             send_block(x, i)
             return carry
 
-        lax.fori_loop(1, DEVICES if x == 3 else EARLY + 1, send, 0)
+        lax.fori_loop(1, DEVICES, send, 0)
         mine = pl.ds(pl.multiple_of(me * 8, 8), 8)
         landed[x, mine, :] = leaving[x, mine, :]
 
@@ -594,7 +588,6 @@
             normalize(k)
 
             def piece(y, inner):
-                send_share(e, k * ROWS + y, CHUNKS * ROWS)
                 activate(k, y)
                 return inner
 
@@ -609,13 +602,7 @@
         def chunk(k, carry):
             take_halo(e, k)
             conv(e, k)
-
-            def part(q, at):
-                if e == 2:
-                    send_share(e, k * 2 + q, CHUNKS * 2)
-                one(k, q, at)
-
-            halves(part)
+            halves(lambda q, at: one(k, q, at))
             if after is not None:
                 after(k)
             if e < 3:

time: 173 us -> 166 us (0.960)
  Pallas kernels: 159 us -> 152 us
    pallas_call x1, Pallas kernels: 159 us -> 152 us  [ocean(): pl.pallas_call(functools.partial(ocean_kernel, linked), out_shape=(jax.Sh...]
where the time goes in v7:
time: 166 us
  Pallas kernels  152 us (92%)
  local copies, waits for them, and re-layouts  9.48 us (6%)
  other arithmetic  3.33 us (2%)
    pallas_call x1, Pallas kernels, ocean(): pl.pallas_call(functools.partial(ocean_kernel, linked), out_shape=(jax.Sh...  152 us
    unnamed x9, local copies, waits for them, and re-layouts  8.24 us

profile of v7, /device:TPU:1, one launch (start us, length us, event | category | flops | bytes accessed | tf_op | source)
XLA Modules:
  0.0 165.7 jit_solution(13659648327140200364)
XLA Ops:
  0.6 0.7 subtract_bitcast_fusion
  1.3 1.2 bitcast_convert_fusion.surface_read_ref
  2.5 0.1 fusion
  2.6 1.2 broadcast_in_dim.18.surface_embed_ref
  3.8 1.4 multiply_reduce_fusion
  5.2 1.4 copy.27.kernel_ref
  6.6 152.2 %ocean.1 = (bf16[8,720,128]{2,1,0:T(8,128)(2,1)}, f32[8,720,128]{2,1,0:T(8,128)}, bf16[360,384]{1,0:T(8,128)(2,1)}, f32[360,384]{1,0:T(8,128)}) custom-call(bf16[8,720,128]{2,1,0:T(8,128)(2,1)} %state_ref.1, s32[8,720]{1,0:T(8,128)} %land_ref.1, bf16[8,720,128]{2,1,0:T(8,128)(2,1)} %cot_ref.1, bf16[2,7,7,128]{3,2,1,0:T(8,128)(2,1)} %copy.27.kernel_ref, ...), custom_call_target="tpu_custom_call" | custom-call | tf_op jit(solution)/shard_map/ocean/pallas_call | solution.py:869
  158.8 0.0 copy-start.1
  158.8 1.7 %copy.32 = bf16[1,360,384]{2,1,0:T(8,128)(2,1)} copy(bf16[1,360,384]{2,1,0:T(8,128)(2,1)} %bitcast.17) | data formatting | bytes 552960
  160.5 0.0 copy-start
  160.5 2.7 %copy.33 = bf16[8,720,128]{2,1,0:T(8,128)(2,1)} copy(bf16[8,720,128]{2,1,0:T(8,128)(2,1)} %get-tuple-element.19) | data formatting | bytes 2949120
  163.3 0.0 copy-done.1
  163.3 0.8 copy.34
  164.1 0.0 copy-done
  164.1 1.6 copy.35
Async XLA Ops:
  158.8 4.5 %copy-start.1 = (f32[360,384]{1,0:T(8,128)S(1)}, f32[360,384]{1,0:T(8,128)}, u32[]{:S(2)}) copy-start(f32[360,384]{1,0:T(8,128)} %get-tuple-element.10) | copy-start | bytes 1658884
  160.5 3.5 %copy-start = (f32[8,720,128]{2,1,0:T(8,128)S(1)}, f32[8,720,128]{2,1,0:T(8,128)}, u32[]{:S(2)}) copy-start(f32[8,720,128]{2,1,0:T(8,128)} %get-tuple-element.21) | copy-start | bytes 8847364
